TPU v7x, 8 devices: a whole 2x2x1 slice. The times are simulated.
8 devices in a mesh: dp: 1 (over z), tp: 2 (over y), cp: 4 (over x, core).
Axes of the slice: x: 2, y: 2, z: 1, core: 2. Of those that a mesh axis runs over, the one named last changes fastest.
Arguments:
- x_chunk: bfloat16 [32, 128, 4096], P('dp', 'cp')
- w_query: bfloat16 [4096, 4096], P(None, 'tp')
- w_key: bfloat16 [4096, 4096], P(None, 'tp')
- w_value: bfloat16 [4096, 4096], P(None, 'tp')
- w_out: bfloat16 [4096, 4096], P('tp')
- q_gain: bfloat16 [4096], P('tp')
- k_gain: bfloat16 [4096], P('tp')
- post_gain: bfloat16 [4096], replicated
- cache_k: bfloat16 [32, 1024, 32, 128], P('dp', 'cp', 'tp')
- cache_v: bfloat16 [32, 1024, 32, 128], P('dp', 'cp', 'tp')
- prefix_len: int32 [32], P('dp')
Outputs:
- output 1: bfloat16 [32, 128, 4096], P('dp', 'cp')
- output 2: bfloat16 [32, 128, 32, 128], P('dp', 'cp', 'tp')
- output 3: bfloat16 [32, 128, 32, 128], P('dp', 'cp', 'tp')
All inputs are finite; a program needn't handle non-finite values.
Results may differ from a plain program's by a relative error of at most 0.0065922.
Values are sent between devices in bfloat16 or wider.
A program may use at most 1 GiB of HBM per device.

v0:
```python
import jax
import jax.numpy as jnp
from jax import lax
from jax.sharding import PartitionSpec as P

NORM_EPS = 1e-6
ROPE_BASE = 500000.0
MASK_VALUE = -1e30


def rope_apply(head_vals, positions):
    head_dim = head_vals.shape[-1]
    half_dim = head_dim // 2
    inv_freq = ROPE_BASE ** (-(jnp.arange(half_dim, dtype=jnp.float32) * 2.0 / head_dim))
    angles = positions.astype(jnp.float32)[..., None] * inv_freq
    cos_tab = jnp.cos(angles)[..., None, :]
    sin_tab = jnp.sin(angles)[..., None, :]
    first_half = head_vals[..., :half_dim]
    second_half = head_vals[..., half_dim:]
    return jnp.concatenate([first_half * cos_tab - second_half * sin_tab, second_half * cos_tab + first_half * sin_tab], axis=-1)


def solution(mesh):
    cp_size = mesh.shape['cp']
    tp_size = mesh.shape['tp']

    def local_step(x_chunk, w_query, w_key, w_value, w_out, q_gain, k_gain, post_gain, cache_k, cache_v, prefix_len):
        batch_rows, chunk_dev, model_dim = x_chunk.shape
        cache_dev = cache_k.shape[1]
        kv_local = cache_k.shape[2]
        head_dim = cache_k.shape[3]
        q_local = w_query.shape[1] // head_dim
        groups = q_local // kv_local
        cp_index = lax.axis_index('cp')
        tokens = x_chunk.reshape(batch_rows * chunk_dev, model_dim)
        q_raw = jnp.dot(tokens, w_query, preferred_element_type=jnp.float32)
        k_raw = jnp.dot(tokens, w_key, preferred_element_type=jnp.float32)
        v_raw = jnp.dot(tokens, w_value, preferred_element_type=jnp.float32)
        square_sums = lax.psum(jnp.stack([jnp.sum(q_raw * q_raw, axis=-1), jnp.sum(k_raw * k_raw, axis=-1)]), 'tp')
        q_inv = lax.rsqrt(square_sums[0] / (w_query.shape[1] * tp_size) + NORM_EPS)
        k_inv = lax.rsqrt(square_sums[1] / (w_key.shape[1] * tp_size) + NORM_EPS)
        q_norm = (q_raw * q_inv[:, None] * q_gain.astype(jnp.float32)).reshape(batch_rows, chunk_dev, q_local, head_dim)
        k_norm = (k_raw * k_inv[:, None] * k_gain.astype(jnp.float32)).reshape(batch_rows, chunk_dev, kv_local, head_dim)
        positions = prefix_len[:, None] + cp_index * chunk_dev + jnp.arange(chunk_dev, dtype=jnp.int32)[None, :]
        q_new = rope_apply(q_norm, positions).astype(jnp.bfloat16).reshape(batch_rows, chunk_dev, kv_local, groups, head_dim)
        chunk_k = rope_apply(k_norm, positions).astype(jnp.bfloat16)
        chunk_v = v_raw.astype(jnp.bfloat16).reshape(batch_rows, chunk_dev, kv_local, head_dim)
        q_all = lax.all_gather(q_new, 'cp', axis=1, tiled=True)
        score_scale = head_dim ** -0.5
        slot_index = cp_index * cache_dev + jnp.arange(cache_dev)
        cache_ok = (slot_index[None, :] < prefix_len[:, None])[:, None, None, None, :]
        key_index = cp_index * chunk_dev + jnp.arange(chunk_dev)

        def block_attention(block_id):
            q_blk = lax.dynamic_slice_in_dim(q_all, block_id * chunk_dev, chunk_dev, axis=1)
            query_index = block_id * chunk_dev + jnp.arange(chunk_dev)
            chunk_ok = (key_index[None, :] <= query_index[:, None])[None, :, None, None, :]
            s_cache = jnp.einsum('bqkgd,btkd->bqkgt', q_blk, cache_k, preferred_element_type=jnp.float32) * score_scale
            s_cache = jnp.where(cache_ok, s_cache, MASK_VALUE)
            s_chunk = jnp.einsum('bqkgd,btkd->bqkgt', q_blk, chunk_k, preferred_element_type=jnp.float32) * score_scale
            s_chunk = jnp.where(chunk_ok, s_chunk, MASK_VALUE)
            row_max = jnp.maximum(jnp.max(s_cache, axis=-1), jnp.max(s_chunk, axis=-1))
            p_cache = jnp.exp(s_cache - row_max[..., None])
            p_chunk = jnp.exp(s_chunk - row_max[..., None])
            den_sum = jnp.sum(p_cache, axis=-1) + jnp.sum(p_chunk, axis=-1)
            num_sum = jnp.einsum('bqkgt,btkd->bqkgd', p_cache.astype(jnp.bfloat16), cache_v, preferred_element_type=jnp.float32)
            num_sum = num_sum + jnp.einsum('bqkgt,btkd->bqkgd', p_chunk.astype(jnp.bfloat16), chunk_v, preferred_element_type=jnp.float32)
            return row_max, den_sum, num_sum

        part_max, part_den, part_num = lax.map(block_attention, jnp.arange(cp_size))
        glob_max = lax.pmax(part_max, 'cp')
        factor = jnp.exp(part_max - glob_max)
        den_total = lax.psum_scatter(part_den * factor, 'cp', scatter_dimension=0, tiled=False)
        num_total = lax.psum_scatter(part_num * factor[..., None], 'cp', scatter_dimension=0, tiled=False)
        attn_out = (num_total / den_total[..., None]).astype(jnp.bfloat16).reshape(batch_rows * chunk_dev, q_local * head_dim)
        mixed_part = jnp.dot(attn_out, w_out, preferred_element_type=jnp.float32)
        mixed_sum = lax.psum(mixed_part, 'tp')
        normed = mixed_sum * lax.rsqrt(jnp.mean(mixed_sum * mixed_sum, axis=-1, keepdims=True) + NORM_EPS) * post_gain.astype(jnp.float32)
        block_out = (x_chunk.astype(jnp.float32) + normed.reshape(batch_rows, chunk_dev, model_dim)).astype(jnp.bfloat16)
        return block_out, chunk_k, chunk_v

    x_spec = P('dp', 'cp', None)
    head_spec = P('dp', 'cp', 'tp', None)
    in_specs = (x_spec, P(None, 'tp'), P(None, 'tp'), P(None, 'tp'), P('tp', None), P('tp'), P('tp'), P(None), head_spec, head_spec, P('dp'))
    out_specs = (x_spec, head_spec, head_spec)
    return jax.shard_map(local_step, mesh=mesh, in_specs=in_specs, out_specs=out_specs, check_vma=False)
```

profile of v0, /device:TPU:0, one launch (start us, length us, event | category | flops | bytes accessed | tf_op | source)
XLA Modules:
  0.0 1267.8 jit_solution(17212133399723902515)
XLA Ops:
  7.9 24.3 %multiply_reduce_fusion.1 = (f32[1024]{0:T(1024)S(1)}, f32[1024,2048]{1,0:T(8,128)}) fusion(bf16[1024,4096]{1,0:T(8,128)(2,1)} %bitcast.190, bf16[4096,2048]{1,0:T(8,128)(2,1)} %param.15), kind=kOutput, calls=%fused_computation.52 | convolution fusion | flops 17184063488 | bytes 33558528 | tf_op jit(solution)/shard_map/dot_general | solution.py:37
  32.3 19.8 %multiply_reduce_fusion.2 = (f32[1024]{0:T(1024)S(1)}, f32[1024,2048]{1,0:T(8,128)}) fusion(bf16[1024,4096]{1,0:T(8,128)(2,1)S(1)} %bitcast.192, bf16[4096,2048]{1,0:T(8,128)(2,1)S(1)} %copy-done.11), kind=kOutput, calls=%fused_computation.53 | convolution fusion | flops 17184063488 | bytes 33558528 | tf_op jit(solution)/shard_map/dot_general | solution.py:36
  68.3 7.5 multiply_bitcast_fusion.1
  83.3 7.3 subtract_convert_fusion
  95.9 23.3 %copy.38 = bf16[32,256,16,128]{3,1,2,0:T(8,128)(2,1)} copy(bf16[32,256,16,128]{3,2,1,0:T(8,128)(2,1)} %param.21) | data formatting | bytes 67108864
  128.9 23.3 %copy.40 = bf16[32,256,16,128]{3,1,2,0:T(8,128)(2,1)} copy(bf16[32,256,16,128]{3,2,1,0:T(8,128)(2,1)} %param.22) | data formatting | bytes 67108864
  152.2 22.7 %convert_bitcast_fusion = bf16[128,8,16,128]{3,1,2,0:T(8,128)(2,1)S(1)} fusion(bf16[1024,4096]{1,0:T(8,128)(2,1)} %bitcast.191, bf16[4096,2048]{1,0:T(8,128)(2,1)} %param.16), kind=kOutput, calls=%fused_computation.59 | convolution fusion | flops 17181966336 | bytes 29360128 | tf_op jit(solution)/shard_map/dot_general | solution.py:38
  181.4 18.8 %all-gather.2.cloned.1.call-done = bf16[32,128,16,1,128]{4,2,1,0,3:T(8,128)(2,1)} async-done(((bf16[32,32,16,1,128]{4,2,1,0,3:T(8,128)(2,1)}), bf16[32,128,16,1,128]{4,2,1,0,3:T(8,128)(2,1)}) %all-gather.2.cloned.1.call-update) | async-done | bytes 16777232 | tf_op jit(solution)/shard_map/all_gather | solution.py:48
  200.2 337.9 %while.15 = (s32[]{:T(128)}, f32[4,32,32,16,1]{2,3,1,4,0:T(8,128)S(1)}, f32[4,32,32,16,1]{2,4,3,1,0:T(1,128)S(1)}, f32[4,32,32,16,1,128]{5,2,3,1,4,0:T(8,128)}, ...) while((s32[]{:T(128)}, ...), condition=%wide.region_8.9_spmd.clone, body=%wide.region_3.8_spmd.clone.sunk | while | flops 2469897216 | bytes 277059552 | solution.py:70
  207.0 25.2 %fusion.72 = (f32[32,32,16]{1,2,0:T(8,128)S(1)}, f32[32,16,32,256]{3,2,1,0:T(8,128)}) fusion(pred[32,256]{1,0:T(8,128)(4,1)S(1)} %compare_bitcast_fusion.2, bf16[32,256,16,128]{3,1,2,0:T(8,128)(2,1)} %get-tuple-element.326, bf16[32,32,16,1,128]{4,2,1,0,3:T(8,128)(2,1)} %constant_dynamic-slice_fusion.2), kind=kOutput, calls=%fused_computation.7.clone.1 | convolution fusion | flops 1086308352 | bytes 54599680 | tf_op jit(solution)/shard_map/while/body/eval_jaxpr/bqkgd,btkd->bqkgt/dot_general | solution.py:58
  232.3 10.2 fusion.73
  253.3 7.6 fusion.76
  260.9 23.8 %bitcast_dynamic-update-slice_fusion.5 = f32[4,32,32,16,1,128]{5,2,3,1,4,0:T(8,128)} fusion(f32[4,32,32,16,1,128]{5,2,3,1,4,0:T(8,128)} %get-tuple-element.306, s32[]{:T(128)S(6)} %copy.76, f32[32,16,32,128]{3,2,1,0:T(8,128)} %fusion.76, bf16[32,256,16,128]{3,1,2,0:T(8,128)(2,1)} %get-tuple-element.328, f32[32,16,32,256]{3,2,1,0:T(8,128)} %get-tuple-element.283, ...), kind=kOutput, calls=%fused_computation.10.clone.1 | convolution fusion | flops 1092616192 | bytes 67182592 | tf_op jit(solution)/shard_map/while/body/eval_jaxpr/bqkgt,btkd->bqkgd/dot_general | solution.py:66
  291.4 25.2 %fusion.72 = (f32[32,32,16]{1,2,0:T(8,128)S(1)}, f32[32,16,32,256]{3,2,1,0:T(8,128)}) fusion(pred[32,256]{1,0:T(8,128)(4,1)S(1)} %compare_bitcast_fusion.2, bf16[32,256,16,128]{3,1,2,0:T(8,128)(2,1)} %get-tuple-element.326, bf16[32,32,16,1,128]{4,2,1,0,3:T(8,128)(2,1)} %constant_dynamic-slice_fusion.2), kind=kOutput, calls=%fused_computation.7.clone.1 | convolution fusion | flops 1086308352 | bytes 54599680 | tf_op jit(solution)/shard_map/while/body/eval_jaxpr/bqkgd,btkd->bqkgt/dot_general | solution.py:58
  316.7 10.2 fusion.73
  337.7 7.6 fusion.76
  345.3 23.8 %bitcast_dynamic-update-slice_fusion.5 = f32[4,32,32,16,1,128]{5,2,3,1,4,0:T(8,128)} fusion(f32[4,32,32,16,1,128]{5,2,3,1,4,0:T(8,128)} %get-tuple-element.306, s32[]{:T(128)S(6)} %copy.76, f32[32,16,32,128]{3,2,1,0:T(8,128)} %fusion.76, bf16[32,256,16,128]{3,1,2,0:T(8,128)(2,1)} %get-tuple-element.328, f32[32,16,32,256]{3,2,1,0:T(8,128)} %get-tuple-element.283, ...), kind=kOutput, calls=%fused_computation.10.clone.1 | convolution fusion | flops 1092616192 | bytes 67182592 | tf_op jit(solution)/shard_map/while/body/eval_jaxpr/bqkgt,btkd->bqkgd/dot_general | solution.py:66
  375.8 25.2 %fusion.72 = (f32[32,32,16]{1,2,0:T(8,128)S(1)}, f32[32,16,32,256]{3,2,1,0:T(8,128)}) fusion(pred[32,256]{1,0:T(8,128)(4,1)S(1)} %compare_bitcast_fusion.2, bf16[32,256,16,128]{3,1,2,0:T(8,128)(2,1)} %get-tuple-element.326, bf16[32,32,16,1,128]{4,2,1,0,3:T(8,128)(2,1)} %constant_dynamic-slice_fusion.2), kind=kOutput, calls=%fused_computation.7.clone.1 | convolution fusion | flops 1086308352 | bytes 54599680 | tf_op jit(solution)/shard_map/while/body/eval_jaxpr/bqkgd,btkd->bqkgt/dot_general | solution.py:58
  401.1 10.2 fusion.73
  422.1 7.6 fusion.76
  429.7 23.8 %bitcast_dynamic-update-slice_fusion.5 = f32[4,32,32,16,1,128]{5,2,3,1,4,0:T(8,128)} fusion(f32[4,32,32,16,1,128]{5,2,3,1,4,0:T(8,128)} %get-tuple-element.306, s32[]{:T(128)S(6)} %copy.76, f32[32,16,32,128]{3,2,1,0:T(8,128)} %fusion.76, bf16[32,256,16,128]{3,1,2,0:T(8,128)(2,1)} %get-tuple-element.328, f32[32,16,32,256]{3,2,1,0:T(8,128)} %get-tuple-element.283, ...), kind=kOutput, calls=%fused_computation.10.clone.1 | convolution fusion | flops 1092616192 | bytes 67182592 | tf_op jit(solution)/shard_map/while/body/eval_jaxpr/bqkgt,btkd->bqkgd/dot_general | solution.py:66
  460.2 25.2 %fusion.72 = (f32[32,32,16]{1,2,0:T(8,128)S(1)}, f32[32,16,32,256]{3,2,1,0:T(8,128)}) fusion(pred[32,256]{1,0:T(8,128)(4,1)S(1)} %compare_bitcast_fusion.2, bf16[32,256,16,128]{3,1,2,0:T(8,128)(2,1)} %get-tuple-element.326, bf16[32,32,16,1,128]{4,2,1,0,3:T(8,128)(2,1)} %constant_dynamic-slice_fusion.2), kind=kOutput, calls=%fused_computation.7.clone.1 | convolution fusion | flops 1086308352 | bytes 54599680 | tf_op jit(solution)/shard_map/while/body/eval_jaxpr/bqkgd,btkd->bqkgt/dot_general | solution.py:58
  485.5 10.2 fusion.73
  506.5 7.6 fusion.76
  514.1 23.8 %bitcast_dynamic-update-slice_fusion.5 = f32[4,32,32,16,1,128]{5,2,3,1,4,0:T(8,128)} fusion(f32[4,32,32,16,1,128]{5,2,3,1,4,0:T(8,128)} %get-tuple-element.306, s32[]{:T(128)S(6)} %copy.76, f32[32,16,32,128]{3,2,1,0:T(8,128)} %fusion.76, bf16[32,256,16,128]{3,1,2,0:T(8,128)(2,1)} %get-tuple-element.328, f32[32,16,32,256]{3,2,1,0:T(8,128)} %get-tuple-element.283, ...), kind=kOutput, calls=%fused_computation.10.clone.1 | convolution fusion | flops 1092616192 | bytes 67182592 | tf_op jit(solution)/shard_map/while/body/eval_jaxpr/bqkgt,btkd->bqkgd/dot_general | solution.py:66
  539.1 30.9 %all-reduce.5.cloned.1.call-done = f32[4,32,32,16,1]{2,3,4,1,0:T(8,128)} async-done(((f32[4,32,32,16,1]{2,3,4,1,0:T(8,128)}), f32[4,32,32,16,1]{2,3,4,1,0:T(8,128)}) %all-reduce.5.cloned.1.call-update) | async-done | bytes 262160 | tf_op jit(solution)/shard_map/pmax | solution.py:71
  572.9 23.1 %broadcast_multiply_fusion = f32[4,32,32,16,1,128]{5,2,3,1,4,0:T(8,128)} fusion(f32[4,32,32,16,1,128]{5,2,3,1,4,0:T(8,128)} %get-tuple-element.67, f32[4,32,32,16]{2,3,1,0:T(8,128)S(1)} %get-tuple-element.179), kind=kLoop, calls=%fused_computation.43 | loop fusion | flops 8388608 | bytes 67371008 | tf_op jit(solution)/shard_map/mul | solution.py:74
  597.2 225.2 %reduce-scatter.7.cloned.1.call-done = f32[1,32,32,16,1,128]{5,2,3,1,4,0:T(8,128)} async-done(((f32[4,32,32,16,1,128]{5,2,3,1,4,0:T(8,128)}), f32[1,32,32,16,1,128]{5,2,3,1,4,0:T(8,128)}) %reduce-scatter.7.cloned.1.call-update) | async-done | bytes 8388624
  822.4 10.9 copy.44
  836.0 33.6 %fusion.36 = f32[1024,4096]{1,0:T(8,128)} fusion(bf16[2048,4096]{1,0:T(8,128)(2,1)} %param.17, f32[128,8,16,128]{3,2,1,0:T(8,128)S(1)} %bitcast.189, f32[128,8,16,128]{3,2,1,0:T(8,128)S(1)} %bitcast.188), kind=kOutput, calls=%fused_computation.56 | convolution fusion | flops 17184063488 | bytes 50331648 | tf_op jit(solution)/shard_map/dot_general | solution.py:76
  870.2 371.6 %all-reduce.7.cloned.1.call-done = f32[1024,4096]{1,0:T(8,128)} async-done(((f32[1024,4096]{1,0:T(8,128)}), f32[1024,4096]{1,0:T(8,128)}) %all-reduce.7.cloned.1.call-update) | async-done | bytes 16777232 | tf_op jit(solution)/shard_map/psum | solution.py:77
  1249.0 7.2 multiply_multiply_fusion
  (146 shorter events, 133.2 us)
Async XLA Ops:
  7.2 193.0 %all-gather.2.cloned.1.call-start = ((), (), s32[]{:S(2)}) async-start(), calls=%async_computation.2 | async-start | bytes 20971520 | tf_op jit(solution)/shard_map/all_gather | solution.py:48
  7.9 24.3 %copy-start.7 = (bf16[32,32,4096]{2,1,0:T(8,128)(2,1)S(1)}, bf16[32,32,4096]{2,1,0:T(8,128)(2,1)}, u32[]{:S(2)}) copy-start(bf16[32,32,4096]{2,1,0:T(8,128)(2,1)} %param.13) | copy-start | bytes 25165828
  7.9 24.3 %copy-start.11 = (bf16[4096,2048]{1,0:T(8,128)(2,1)S(1)}, bf16[4096,2048]{1,0:T(8,128)(2,1)}, u32[]{:S(2)}) copy-start(bf16[4096,2048]{1,0:T(8,128)(2,1)} %param.14) | copy-start | bytes 50331652
  62.8 5.4 copy-start.8
  62.8 5.5 copy-start.10
  68.3 15.0 %slice-start.2 = ((s8[8388608]{0:T(1024)(128)(4,1)}), s8[4194304]{0:T(1024)(128)(4,1)S(1)}, s32[]{:S(2)}) async-start(s8[8388608]{0:T(1024)(128)(4,1)} %bitcast.178), calls=%async_computation.9 | async-start | bytes 8388608
  75.9 7.5 slice-start.3
  94.3 475.7 %all-reduce.5.cloned.1.call-start = ((), (), s32[]{:S(2)}) async-start(), calls=%async_computation.3 | async-start | bytes 2097152 | tf_op jit(solution)/shard_map/pmax | solution.py:71
  123.9 2.0 copy-start.2
  174.9 25.3 %copy-start.4 = (f32[4,32,32,16,1]{2,3,1,4,0:T(8,128)S(1)}, f32[4,32,32,16,1]{2,3,1,4,0:T(8,128)}, u32[]{:S(2)}) copy-start(f32[4,32,32,16,1]{2,3,1,4,0:T(8,128)} %copy-done.3) | copy-start | bytes 786436
  176.3 2.0 copy-start.6
  232.3 11.3 copy-start
  242.5 7.4 slice-start
  243.6 6.4 slice-start.1
  250.0 3.4 copy-start.1
  316.7 11.3 copy-start
  326.9 7.4 slice-start
  328.0 6.4 slice-start.1
  334.4 3.4 copy-start.1
  401.1 11.3 copy-start
  411.3 7.4 slice-start
  412.3 6.4 slice-start.1
  418.7 3.4 copy-start.1
  485.5 11.3 copy-start
  495.7 7.4 slice-start
  496.7 6.4 slice-start.1
  503.1 3.4 copy-start.1
  539.1 57.0 %reduce-scatter.9.cloned.1.call-start = ((), (), s32[]{:S(2)}) async-start(), calls=%async_computation.6 | async-start | bytes 1310720
  572.9 249.6 %reduce-scatter.7.cloned.1.call-start = ((), (), s32[]{:S(2)}) async-start(), calls=%async_computation.5 | async-start | bytes 41943040
  596.0 645.9 %all-reduce.7.cloned.1.call-start = ((), (), s32[]{:S(2)}) async-start(), calls=%async_computation.4 | async-start | bytes 33554432 | tf_op jit(solution)/shard_map/psum | solution.py:77
  1241.9 14.3 %slice-start.4 = ((s8[8388608]{0:T(1024)(128)(4,1)}), s8[4194304]{0:T(1024)(128)(4,1)S(1)}, s32[]{:S(2)}) async-start(s8[8388608]{0:T(1024)(128)(4,1)} %bitcast.193), calls=%async_computation.11 | async-start | bytes 8388608
  1249.0 7.2 slice-start.5
  (3 other events, 2.7 us)
Sparse Core Ops, SparseCore 0:
  94.5 105.6 all-gather.1
  539.2 30.8 all-reduce.4
  573.1 19.4 reduce-scatter.8
  596.1 226.2 reduce-scatter.6
  869.7 372.1 all-reduce.6
where the time goes:
time: 1280 us; the launch traced here: 1270 us
  waiting for transfers between devices  647 us (51%)
  matrix products  368 us (29%)
  local copies, waits for them, and re-layouts  116 us (9%)
  other arithmetic  112 us (9%)
  between operations  14.5 us (1%)
    psum x1, waiting for transfers between devices, local_step(): mixed_sum = lax.psum(mixed_part, 'tp')  372 us
    unnamed x7, waiting for transfers between devices  225 us
    dot_general x4, matrix products, block_attention(): jnp.einsum('bqkgd,btkd->bqkgt', q_blk, cache_k, preferred_element_type=jn...  101 us
    dot_general x4, matrix products, block_attention(): jnp.einsum('bqkgt,btkd->bqkgd', p_cache.astype(jnp.bfloat16), cache_v, pr...  95.2 us
    unnamed x36, local copies, waits for them, and re-layouts  71.7 us
    dot_general x4, matrix products, block_attention(): jnp.einsum('bqkgd,btkd->bqkgt', q_blk, chunk_k, preferred_element_type=jn...  41 us
    reduce_sum x8, other arithmetic, block_attention(): den_sum = jnp.sum(p_cache, axis=-1) + jnp.sum(p_chunk, axis=-1)  36.6 us
    dot_general x1, matrix products, local_step(): mixed_part = jnp.dot(attn_out, w_out, preferred_element_type=jnp.float32)  33.6 us
  transfers between devices with their start and end apart: 5, of which 4 were waited for; matrix products, arithmetic and copies ran while one was open for 8% of the time, Pallas kernels for 0%

commit v1 on v0

v1 whole, which is shorter than its diff:
```python
import functools

import jax
import jax.numpy as jnp
from jax import lax
from jax.experimental import pallas as pl
from jax.experimental.pallas import tpu as pltpu
from jax.sharding import PartitionSpec as P

NORM_EPS = 1e-6
ROPE_BASE = 500000.0
NEG = -1e30
FLOOR = -5e29
LOG2E = 1.4426950408889634
HD = 128
LAG = 1
GROUPS = (4, 8, 8, 8, 4)
P_GROUPS = (3, 1, 1)
VMEM_LIMIT = 60 * 1024 * 1024


def cost(micros, moved):
    return pl.CostEstimate(flops=int(micros * 9e8), bytes_accessed=moved, transcendentals=0)


def params():
    return pltpu.CompilerParams(dimension_semantics=("arbitrary",), vmem_limit_bytes=VMEM_LIMIT)


def rope_body(total_width, n_heads, raw, own, peer, gain, cos, sin, out):
    inv = lax.rsqrt((own[...] + peer[...]) / total_width + NORM_EPS)
    inv = jnp.broadcast_to(inv, (HD, HD)).T
    cos_t = cos[...]
    sin_t = sin[...]
    for h in range(n_heads):
        cols = slice(h * HD, (h + 1) * HD)
        u = raw[:, cols] * inv * gain[:, cols]
        out[:, cols] = (u * cos_t + pltpu.roll(u, HD // 2, 1) * sin_t).astype(jnp.bfloat16)


def rope(raw, own, peer, gain, cos, sin, row0, total_width, tokens, raw_row0):
    width = raw.shape[1]
    block = 128
    base = row0 // block
    off = (row0 - raw_row0) // block
    return pl.pallas_call(
        functools.partial(rope_body, total_width, width // HD),
        grid=(tokens // block,),
        in_specs=[pl.BlockSpec((block, width), lambda i: (i + off, 0)),
                  pl.BlockSpec((1, block), lambda i: (0, i + off)),
                  pl.BlockSpec((1, block), lambda i: (0, i + off)),
                  pl.BlockSpec((1, width), lambda i: (0, 0)),
                  pl.BlockSpec((block, HD), lambda i: (i + base, 0)),
                  pl.BlockSpec((block, HD), lambda i: (i + base, 0))],
        out_specs=pl.BlockSpec((block, width), lambda i: (i, 0)),
        out_shape=jax.ShapeDtypeStruct((tokens, width), jnp.bfloat16),
        compiler_params=params(),
        cost_estimate=cost(tokens * 0.005, tokens * width * 6),
        name="rope",
    )(raw, own, peer, gain, cos, sin)


def attn_body(n_heads, row0, chunk, slots, pitch, sc_ref, qa, qb, qc, qd, ck, cv, kc, vc, keep, give, stat, ks, vs):
    b = pl.program_id(0)
    cp = sc_ref[0]
    valid_len = sc_ref[1 + row0 + b]
    tokens = 4 * chunk
    keys = slots + chunk
    for t in range(slots):
        ks[t * pitch:t * pitch + n_heads, :] = ck[0, t].astype(jnp.float32)
        vs[t * pitch:t * pitch + n_heads, :] = cv[0, t].astype(jnp.float32)
    row = lax.broadcasted_iota(jnp.int32, (keys, tokens), 0)
    col = lax.broadcasted_iota(jnp.int32, (keys, tokens), 1)
    part = col // chunk
    rel = jnp.where(part == 1, 2, jnp.where(part == 2, 1, part))
    query = jnp.bitwise_xor(rel, cp) * chunk + col % chunk
    chunk_key = cp * chunk + row - slots
    ok = jnp.where(row < slots, row + cp * slots - valid_len, chunk_key - query - 1) < 0
    scale = HD ** -0.5 * LOG2E
    contract_last = (((1,), (1,)), ((), ()))
    contract_first = (((0,), (0,)), ((), ()))

    def cols(h):
        return slice(h * HD, (h + 1) * HD)

    def scores(h):
        q = jnp.concatenate([qa[0, :, cols(h)], qb[0, :, cols(h)], qc[0, :, cols(h)], qd[0, :, cols(h)]], axis=0)
        k = jnp.concatenate([ks[pl.ds(h, slots, stride=pitch), :].astype(jnp.bfloat16), kc[0, :, cols(h)]], axis=0)
        return lax.dot_general(k, q, contract_last, preferred_element_type=jnp.float32)

    def soft(h, s):
        s = jnp.where(ok, s * scale, NEG)
        top = jnp.maximum(jnp.max(s, axis=0, keepdims=True), FLOOR)
        p = jnp.exp2(s - top)
        stat[0, h:h + 1, :] = top
        stat[0, n_heads + h:n_heads + h + 1, :] = jnp.sum(p, axis=0, keepdims=True)
        return p.astype(jnp.bfloat16)

    def values(h, p):
        v = jnp.concatenate([vs[pl.ds(h, slots, stride=pitch), :].astype(jnp.bfloat16), vc[0, :, cols(h)]], axis=0)
        num = lax.dot_general(p, v, contract_first, preferred_element_type=jnp.float32)
        keep[0, :, cols(h)] = num[:2 * chunk]
        give[0, :, cols(h)] = num[2 * chunk:]

    s_live, p_live = {}, {}
    for step in range(n_heads + 2 * LAG):
        if step < n_heads:
            s_live[step] = scores(step)
        h = step - LAG
        if 0 <= h < n_heads:
            p_live[h] = soft(h, s_live.pop(h))
        h = step - 2 * LAG
        if 0 <= h < n_heads:
            values(h, p_live.pop(h))


def attention(scalars, q_parts, cache_k, cache_v, k_new, v_new, row0):
    rows, chunk, width = q_parts[0].shape
    _, slots, n_heads, _ = cache_k.shape
    pitch = n_heads + 8
    q_spec = pl.BlockSpec((1, chunk, width), lambda b, s: (b, 0, 0))
    new_spec = pl.BlockSpec((1, chunk, width), lambda b, s: (b + row0, 0, 0))
    cache_spec = pl.BlockSpec((1, slots, n_heads, HD), lambda b, s: (b + row0, 0, 0, 0))
    out_spec = pl.BlockSpec((1, 2 * chunk, width), lambda b, s: (b, 0, 0))
    stat_spec = pl.BlockSpec((1, 2 * n_heads, 4 * chunk), lambda b, s: (b, 0, 0))
    out = jax.ShapeDtypeStruct((rows, 2 * chunk, width), jnp.float32)
    return pl.pallas_call(
        functools.partial(attn_body, n_heads, row0, chunk, slots, pitch),
        grid_spec=pltpu.PrefetchScalarGridSpec(
            num_scalar_prefetch=1, grid=(rows,),
            in_specs=[q_spec] * 4 + [cache_spec] * 2 + [new_spec] * 2,
            out_specs=[out_spec] * 2 + [stat_spec],
            scratch_shapes=[pltpu.VMEM((slots * pitch, HD), jnp.float32)] * 2),
        out_shape=[out, out, jax.ShapeDtypeStruct((rows, 2 * n_heads, 4 * chunk), jnp.float32)],
        compiler_params=params(),
        cost_estimate=cost(rows * 3.9, rows * slots * width * 6),
        name="attention",
    )(scalars, *q_parts, cache_k, cache_v, k_new, v_new)


def pair_weights(n_heads, mine, theirs):
    theirs = pltpu.roll(theirs, mine.shape[1] // 2, 1)
    return [(s[:n_heads], s[n_heads:]) for s in (mine, theirs)]


def merge_body(n_heads, chunk, span, keep, got, stat, gstat, out, ostat):
    packed = jnp.zeros((2 * n_heads, 4 * chunk), jnp.float32)
    lane = lax.broadcasted_iota(jnp.int32, (2 * n_heads, 4 * chunk), 1) // chunk
    for i in range(span):
        (t0, d0), (t1, d1) = pair_weights(n_heads, stat[i], gstat[i])
        top = jnp.maximum(t0, t1)
        w0 = jnp.exp2(t0 - top)
        w1 = jnp.exp2(t1 - top)
        new = jnp.concatenate([top, w0 * d0 + w1 * d1], axis=0)
        packed = jnp.where(lane == i, pltpu.roll(new, ((i - 1) * chunk) % (4 * chunk), 1), packed)
        w = jnp.concatenate([w0, w1], axis=0).T[chunk:2 * chunk]
        for h in range(n_heads):
            cols = slice(h * HD, (h + 1) * HD)
            out[i, :, cols] = keep[i, :, cols] * w[:, h:h + 1] + got[i, :, cols] * w[:, n_heads + h:n_heads + h + 1]
    ostat[0] = packed


def merge(keep, got, stat, gstat, n_heads):
    rows, chunk2, width = keep.shape
    chunk = chunk2 // 2
    span = 4
    half = pl.BlockSpec((span, chunk, width), lambda i: (i, 1, 0))
    stats = pl.BlockSpec((span, 2 * n_heads, 4 * chunk), lambda i: (i, 0, 0))
    return pl.pallas_call(
        functools.partial(merge_body, n_heads, chunk, span),
        grid=(rows // span,),
        in_specs=[half, half, stats, stats],
        out_specs=[pl.BlockSpec((span, chunk, width), lambda i: (i, 0, 0)),
                   pl.BlockSpec((1, 2 * n_heads, 4 * chunk), lambda i: (i, 0, 0))],
        out_shape=[jax.ShapeDtypeStruct((rows, chunk, width), jnp.float32),
                   jax.ShapeDtypeStruct((rows // span, 2 * n_heads, 4 * chunk), jnp.float32)],
        compiler_params=params(),
        cost_estimate=cost(rows * 0.3, rows * chunk * width * 12),
        name="merge",
    )(keep, got, stat, gstat)


def finish_body(n_heads, chunk, span, keep, got, far, stat, gstat, fstat, out):
    for i in range(span):
        pairs = pair_weights(n_heads, stat[i], gstat[i])
        third = pltpu.roll(fstat[0], (-i * chunk) % (4 * chunk), 1)
        pairs.append((third[:n_heads], third[n_heads:]))
        top = jnp.maximum(jnp.maximum(pairs[0][0], pairs[1][0]), pairs[2][0])
        ws = [jnp.exp2(t - top) for t, _ in pairs]
        den = ws[0] * pairs[0][1] + ws[1] * pairs[1][1] + ws[2] * pairs[2][1]
        inv = 1.0 / den
        w = jnp.concatenate([x * inv for x in ws], axis=0).T[:chunk]
        for h in range(n_heads):
            cols = slice(h * HD, (h + 1) * HD)
            val = keep[i, :, cols] * w[:, h:h + 1]
            val = val + got[i, :, cols] * w[:, n_heads + h:n_heads + h + 1]
            val = val + far[i, :, cols] * w[:, 2 * n_heads + h:2 * n_heads + h + 1]
            out[i, :, cols] = val.astype(jnp.bfloat16)


def finish(keep, got, far, stat, gstat, fstat, n_heads):
    rows, chunk2, width = keep.shape
    chunk = chunk2 // 2
    span = 4
    half = pl.BlockSpec((span, chunk, width), lambda i: (i, 0, 0))
    stats = pl.BlockSpec((span, 2 * n_heads, 4 * chunk), lambda i: (i, 0, 0))
    return pl.pallas_call(
        functools.partial(finish_body, n_heads, chunk, span),
        grid=(rows // span,),
        in_specs=[half, half, half, stats, stats, pl.BlockSpec((1, 2 * n_heads, 4 * chunk), lambda i: (i, 0, 0))],
        out_specs=half,
        out_shape=jax.ShapeDtypeStruct((rows, chunk, width), jnp.bfloat16),
        compiler_params=params(),
        cost_estimate=cost(rows * 0.4, rows * chunk * width * 14),
        name="finish",
    )(keep, got, far, stat, gstat, fstat)


def project_body(half, steps, block, sizes, row0, sc_ref, *refs):
    n = len(sizes)
    o_in, ro_in = refs[:n], refs[n:2 * n]
    w_own, w_near, w_far, x_hbm, gain = refs[2 * n:2 * n + 5]
    out_hbm, o, ro, x, acc, ssq, sem, out_sem = refs[-8:]
    j = pl.program_id(0)
    core = sc_ref[0] % 2
    tp = sc_ref[1]
    first = pl.multiple_of(core * half, half)
    second = pl.multiple_of((1 - core) * half, half)
    f32 = jnp.float32
    tokens = sum(sizes)
    residual = pltpu.make_async_copy(x_hbm.at[pl.ds(row0, tokens)], x, sem)

    @pl.when(j == 0)
    def _():
        residual.start()
        at = 0
        for k, size in enumerate(sizes):
            o[at:at + size, :] = o_in[k][...]
            ro[at:at + size, :] = ro_in[k][...]
            at += size

    def own():
        return (jnp.dot(o[:, pl.ds(first, half)], w_own[pl.ds(first, half), :], preferred_element_type=f32)
                + jnp.dot(o[:, pl.ds(second, half)], w_own[pl.ds(second, half), :], preferred_element_type=f32))

    def peer():
        return (jnp.dot(ro[:, pl.ds(first, half)], w_near[...], preferred_element_type=f32)
                + jnp.dot(ro[:, pl.ds(second, half)], w_far[...], preferred_element_type=f32))

    def put(a):
        acc[j] = a
        sq = jnp.sum(a * a, axis=-1, keepdims=True)
        ssq[...] = jnp.where(j == 0, sq, ssq[...] + sq)

    @pl.when(tp == 0)
    def _():
        put(own() + peer())

    @pl.when(tp != 0)
    def _():
        put(peer() + own())

    @pl.when(j == steps - 1)
    def _():
        residual.wait()
        inv = lax.rsqrt(ssq[...] / (steps * block) + NORM_EPS)
        for k in range(steps):
            cols = slice(k * block, (k + 1) * block)
            y = x[:, cols].astype(f32) + acc[k] * inv * gain[:, cols].astype(f32)
            x[:, cols] = y.astype(jnp.bfloat16)
        result = pltpu.make_async_copy(x, out_hbm.at[pl.ds(row0, tokens)], out_sem)
        result.start()
        result.wait()


def project(scalars, o_list, ro_list, w_own, w_near, w_far, x, gain, row0, so_far):
    sizes = tuple(o.shape[0] for o in o_list)
    tokens, width = sum(sizes), o_list[0].shape[1]
    half = width // 2
    model = w_own.shape[1]
    block = 512
    steps = model // block
    once = pl.Buffered(1)
    extra = [] if so_far is None else [so_far]
    o_specs = [pl.BlockSpec((size, width), lambda j, s: (0, 0), pipeline_mode=once) for size in sizes]
    return pl.pallas_call(
        functools.partial(project_body, half, steps, block, sizes, row0),
        grid_spec=pltpu.PrefetchScalarGridSpec(
            num_scalar_prefetch=1, grid=(steps,),
            in_specs=o_specs + o_specs + [
                pl.BlockSpec((width, block), lambda j, s: (0, j)),
                pl.BlockSpec((half, block), lambda j, s: (0, j)),
                pl.BlockSpec((half, block), lambda j, s: (0, j)),
                pl.BlockSpec(memory_space=pl.ANY),
                pl.BlockSpec((1, model), lambda j, s: (0, 0))] + [pl.BlockSpec(memory_space=pl.ANY)] * len(extra),
            out_specs=pl.BlockSpec(memory_space=pl.ANY),
            scratch_shapes=[pltpu.VMEM((tokens, width), jnp.bfloat16), pltpu.VMEM((tokens, width), jnp.bfloat16),
                            pltpu.VMEM((tokens, model), jnp.bfloat16),
                            pltpu.VMEM((steps, tokens, block), jnp.float32), pltpu.VMEM((tokens, 1), jnp.float32),
                            pltpu.SemaphoreType.DMA, pltpu.SemaphoreType.DMA]),
        out_shape=jax.ShapeDtypeStruct(x.shape, jnp.bfloat16),
        input_output_aliases={2 * len(sizes) + 6: 0} if extra else {},
        compiler_params=params(),
        cost_estimate=cost(tokens * 0.045, 4 * width * model),
        name="project",
    )(scalars, *o_list, *ro_list, w_own, w_near, w_far, x, gain, *extra)


def solution(mesh):
    tp_size = mesh.shape['tp']
    OTHER_CHIP = [(0, 2), (2, 0), (1, 3), (3, 1)]
    OTHER_CORE = [(0, 1), (1, 0), (2, 3), (3, 2)]
    OTHER_HALF = [(0, 1), (1, 0)]

    def local_step(x_chunk, w_query, w_key, w_value, w_out, q_gain, k_gain, post_gain, cache_k, cache_v, prefix_len):
        rows, chunk, model = x_chunk.shape
        n_heads = cache_k.shape[2]
        width = n_heads * HD
        total_width = width * tp_size
        cp = lax.axis_index('cp')
        tp = lax.axis_index('tp')
        core = cp % 2
        tokens = x_chunk.reshape(rows * chunk, model)
        scalars = jnp.concatenate([cp[None], prefix_len]).astype(jnp.int32)
        places = jnp.stack([cp, tp]).astype(jnp.int32)
        positions = prefix_len[:, None] + cp * chunk + jnp.arange(chunk, dtype=jnp.int32)[None, :]
        inv_freq = ROPE_BASE ** (-(jnp.arange(HD // 2, dtype=jnp.float32) * 2.0 / HD))
        angles = positions.astype(jnp.float32).reshape(-1, 1) * inv_freq[None, :]
        cos_h, sin_h = jnp.cos(angles), jnp.sin(angles)
        cos = jnp.concatenate([cos_h, cos_h], axis=-1)
        sin = jnp.concatenate([-sin_h, sin_h], axis=-1)
        qg = q_gain.astype(jnp.float32)[None]
        kg = k_gain.astype(jnp.float32)[None]
        pg = post_gain[None]

        def after(value, done):
            return lax.optimization_barrier((value, done))[0]

        def swap_sums(raw):
            own = jnp.sum(raw * raw, axis=-1)[None]
            return own, lax.ppermute(own, 'tp', OTHER_HALF)

        def w_slice(lo, size, done):
            return lax.dynamic_slice_in_dim(after(w_out, done), core * (width // 2) + lo, size, axis=0)

        def rotated(raw, sums, gain, row0, count, raw_row0, done):
            return rope(raw, *sums, after(gain, done), cos, sin, row0, total_width, count, raw_row0)

        def spread(q, r):
            q = q.reshape(r, chunk, width)
            q_chip = lax.ppermute(q, 'cp', OTHER_CHIP)
            q_core = lax.ppermute(q, 'cp', OTHER_CORE)
            return q, q_chip, q_core, lax.ppermute(q_chip, 'cp', OTHER_CORE)

        f32 = jnp.float32
        starts = [sum(GROUPS[:g]) for g in range(len(GROUPS))]
        last_group = len(GROUPS) - 1
        cut = GROUPS[0] * chunk
        raw0 = jnp.dot(tokens[:cut], w_query, preferred_element_type=f32)
        sums0 = swap_sums(raw0)
        ws0 = w_slice(0, 128, raw0)
        ws1 = w_slice(128, 128, raw0)
        q0 = rotated(raw0, sums0, qg, 0, cut, 0, ws1)
        q_sets = [spread(q0, GROUPS[0])]
        wn0 = lax.ppermute(after(ws0, sums0[1]), 'tp', OTHER_HALF)
        raw1 = jnp.dot(after(tokens, q0), w_query, preferred_element_type=f32)
        sums1 = swap_sums(raw1)
        ws2 = w_slice(256, width // 2 - 256, raw1)
        last = ws2
        for g in range(1, len(GROUPS)):
            last = rotated(raw1, sums1, qg, starts[g] * chunk, GROUPS[g] * chunk, 0, last)
            q_sets.append(spread(last, GROUPS[g]))
        wn1 = lax.ppermute(after(ws1, sums1[1]), 'tp', OTHER_HALF)
        k_raw = jnp.dot(after(tokens, last), w_key, preferred_element_type=f32)
        k_sums = swap_sums(k_raw)
        v_flat = jnp.dot(after(tokens, k_sums[0]), w_value, preferred_element_type=f32).astype(jnp.bfloat16)
        k_flat = rotated(k_raw, k_sums, kg, 0, rows * chunk, 0, v_flat)
        wn2 = lax.ppermute(after(ws2, k_sums[1]), 'tp', OTHER_HALF)
        k_new = k_flat.reshape(rows, chunk, width)
        v_new = v_flat.reshape(rows, chunk, width)

        parts = []
        last = k_flat
        merged = []

        def do_merge(g, done):
            keep, _, stat, got, gstat = parts[g]
            send, sstat = merge(keep, got, after(stat, done), gstat, n_heads)
            merged.append((lax.ppermute(send, 'cp', OTHER_CHIP), lax.ppermute(sstat, 'cp', OTHER_CHIP)))
            return sstat

        for g in range(len(GROUPS)):
            keep, give, stat = attention(after(scalars, last), q_sets[g], cache_k, cache_v, k_new, v_new, starts[g])
            parts.append((keep, give, stat, lax.ppermute(give, 'cp', OTHER_CORE), lax.ppermute(stat, 'cp', OTHER_CORE)))
            last = stat
            if g >= 1:
                last = do_merge(g - 1, last)
        last = do_merge(last_group, last)
        w_near = jnp.concatenate([after(wn0, last), wn1, wn2], axis=0)
        w_far = lax.ppermute(w_near, 'cp', OTHER_CORE)
        last = w_near

        block_out = None
        g = 0
        for count in P_GROUPS:
            o_list, ro_list = [], []
            first_row = starts[g]
            for _ in range(count):
                keep, give, stat, got, gstat = parts[g]
                far, fstat = merged[g]
                o = finish(keep, got, far, after(stat, last), gstat, fstat, n_heads).reshape(GROUPS[g] * chunk, width)
                o_list.append(o)
                ro_list.append(lax.ppermute(o, 'tp', OTHER_HALF))
                last = o
                g += 1
            block_out = project(after(places, last), o_list, ro_list, w_out, w_near, w_far, tokens, pg, first_row * chunk, block_out)
            last = block_out
        block_out = block_out.reshape(rows, chunk, model)
        shape = (rows, chunk, n_heads, HD)
        return block_out, k_new.reshape(shape), v_new.reshape(shape)

    x_spec = P('dp', 'cp', None)
    head_spec = P('dp', 'cp', 'tp', None)
    in_specs = (x_spec, P(None, 'tp'), P(None, 'tp'), P(None, 'tp'), P('tp', None), P('tp'), P('tp'), P(None), head_spec, head_spec, P('dp'))
    out_specs = (x_spec, head_spec, head_spec)

    return jax.shard_map(local_step, mesh=mesh, in_specs=in_specs, out_specs=out_specs, check_vma=False)
```

time: 1280 us -> 731 us (0.57)
  waiting for transfers between devices: 647 us -> 319 us
  matrix products: 368 us -> 81.5 us
  Pallas kernels: 0 us -> 240 us
  other arithmetic: 112 us -> 5.84 us
  local copies, waits for them, and re-layouts: 116 us -> 46.2 us
  starting transfers between devices: 0.61 us -> 32 us
  between operations: 14.5 us -> 1.29 us
    psum x1 -> x0, waiting for transfers between devices: 372 us -> none  [local_step(): mixed_sum = lax.psum(mixed_part, 'tp')]
    ppermute x0 -> x47, waiting for transfers between devices: none -> 319 us  [the longest x5 112 us: do_merge(): lax.ppermute(sstat, 'cp', OTHER_CHIP)]
    dot_general x20 -> x4, matrix products: 368 us -> 81.5 us  [the longest x1 24.4 us: local_step(): raw1 = jnp.dot(after(tokens, q0), w_query, preferred_element_type=f32)]
    pallas_call x0 -> x24, Pallas kernels: none -> 240 us  [the longest x5 87.2 us: attention(): pl.pallas_call(functools.partial(attn_body, n_heads, row0, chunk, slots,...]
    unnamed x7 -> x0, waiting for transfers between devices: 225 us -> none
    reduce_sum x9 -> x0, other arithmetic: 43.6 us -> none  [the longest x8 36.6 us: block_attention(): den_sum = jnp.sum(p_cache, axis=-1) + jnp.sum(p_chunk, axis=-1)]
    unnamed x36 -> x110, local copies, waits for them, and re-layouts: 71.7 us -> 28.7 us
    mul x3 -> x0, other arithmetic: 33 us -> none  [the longest x2 25.9 us: local_step(): part_num * factor[..., None]]
  transfers between devices with their start and end apart: 5 -> 47, of which waited for: 4 -> 13; matrix products, arithmetic and copies ran while one was open for 8% -> 14% of each run, Pallas kernels for 0% -> 29%
where the time goes in v1:
time: 731 us; the launch traced here: 726 us
  waiting for transfers between devices  319 us (44%)
  Pallas kernels  240 us (33%)
  matrix products  81.5 us (11%)
  local copies, waits for them, and re-layouts  46.2 us (6%)
  starting transfers between devices  32 us (4%)
    ppermute x5, waiting for transfers between devices, do_merge(): lax.ppermute(sstat, 'cp', OTHER_CHIP)  112 us
    ppermute x1, waiting for transfers between devices, local_step(): wn0 = lax.ppermute(after(ws0, sums0[1]), 'tp', OTHER_HALF)  87.9 us
    pallas_call x5, Pallas kernels, attention(): pl.pallas_call(functools.partial(attn_body, n_heads, row0, chunk, slots,...  87.2 us
    pallas_call x3, Pallas kernels, project(): pl.pallas_call(functools.partial(project_body, half, steps, block, sizes,...  72.4 us
    ppermute x5, waiting for transfers between devices, local_step(): ro_list.append(lax.ppermute(o, 'tp', OTHER_HALF))  65.3 us
    pallas_call x5, Pallas kernels, finish(): pl.pallas_call(functools.partial(finish_body, n_heads, chunk, span), grid...  30.8 us
    unnamed x110, local copies, waits for them, and re-layouts  28.7 us
    pallas_call x5, Pallas kernels, merge(): pl.pallas_call(functools.partial(merge_body, n_heads, chunk, span), grid=...  26.4 us
  transfers between devices with their start and end apart: 47, of which 13 were waited for; matrix products, arithmetic and copies ran while one was open for 14% of the time, Pallas kernels for 29%

profile of v1, /device:TPU:0, one launch (start us, length us, event | category | flops | bytes accessed | tf_op | source)
XLA Modules:
  0.0 725.8 jit_solution(7003046245819617933)
XLA Ops:
  2.0 9.2 %multiply_reduce_fusion.2 = (f32[128]{0:T(128)S(1)}, f32[128,2048]{1,0:T(8,128)}) fusion(bf16[128,4096]{1,0:T(8,128)(2,1)S(1)} %bitcast.55, bf16[4096,2048]{1,0:T(8,128)(2,1)} %param.12), kind=kOutput, calls=%fused_computation.3 | convolution fusion | flops 2148007936 | bytes 18874880 | tf_op jit(solution)/shard_map/dot_general | solution.py:359
  27.5 24.4 %multiply_reduce_fusion.1 = (f32[1024]{0:T(1024)S(1)}, f32[1024,2048]{1,0:T(8,128)}) fusion(bf16[1024,4096]{1,0:T(8,128)(2,1)} %bitcast.36, bf16[4096,2048]{1,0:T(8,128)(2,1)} %param.12), kind=kOutput, calls=%fused_computation.1 | convolution fusion | flops 17184063488 | bytes 33558528 | tf_op jit(solution)/shard_map/dot_general | solution.py:366
  52.4 6.2 constant_dynamic-slice_fusion.1
  70.8 24.3 %multiply_reduce_fusion = (f32[1024]{0:T(1024)S(1)}, f32[1024,2048]{1,0:T(8,128)}) fusion(bf16[1024,4096]{1,0:T(8,128)(2,1)} %bitcast.37, bf16[4096,2048]{1,0:T(8,128)(2,1)} %param.13), kind=kOutput, calls=%fused_computation | convolution fusion | flops 17184063488 | bytes 33558528 | tf_op jit(solution)/shard_map/dot_general | solution.py:374
  97.6 23.7 %convolution_convert_fusion = bf16[1024,2048]{1,0:T(8,128)(2,1)} fusion(bf16[1024,4096]{1,0:T(8,128)(2,1)} %bitcast.38, bf16[4096,2048]{1,0:T(8,128)(2,1)} %param.14), kind=kOutput, calls=%fused_computation.2 | convolution fusion | flops 17181966336 | bytes 29360128 | tf_op jit(solution)/shard_map/dot_general | solution.py:376
  122.9 9.2 %rope.11 = bf16[1024,2048]{1,0:T(8,128)(2,1)} custom-call(f32[1024,2048]{1,0:T(8,128)} %get-tuple-element.129.raw, f32[1,1024]{1,0:T(1,128)} %bitcast.94, f32[1,1024]{1,0:T(1,128)} %copy-done.51, f32[1,2048]{1,0:T(1,128)} %bitcast.90, f32[1024,128]{1,0:T(8,128)} %get-tuple-element.130.cos, f32[1024,128]{1,0:T(8,128)} %get-tuple-element.131.sin), custom_call_target="tpu_custom_call" | custom-call | flops 4608000000 | bytes 12582912 | tf_op jit(solution)/shard_map/rope/pallas_call | solution.py:46
  133.0 12.2 %attention.5 = (f32[4,64,2048]{2,1,0:T(8,128)}, f32[4,64,2048]{2,1,0:T(8,128)}, f32[4,32,128]{2,1,0:T(8,128)}) custom-call(s32[33]{0:T(128)} %pad_add_fusion.1.sc_ref, bf16[4,32,2048]{2,1,0:T(8,128)(2,1)} %bitcast.65, bf16[4,32,2048]{2,1,0:T(8,128)(2,1)} %copy-done.12, bf16[4,32,2048]{2,1,0:T(8,128)(2,1)} %copy-done.13, bf16[4,32,2048]{2,1,0:T(8,128)(2,1)} %copy-done.15, ...), custom_call_target="tpu_custom_call" | custom-call | flops 14040000512 | bytes 12582912 | tf_op jit(solution)/shard_map/attention/pallas_call | solution.py:127
  147.7 20.7 %attention.6 = (f32[8,64,2048]{2,1,0:T(8,128)}, f32[8,64,2048]{2,1,0:T(8,128)}, f32[8,32,128]{2,1,0:T(8,128)}) custom-call(s32[33]{0:T(128)} %pad_add_fusion.1.sc_ref, bf16[8,32,2048]{2,1,0:T(8,128)(2,1)} %bitcast.71, bf16[8,32,2048]{2,1,0:T(8,128)(2,1)} %collective-permute-done.7.qb, bf16[8,32,2048]{2,1,0:T(8,128)(2,1)} %collective-permute-done.8.qc, ...), custom_call_target="tpu_custom_call" | custom-call | flops 28080001024 | bytes 25165824 | tf_op jit(solution)/shard_map/attention/pallas_call | solution.py:127
  169.4 6.7 collective-permute-done.10.gstat
  182.0 20.9 %attention.7 = (f32[8,64,2048]{2,1,0:T(8,128)}, f32[8,64,2048]{2,1,0:T(8,128)}, f32[8,32,128]{2,1,0:T(8,128)}) custom-call(s32[33]{0:T(128)} %pad_add_fusion.1.sc_ref, bf16[8,32,2048]{2,1,0:T(8,128)(2,1)} %bitcast.13.qa, bf16[8,32,2048]{2,1,0:T(8,128)(2,1)} %collective-permute-done.11.qb, bf16[8,32,2048]{2,1,0:T(8,128)(2,1)} %collective-permute-done.12.qc, ...), custom_call_target="tpu_custom_call" | custom-call | flops 28080001024 | bytes 25165824 | tf_op jit(solution)/shard_map/attention/pallas_call | solution.py:127
  203.4 7.0 collective-permute-done.16.gstat
  212.5 5.9 merge.6
  218.5 20.9 %attention.8 = (f32[8,64,2048]{2,1,0:T(8,128)}, f32[8,64,2048]{2,1,0:T(8,128)}, f32[8,32,128]{2,1,0:T(8,128)}) custom-call(s32[33]{0:T(128)} %pad_add_fusion.1.sc_ref, bf16[8,32,2048]{2,1,0:T(8,128)(2,1)} %bitcast.68, bf16[8,32,2048]{2,1,0:T(8,128)(2,1)} %collective-permute-done.17.qb, bf16[8,32,2048]{2,1,0:T(8,128)(2,1)} %collective-permute-done.18.qc, ...), custom_call_target="tpu_custom_call" | custom-call | flops 28080001024 | bytes 25165824 | tf_op jit(solution)/shard_map/attention/pallas_call | solution.py:127
  239.9 7.0 collective-permute-done.20.gstat
  247.6 6.0 merge.7
  255.2 12.5 %attention.9 = (f32[4,64,2048]{2,1,0:T(8,128)}, f32[4,64,2048]{2,1,0:T(8,128)}, f32[4,32,128]{2,1,0:T(8,128)}) custom-call(s32[33]{0:T(128)} %pad_add_fusion.1.sc_ref, bf16[4,32,2048]{2,1,0:T(8,128)(2,1)} %bitcast.60, bf16[4,32,2048]{2,1,0:T(8,128)(2,1)} %copy-done.14, bf16[4,32,2048]{2,1,0:T(8,128)(2,1)} %copy-done.16, bf16[4,32,2048]{2,1,0:T(8,128)(2,1)} %copy-done.17, ...), custom_call_target="tpu_custom_call" | custom-call | flops 14040000512 | bytes 12582912 | tf_op jit(solution)/shard_map/attention/pallas_call | solution.py:127
  273.8 6.0 merge.8
  285.3 87.9 %collective-permute-done.33 = bf16[128,4096]{1,0:T(8,128)(2,1)} collective-permute-done((bf16[128,4096]{1,0:T(8,128)(2,1)}, bf16[128,4096]{1,0:T(8,128)(2,1)}, u32[]{:S(2)}, u32[]{:S(2)}) %collective-permute-start.33) | collective-permute-done | bytes 1048608 | tf_op jit(solution)/shard_map/ppermute | solution.py:365
  375.5 19.0 %collective-permute-done.34 = bf16[128,4096]{1,0:T(8,128)(2,1)} collective-permute-done((bf16[128,4096]{1,0:T(8,128)(2,1)S(1)}, bf16[128,4096]{1,0:T(8,128)(2,1)}, u32[]{:S(2)}, u32[]{:S(2)}) %collective-permute-start.34) | collective-permute-done | bytes 1048608 | tf_op jit(solution)/shard_map/ppermute | solution.py:373
  396.8 6.2 constant_dynamic-update-slice_fusion.refs_7_.refs_3_
  407.1 112.0 %collective-permute-done.36.fstat = f32[1,32,128]{2,1,0:T(8,128)S(1)} collective-permute-done((f32[1,32,128]{2,1,0:T(8,128)S(1)}, f32[1,32,128]{2,1,0:T(8,128)S(1)}, u32[]{:S(2)}, u32[]{:S(2)}) %collective-permute-start.36) | collective-permute-done | bytes 16416 | tf_op jit(solution)/shard_map/ppermute | solution.py:389
  521.1 4.8 finish.5
  526.5 7.1 finish.6
  536.1 7.1 finish.7
  547.3 44.4 %collective-permute-done.39.refs_3_ = bf16[128,2048]{1,0:T(8,128)(2,1)S(1)} collective-permute-done((bf16[128,2048]{1,0:T(8,128)(2,1)S(1)}, bf16[128,2048]{1,0:T(8,128)(2,1)S(1)}, u32[]{:S(2)}, u32[]{:S(2)}) %collective-permute-start.39) | collective-permute-done | bytes 524320 | tf_op jit(solution)/shard_map/ppermute | solution.py:413
  594.7 35.1 %project.3.refs_7_ = bf16[1024,4096]{1,0:T(8,128)(2,1)} custom-call(s32[2]{0:T(128)} %pad_add_fusion.sc_ref, bf16[128,2048]{1,0:T(8,128)(2,1)} %bitcast.78, bf16[256,2048]{1,0:T(8,128)(2,1)} %bitcast.75, bf16[256,2048]{1,0:T(8,128)(2,1)} %bitcast.77, bf16[128,2048]{1,0:T(8,128)(2,1)} %copy-done.44, bf16[256,2048]{1,0:T(8,128)(2,1)} %collective-permute-done.40.refs_4_, ...), custom_call_target="tpu_custom_call" | custom-call | flops 25920000000 | bytes 33554432 | tf_op jit(solution)/shard_map/project/pallas_call | solution.py:286
  629.8 8.7 %collective-permute-done.29.far = f32[8,32,2048]{2,1,0:T(8,128)S(1)} collective-permute-done((f32[8,32,2048]{2,1,0:T(8,128)}, f32[8,32,2048]{2,1,0:T(8,128)S(1)}, u32[]{:S(2)}, u32[]{:S(2)}) %collective-permute-start.29) | collective-permute-done | bytes 2097184 | tf_op jit(solution)/shard_map/ppermute | solution.py:389
  639.8 7.0 finish.8
  649.4 20.1 %collective-permute-done.44.refs_1_ = bf16[256,2048]{1,0:T(8,128)(2,1)S(1)} collective-permute-done((bf16[256,2048]{1,0:T(8,128)(2,1)}, bf16[256,2048]{1,0:T(8,128)(2,1)S(1)}, u32[]{:S(2)}, u32[]{:S(2)}) %collective-permute-start.44) | collective-permute-done | bytes 1048608 | tf_op jit(solution)/shard_map/ppermute | solution.py:413
  670.5 20.6 %project.4.refs_7_ = bf16[1024,4096]{1,0:T(8,128)(2,1)} custom-call(s32[2]{0:T(128)} %pad_add_fusion.sc_ref, bf16[256,2048]{1,0:T(8,128)(2,1)} %bitcast.59, bf16[256,2048]{1,0:T(8,128)(2,1)} %copy-done.11, bf16[2048,4096]{1,0:T(8,128)(2,1)} %refs_2_.3, ...), custom_call_target="tpu_custom_call", output_to_operand_aliasing={{}: (8, {})} | custom-call | flops 10368000000 | bytes 33554432 | tf_op jit(solution)/shard_map/project/pallas_call | solution.py:286
  697.9 5.9 copy.17
  708.8 16.7 %project.5 = bf16[1024,4096]{1,0:T(8,128)(2,1)} custom-call(s32[2]{0:T(128)} %pad_add_fusion.sc_ref, bf16[128,2048]{1,0:T(8,128)(2,1)} %bitcast.67, bf16[128,2048]{1,0:T(8,128)(2,1)} %copy-done.18, bf16[2048,4096]{1,0:T(8,128)(2,1)} %refs_2_.3, bf16[1024,4096]{1,0:T(8,128)(2,1)} %constant_dynamic-update-slice_fusion.refs_7_.refs_3_, ...), custom_call_target="tpu_custom_call", output_to_operand_aliasing={{}: (8, {})} | custom-call | flops 5184000000 | bytes 33554432 | tf_op jit(solution)/shard_map/project/pallas_call | solution.py:286
  (215 shorter events, 99.5 us)
Async XLA Ops:
  26.0 71.1 %collective-permute-start.3 = (bf16[4,32,2048]{2,1,0:T(8,128)(2,1)}, bf16[4,32,2048]{2,1,0:T(8,128)(2,1)S(1)}, u32[]{:S(2)}, u32[]{:S(2)}) collective-permute-start(bf16[4,32,2048]{2,1,0:T(8,128)(2,1)} %bitcast.63), channel_id=1, source_target_pairs={{0,2},{2,0},{1,3},{3,1},{4,6},{6,4},{5,7},{7,5}} | collective-permute-start | bytes 1572872 | tf_op jit(solution)/shard_map/ppermute | solution.py:351
  27.5 104.6 %collective-permute-start.4 = (bf16[4,32,2048]{2,1,0:T(8,128)(2,1)}, bf16[4,32,2048]{2,1,0:T(8,128)(2,1)S(1)}, u32[]{:S(2)}, u32[]{:S(2)}) collective-permute-start(bf16[4,32,2048]{2,1,0:T(8,128)(2,1)} %bitcast.64), channel_id=1, source_target_pairs={{0,1},{1,0},{2,3},{3,2},{4,5},{5,4},{6,7},{7,6}} | collective-permute-start | bytes 1572872 | tf_op jit(solution)/shard_map/ppermute | solution.py:352
  95.1 26.3 %collective-permute-start.2 = (f32[1,1024]{1,0:T(1,128)S(1)}, f32[1,1024]{1,0:T(1,128)S(1)}, u32[]{:S(2)}, u32[]{:S(2)}) collective-permute-start(f32[1,1024]{1,0:T(1,128)S(1)} %bitcast.93), channel_id=1, source_target_pairs={{0,4},{4,0},{1,5},{5,1},{2,6},{6,2},{3,7},{7,3}} | collective-permute-start | bytes 12296 | tf_op jit(solution)/shard_map/ppermute | solution.py:341
  96.6 36.3 %collective-permute-start.7 = (bf16[8,32,2048]{2,1,0:T(8,128)(2,1)S(1)}, bf16[8,32,2048]{2,1,0:T(8,128)(2,1)}, u32[]{:S(2)}, u32[]{:S(2)}) collective-permute-start(bf16[8,32,2048]{2,1,0:T(8,128)(2,1)S(1)} %bitcast.72), channel_id=1, source_target_pairs={{0,2},{2,0},{1,3},{3,1},{4,6},{6,4},{5,7},{7,5}} | collective-permute-start | bytes 3145736 | tf_op jit(solution)/shard_map/ppermute | solution.py:351
  97.1 48.1 %collective-permute-start.8 = (bf16[8,32,2048]{2,1,0:T(8,128)(2,1)S(1)}, bf16[8,32,2048]{2,1,0:T(8,128)(2,1)}, u32[]{:S(2)}, u32[]{:S(2)}) collective-permute-start(bf16[8,32,2048]{2,1,0:T(8,128)(2,1)S(1)} %bitcast.73), channel_id=1, source_target_pairs={{0,1},{1,0},{2,3},{3,2},{4,5},{5,4},{6,7},{7,6}} | collective-permute-start | bytes 3145736 | tf_op jit(solution)/shard_map/ppermute | solution.py:352
  97.1 35.0 %collective-permute-start.5 = (bf16[4,32,2048]{2,1,0:T(8,128)(2,1)S(1)}, bf16[4,32,2048]{2,1,0:T(8,128)(2,1)S(1)}, u32[]{:S(2)}, u32[]{:S(2)}) collective-permute-start(bf16[4,32,2048]{2,1,0:T(8,128)(2,1)S(1)} %collective-permute-done.3.qb), channel_id=1, source_target_pairs={{0,1},{1,0},{2,3},{3,2},{4,5},{5,4},{6,7},{7,6}} | collective-permute-start | bytes 1572872 | tf_op jit(solution)/shard_map/ppermute | solution.py:353
  121.3 26.4 %collective-permute-start.11 = (bf16[8,32,2048]{2,1,0:T(8,128)(2,1)}, bf16[8,32,2048]{2,1,0:T(8,128)(2,1)}, u32[]{:S(2)}, u32[]{:S(2)}) collective-permute-start(bf16[8,32,2048]{2,1,0:T(8,128)(2,1)} %bitcast.13.qa), channel_id=1, source_target_pairs={{0,2},{2,0},{1,3},{3,1},{4,6},{6,4},{5,7},{7,5}} | collective-permute-start | bytes 3145736 | tf_op jit(solution)/shard_map/ppermute | solution.py:351
  132.1 49.9 %collective-permute-start.12 = (bf16[8,32,2048]{2,1,0:T(8,128)(2,1)}, bf16[8,32,2048]{2,1,0:T(8,128)(2,1)}, u32[]{:S(2)}, u32[]{:S(2)}) collective-permute-start(bf16[8,32,2048]{2,1,0:T(8,128)(2,1)} %bitcast.13.qa), channel_id=1, source_target_pairs={{0,1},{1,0},{2,3},{3,2},{4,5},{5,4},{6,7},{7,6}} | collective-permute-start | bytes 3145736 | tf_op jit(solution)/shard_map/ppermute | solution.py:352
  132.2 37.3 %collective-permute-start.17 = (bf16[8,32,2048]{2,1,0:T(8,128)(2,1)S(1)}, bf16[8,32,2048]{2,1,0:T(8,128)(2,1)}, u32[]{:S(2)}, u32[]{:S(2)}) collective-permute-start(bf16[8,32,2048]{2,1,0:T(8,128)(2,1)S(1)} %bitcast.69), channel_id=1, source_target_pairs={{0,2},{2,0},{1,3},{3,1},{4,6},{6,4},{5,7},{7,5}} | collective-permute-start | bytes 3145736 | tf_op jit(solution)/shard_map/ppermute | solution.py:351
  145.3 31.2 %collective-permute-start.6 = (f32[4,64,2048]{2,1,0:T(8,128)}, f32[4,64,2048]{2,1,0:T(8,128)S(1)}, u32[]{:S(2)}, u32[]{:S(2)}) collective-permute-start(f32[4,64,2048]{2,1,0:T(8,128)} %get-tuple-element.74), channel_id=1, source_target_pairs={{0,1},{1,0},{2,3},{3,2},{4,5},{5,4},{6,7},{7,6}} | collective-permute-start | bytes 6291464 | tf_op jit(solution)/shard_map/ppermute | solution.py:394
  147.7 34.3 %collective-permute-start.13 = (bf16[8,32,2048]{2,1,0:T(8,128)(2,1)}, bf16[8,32,2048]{2,1,0:T(8,128)(2,1)}, u32[]{:S(2)}, u32[]{:S(2)}) collective-permute-start(bf16[8,32,2048]{2,1,0:T(8,128)(2,1)} %collective-permute-done.11.qb), channel_id=1, source_target_pairs={{0,1},{1,0},{2,3},{3,2},{4,5},{5,4},{6,7},{7,6}} | collective-permute-start | bytes 3145736 | tf_op jit(solution)/shard_map/ppermute | solution.py:353
  168.5 43.5 %collective-permute-start.15 = (f32[8,64,2048]{2,1,0:T(8,128)}, f32[8,64,2048]{2,1,0:T(8,128)}, u32[]{:S(2)}, u32[]{:S(2)}) collective-permute-start(f32[8,64,2048]{2,1,0:T(8,128)} %get-tuple-element.85), channel_id=1, source_target_pairs={{0,1},{1,0},{2,3},{3,2},{4,5},{5,4},{6,7},{7,6}} | collective-permute-start | bytes 12582920 | tf_op jit(solution)/shard_map/ppermute | solution.py:394
  176.1 42.3 %collective-permute-start.18 = (bf16[8,32,2048]{2,1,0:T(8,128)(2,1)S(1)}, bf16[8,32,2048]{2,1,0:T(8,128)(2,1)}, u32[]{:S(2)}, u32[]{:S(2)}) collective-permute-start(bf16[8,32,2048]{2,1,0:T(8,128)(2,1)S(1)} %bitcast.70), channel_id=1, source_target_pairs={{0,1},{1,0},{2,3},{3,2},{4,5},{5,4},{6,7},{7,6}} | collective-permute-start | bytes 3145736 | tf_op jit(solution)/shard_map/ppermute | solution.py:352
  176.5 42.0 %collective-permute-start.19 = (bf16[8,32,2048]{2,1,0:T(8,128)(2,1)}, bf16[8,32,2048]{2,1,0:T(8,128)(2,1)}, u32[]{:S(2)}, u32[]{:S(2)}) collective-permute-start(bf16[8,32,2048]{2,1,0:T(8,128)(2,1)} %collective-permute-done.17.qb), channel_id=1, source_target_pairs={{0,1},{1,0},{2,3},{3,2},{4,5},{5,4},{6,7},{7,6}} | collective-permute-start | bytes 3145736 | tf_op jit(solution)/shard_map/ppermute | solution.py:353
  202.9 44.1 %collective-permute-start.14 = (f32[8,64,2048]{2,1,0:T(8,128)}, f32[8,64,2048]{2,1,0:T(8,128)}, u32[]{:S(2)}, u32[]{:S(2)}) collective-permute-start(f32[8,64,2048]{2,1,0:T(8,128)} %get-tuple-element.82), channel_id=1, source_target_pairs={{0,1},{1,0},{2,3},{3,2},{4,5},{5,4},{6,7},{7,6}} | collective-permute-start | bytes 12582920 | tf_op jit(solution)/shard_map/ppermute | solution.py:394
  210.5 29.4 %collective-permute-start.21 = (bf16[4,32,2048]{2,1,0:T(8,128)(2,1)S(1)}, bf16[4,32,2048]{2,1,0:T(8,128)(2,1)S(1)}, u32[]{:S(2)}, u32[]{:S(2)}) collective-permute-start(bf16[4,32,2048]{2,1,0:T(8,128)(2,1)S(1)} %bitcast.61), channel_id=1, source_target_pairs={{0,2},{2,0},{1,3},{3,1},{4,6},{6,4},{5,7},{7,5}} | collective-permute-start | bytes 1572872 | tf_op jit(solution)/shard_map/ppermute | solution.py:351
  212.0 184.8 %collective-permute-start.35 = (bf16[768,4096]{1,0:T(8,128)(2,1)}, bf16[768,4096]{1,0:T(8,128)(2,1)}, u32[]{:S(2)}, u32[]{:S(2)}) collective-permute-start(bf16[768,4096]{1,0:T(8,128)(2,1)} %constant_dynamic-slice_fusion.1), channel_id=1, source_target_pairs={{0,4},{4,0},{1,5},{5,1},{2,6},{6,2},{3,7},{7,3}} | collective-permute-start | bytes 18874376 | tf_op jit(solution)/shard_map/ppermute | solution.py:378
  239.3 34.4 %collective-permute-start.25 = (f32[8,64,2048]{2,1,0:T(8,128)}, f32[8,64,2048]{2,1,0:T(8,128)}, u32[]{:S(2)}, u32[]{:S(2)}) collective-permute-start(f32[8,64,2048]{2,1,0:T(8,128)} %get-tuple-element.97), channel_id=1, source_target_pairs={{0,1},{1,0},{2,3},{3,2},{4,5},{5,4},{6,7},{7,6}} | collective-permute-start | bytes 12582920 | tf_op jit(solution)/shard_map/ppermute | solution.py:394
  267.8 105.4 %collective-permute-start.33 = (bf16[128,4096]{1,0:T(8,128)(2,1)}, bf16[128,4096]{1,0:T(8,128)(2,1)}, u32[]{:S(2)}, u32[]{:S(2)}) collective-permute-start(bf16[128,4096]{1,0:T(8,128)(2,1)} %get-tuple-element.106), channel_id=1, source_target_pairs={{0,4},{4,0},{1,5},{5,1},{2,6},{6,2},{3,7},{7,3}} | collective-permute-start | bytes 3145736 | tf_op jit(solution)/shard_map/ppermute | solution.py:365
  272.2 122.3 %collective-permute-start.34 = (bf16[128,4096]{1,0:T(8,128)(2,1)S(1)}, bf16[128,4096]{1,0:T(8,128)(2,1)}, u32[]{:S(2)}, u32[]{:S(2)}) collective-permute-start(bf16[128,4096]{1,0:T(8,128)(2,1)S(1)} %copy-done.6), channel_id=1, source_target_pairs={{0,4},{4,0},{1,5},{5,1},{2,6},{6,2},{3,7},{7,3}} | collective-permute-start | bytes 3145736 | tf_op jit(solution)/shard_map/ppermute | solution.py:373
  403.0 190.7 %collective-permute-start.42 = (bf16[1024,4096]{1,0:T(8,128)(2,1)}, bf16[1024,4096]{1,0:T(8,128)(2,1)}, u32[]{:S(2)}, u32[]{:S(2)}) collective-permute-start(bf16[1024,4096]{1,0:T(8,128)(2,1)} %constant_dynamic-update-slice_fusion.refs_7_.refs_3_), channel_id=1, source_target_pairs={{0,1},{1,0},{2,3},{3,2},{4,5},{5,4},{6,7},{7,6}} | collective-permute-start | bytes 25165832 | tf_op jit(solution)/shard_map/ppermute | solution.py:400
  403.0 122.9 %collective-permute-start.31 = (f32[8,32,2048]{2,1,0:T(8,128)}, f32[8,32,2048]{2,1,0:T(8,128)}, u32[]{:S(2)}, u32[]{:S(2)}) collective-permute-start(f32[8,32,2048]{2,1,0:T(8,128)} %get-tuple-element.104), channel_id=1, source_target_pairs={{0,2},{2,0},{1,3},{3,1},{4,6},{6,4},{5,7},{7,5}} | collective-permute-start | bytes 6291464 | tf_op jit(solution)/shard_map/ppermute | solution.py:389
  403.5 130.6 %collective-permute-start.30 = (f32[8,32,2048]{2,1,0:T(8,128)}, f32[8,32,2048]{2,1,0:T(8,128)S(1)}, u32[]{:S(2)}, u32[]{:S(2)}) collective-permute-start(f32[8,32,2048]{2,1,0:T(8,128)} %get-tuple-element.103), channel_id=1, source_target_pairs={{0,2},{2,0},{1,3},{3,1},{4,6},{6,4},{5,7},{7,5}} | collective-permute-start | bytes 6291464 | tf_op jit(solution)/shard_map/ppermute | solution.py:389
  405.0 114.5 %collective-permute-start.32 = (f32[4,32,2048]{2,1,0:T(8,128)S(1)}, f32[4,32,2048]{2,1,0:T(8,128)S(1)}, u32[]{:S(2)}, u32[]{:S(2)}) collective-permute-start(f32[4,32,2048]{2,1,0:T(8,128)S(1)} %copy-done.41), channel_id=1, source_target_pairs={{0,2},{2,0},{1,3},{3,1},{4,6},{6,4},{5,7},{7,5}} | collective-permute-start | bytes 3145736 | tf_op jit(solution)/shard_map/ppermute | solution.py:389
  405.6 113.4 %collective-permute-start.36 = (f32[1,32,128]{2,1,0:T(8,128)S(1)}, f32[1,32,128]{2,1,0:T(8,128)S(1)}, u32[]{:S(2)}, u32[]{:S(2)}) collective-permute-start(f32[1,32,128]{2,1,0:T(8,128)S(1)} %copy-done.48), channel_id=1, source_target_pairs={{0,2},{2,0},{1,3},{3,1},{4,6},{6,4},{5,7},{7,5}} | collective-permute-start | bytes 49160 | tf_op jit(solution)/shard_map/ppermute | solution.py:389
  533.6 60.1 %collective-permute-start.40 = (bf16[256,2048]{1,0:T(8,128)(2,1)}, bf16[256,2048]{1,0:T(8,128)(2,1)}, u32[]{:S(2)}, u32[]{:S(2)}) collective-permute-start(bf16[256,2048]{1,0:T(8,128)(2,1)} %bitcast.74), channel_id=1, source_target_pairs={{0,4},{4,0},{1,5},{5,1},{2,6},{6,2},{3,7},{7,3}} | collective-permute-start | bytes 3145736 | tf_op jit(solution)/shard_map/ppermute | solution.py:413
  543.1 50.6 %collective-permute-start.41 = (bf16[256,2048]{1,0:T(8,128)(2,1)}, bf16[256,2048]{1,0:T(8,128)(2,1)S(1)}, u32[]{:S(2)}, u32[]{:S(2)}) collective-permute-start(bf16[256,2048]{1,0:T(8,128)(2,1)} %bitcast.76), channel_id=1, source_target_pairs={{0,4},{4,0},{1,5},{5,1},{2,6},{6,2},{3,7},{7,3}} | collective-permute-start | bytes 3145736 | tf_op jit(solution)/shard_map/ppermute | solution.py:413
  544.6 47.0 %collective-permute-start.39 = (bf16[128,2048]{1,0:T(8,128)(2,1)S(1)}, bf16[128,2048]{1,0:T(8,128)(2,1)S(1)}, u32[]{:S(2)}, u32[]{:S(2)}) collective-permute-start(bf16[128,2048]{1,0:T(8,128)(2,1)S(1)} %bitcast.79), channel_id=1, source_target_pairs={{0,4},{4,0},{1,5},{5,1},{2,6},{6,2},{3,7},{7,3}} | collective-permute-start | bytes 1572872 | tf_op jit(solution)/shard_map/ppermute | solution.py:413
  546.4 83.4 %collective-permute-start.43 = (f32[2,32,128]{2,1,0:T(8,128)S(1)}, f32[2,32,128]{2,1,0:T(8,128)S(1)}, u32[]{:S(2)}, u32[]{:S(2)}) collective-permute-start(f32[2,32,128]{2,1,0:T(8,128)S(1)} %copy-done.46), channel_id=1, source_target_pairs={{0,2},{2,0},{1,3},{3,1},{4,6},{6,4},{5,7},{7,5}} | collective-permute-start | bytes 98312 | tf_op jit(solution)/shard_map/ppermute | solution.py:389
  592.5 46.0 %collective-permute-start.29 = (f32[8,32,2048]{2,1,0:T(8,128)}, f32[8,32,2048]{2,1,0:T(8,128)S(1)}, u32[]{:S(2)}, u32[]{:S(2)}) collective-permute-start(f32[8,32,2048]{2,1,0:T(8,128)} %get-tuple-element.102), channel_id=1, source_target_pairs={{0,2},{2,0},{1,3},{3,1},{4,6},{6,4},{5,7},{7,5}} | collective-permute-start | bytes 6291464 | tf_op jit(solution)/shard_map/ppermute | solution.py:389
  647.3 43.7 %collective-permute-start.28 = (f32[4,32,2048]{2,1,0:T(8,128)S(1)}, f32[4,32,2048]{2,1,0:T(8,128)S(1)}, u32[]{:S(2)}, u32[]{:S(2)}) collective-permute-start(f32[4,32,2048]{2,1,0:T(8,128)S(1)} %copy-done.42), channel_id=1, source_target_pairs={{0,2},{2,0},{1,3},{3,1},{4,6},{6,4},{5,7},{7,5}} | collective-permute-start | bytes 3145736 | tf_op jit(solution)/shard_map/ppermute | solution.py:389
  648.9 42.2 %collective-permute-start.45 = (f32[1,32,128]{2,1,0:T(8,128)S(1)}, f32[1,32,128]{2,1,0:T(8,128)S(1)}, u32[]{:S(2)}, u32[]{:S(2)}) collective-permute-start(f32[1,32,128]{2,1,0:T(8,128)S(1)} %copy-done.49), channel_id=1, source_target_pairs={{0,2},{2,0},{1,3},{3,1},{4,6},{6,4},{5,7},{7,5}} | collective-permute-start | bytes 49160 | tf_op jit(solution)/shard_map/ppermute | solution.py:389
  (68 other events, 905.0 us)

commit v2 on v1

v2 whole, which is shorter than its diff:
```python
import functools

import jax
import jax.numpy as jnp
from jax import lax
from jax.experimental import pallas as pl
from jax.experimental.pallas import tpu as pltpu
from jax.sharding import PartitionSpec as P

NORM_EPS = 1e-6
ROPE_BASE = 500000.0
NEG = -1e30
FLOOR = -5e29
LOG2E = 1.4426950408889634
HD = 128
LAG = 1
ROPE_BLOCK = 256
P_BLOCK = 512
GROUPS = ((24, 8), (0, 8), (8, 8), (16, 4), (20, 4))
P_GROUPS = ((0, 1), (2, 3, 4))
PIECES = (256, 768)
VMEM_LIMIT = 60 * 1024 * 1024


def cost(micros, moved):
    return pl.CostEstimate(flops=int(micros * 9e8), bytes_accessed=moved, transcendentals=0)


def params():
    return pltpu.CompilerParams(dimension_semantics=("arbitrary",), vmem_limit_bytes=VMEM_LIMIT)


def dense_body(steps, x, w, out, sums, acc):
    j = pl.program_id(0)
    r = jnp.dot(x[...], w[...], preferred_element_type=jnp.float32)
    out[...] = r
    sq = r * r
    part = sq[:, :HD]
    for c in range(HD, sq.shape[1], HD):
        part = part + sq[:, c:c + HD]
    acc[...] = jnp.where(j == 0, part, acc[...] + part)

    @pl.when(j == steps - 1)
    def _():
        for t in range(0, acc.shape[0], HD):
            sums[:, t:t + HD] = jnp.sum(acc[t:t + HD, :].T, axis=0, keepdims=True)


def dense(x, w, row0, tokens):
    model, width = w.shape
    block = 512
    steps = width // block
    row_block = row0 // tokens
    return pl.pallas_call(
        functools.partial(dense_body, steps),
        grid=(steps,),
        in_specs=[pl.BlockSpec((tokens, model), lambda j: (row_block, 0), pipeline_mode=pl.Buffered(1)),
                  pl.BlockSpec((model, block), lambda j: (0, j))],
        out_specs=[pl.BlockSpec((tokens, block), lambda j: (0, j)), pl.BlockSpec((1, tokens), lambda j: (0, 0))],
        out_shape=[jax.ShapeDtypeStruct((tokens, width), jnp.float32), jax.ShapeDtypeStruct((1, tokens), jnp.float32)],
        scratch_shapes=[pltpu.VMEM((tokens, HD), jnp.float32)],
        compiler_params=params(),
        cost_estimate=cost(8 + tokens * 0.015, model * width * 2),
        name="dense",
    )(x, w)


def rope_body(total_width, n_heads, raw, own, peer, gain, cos, sin, out):
    inv = lax.rsqrt((own[...] + peer[...]) / total_width + NORM_EPS)
    inv = jnp.concatenate([jnp.broadcast_to(inv[:, i:i + HD], (HD, HD)).T for i in range(0, inv.shape[1], HD)], axis=0)
    cos_t = cos[...]
    sin_t = sin[...]
    for h in range(n_heads):
        cols = slice(h * HD, (h + 1) * HD)
        u = raw[:, cols] * inv * gain[:, cols]
        out[:, cols] = (u * cos_t + pltpu.roll(u, HD // 2, 1) * sin_t).astype(jnp.bfloat16)


def rope(raw, own, peer, gain, cos, sin, row0, total_width, tokens, raw_row0):
    width = raw.shape[1]
    block = ROPE_BLOCK if tokens % ROPE_BLOCK == 0 else 128
    base = row0 // block
    off = (row0 - raw_row0) // block
    return pl.pallas_call(
        functools.partial(rope_body, total_width, width // HD),
        grid=(tokens // block,),
        in_specs=[pl.BlockSpec((block, width), lambda i: (i + off, 0)),
                  pl.BlockSpec((1, block), lambda i: (0, i + off)),
                  pl.BlockSpec((1, block), lambda i: (0, i + off)),
                  pl.BlockSpec((1, width), lambda i: (0, 0)),
                  pl.BlockSpec((block, HD), lambda i: (i + base, 0)),
                  pl.BlockSpec((block, HD), lambda i: (i + base, 0))],
        out_specs=pl.BlockSpec((block, width), lambda i: (i, 0)),
        out_shape=jax.ShapeDtypeStruct((tokens, width), jnp.bfloat16),
        compiler_params=params(),
        cost_estimate=cost(tokens * 0.005, tokens * width * 6),
        name="rope",
    )(raw, own, peer, gain, cos, sin)


def attn_body(n_heads, row0, chunk, slots, pitch, sc_ref, qa, qb, qc, qd, ck, cv, kc, vc, keep, give, stat, ks, vs):
    b = pl.program_id(0)
    cp = sc_ref[0]
    valid_len = sc_ref[1 + row0 + b]
    tokens = 4 * chunk
    keys = slots + chunk
    for t in range(slots):
        ks[t * pitch:t * pitch + n_heads, :] = ck[0, t].astype(jnp.float32)
        vs[t * pitch:t * pitch + n_heads, :] = cv[0, t].astype(jnp.float32)
    row = lax.broadcasted_iota(jnp.int32, (keys, tokens), 0)
    col = lax.broadcasted_iota(jnp.int32, (keys, tokens), 1)
    part = col // chunk
    rel = jnp.where(part == 1, 2, jnp.where(part == 2, 1, part))
    query = jnp.bitwise_xor(rel, cp) * chunk + col % chunk
    chunk_key = cp * chunk + row - slots
    ok = jnp.where(row < slots, row + cp * slots - valid_len, chunk_key - query - 1) < 0
    scale = HD ** -0.5 * LOG2E
    contract_last = (((1,), (1,)), ((), ()))
    contract_first = (((0,), (0,)), ((), ()))

    def cols(h):
        return slice(h * HD, (h + 1) * HD)

    def scores(h):
        q = jnp.concatenate([qa[0, :, cols(h)], qb[0, :, cols(h)], qc[0, :, cols(h)], qd[0, :, cols(h)]], axis=0)
        k = jnp.concatenate([ks[pl.ds(h, slots, stride=pitch), :].astype(jnp.bfloat16), kc[0, :, cols(h)]], axis=0)
        return lax.dot_general(k, q, contract_last, preferred_element_type=jnp.float32)

    def soft(h, s):
        s = jnp.where(ok, s * scale, NEG)
        top = jnp.maximum(jnp.max(s, axis=0, keepdims=True), FLOOR)
        p = jnp.exp2(s - top)
        stat[0, h:h + 1, :] = top
        stat[0, n_heads + h:n_heads + h + 1, :] = jnp.sum(p, axis=0, keepdims=True)
        return p.astype(jnp.bfloat16)

    def values(h, p):
        v = jnp.concatenate([vs[pl.ds(h, slots, stride=pitch), :].astype(jnp.bfloat16), vc[0, :, cols(h)]], axis=0)
        num = lax.dot_general(p, v, contract_first, preferred_element_type=jnp.float32)
        keep[0, :, cols(h)] = num[:2 * chunk]
        give[0, :, cols(h)] = num[2 * chunk:]

    s_live, p_live = {}, {}
    for step in range(n_heads + 2 * LAG):
        if step < n_heads:
            s_live[step] = scores(step)
        h = step - LAG
        if 0 <= h < n_heads:
            p_live[h] = soft(h, s_live.pop(h))
        h = step - 2 * LAG
        if 0 <= h < n_heads:
            values(h, p_live.pop(h))


def attention(scalars, q_parts, cache_k, cache_v, k_new, k_row, v_new, v_row, row0):
    rows, chunk, width = q_parts[0].shape
    _, slots, n_heads, _ = cache_k.shape
    pitch = n_heads + 8
    q_spec = pl.BlockSpec((1, chunk, width), lambda b, s: (b, 0, 0))
    k_spec = pl.BlockSpec((1, chunk, width), lambda b, s: (b + k_row, 0, 0))
    v_spec = pl.BlockSpec((1, chunk, width), lambda b, s: (b + v_row, 0, 0))
    cache_spec = pl.BlockSpec((1, slots, n_heads, HD), lambda b, s: (b + row0, 0, 0, 0))
    out_spec = pl.BlockSpec((1, 2 * chunk, width), lambda b, s: (b, 0, 0))
    stat_spec = pl.BlockSpec((1, 2 * n_heads, 4 * chunk), lambda b, s: (b, 0, 0))
    out = jax.ShapeDtypeStruct((rows, 2 * chunk, width), jnp.float32)
    return pl.pallas_call(
        functools.partial(attn_body, n_heads, row0, chunk, slots, pitch),
        grid_spec=pltpu.PrefetchScalarGridSpec(
            num_scalar_prefetch=1, grid=(rows,),
            in_specs=[q_spec] * 4 + [cache_spec] * 2 + [k_spec, v_spec],
            out_specs=[out_spec] * 2 + [stat_spec],
            scratch_shapes=[pltpu.VMEM((slots * pitch, HD), jnp.float32)] * 2),
        out_shape=[out, out, jax.ShapeDtypeStruct((rows, 2 * n_heads, 4 * chunk), jnp.float32)],
        compiler_params=params(),
        cost_estimate=cost(rows * 3.9, rows * slots * width * 6),
        name="attention",
    )(scalars, *q_parts, cache_k, cache_v, k_new, v_new)


def pack_rows(stats, span, chunk, shift):
    lane = lax.broadcasted_iota(jnp.int32, stats[0].shape, 1) // chunk
    width = stats[0].shape[1]
    packed = stats[0] if shift == 0 else pltpu.roll(stats[0], (-shift * chunk) % width, 1)
    for i in range(1, span):
        step = ((i - shift) * chunk) % width
        packed = jnp.where(lane == i, pltpu.roll(stats[i], step, 1) if step else stats[i], packed)
    return packed


def merge_body(n_heads, chunk, span, keep, got, stat, gstat, out, ostat):
    mine = pack_rows([stat[i] for i in range(span)], span, chunk, 1)
    theirs = pack_rows([gstat[i] for i in range(span)], span, chunk, 3)
    t0, d0, t1, d1 = mine[:n_heads], mine[n_heads:], theirs[:n_heads], theirs[n_heads:]
    top = jnp.maximum(t0, t1)
    w0 = jnp.exp2(t0 - top)
    w1 = jnp.exp2(t1 - top)
    ostat[0] = jnp.concatenate([top, w0 * d0 + w1 * d1], axis=0)
    w = jnp.concatenate([w0, w1], axis=0).T
    tokens = span * chunk
    for h in range(n_heads):
        cols = slice(h * HD, (h + 1) * HD)
        val = keep[:, :, cols].reshape(tokens, HD) * w[:, h:h + 1]
        val = val + got[:, :, cols].reshape(tokens, HD) * w[:, n_heads + h:n_heads + h + 1]
        out[:, :, cols] = val.reshape(span, chunk, HD)


def merge(keep, got, stat, gstat, n_heads):
    rows, chunk2, width = keep.shape
    chunk = chunk2 // 2
    span = 4
    half = pl.BlockSpec((span, chunk, width), lambda i: (i, 1, 0))
    stats = pl.BlockSpec((span, 2 * n_heads, 4 * chunk), lambda i: (i, 0, 0))
    return pl.pallas_call(
        functools.partial(merge_body, n_heads, chunk, span),
        grid=(rows // span,),
        in_specs=[half, half, stats, stats],
        out_specs=[pl.BlockSpec((span, chunk, width), lambda i: (i, 0, 0)),
                   pl.BlockSpec((1, 2 * n_heads, 4 * chunk), lambda i: (i, 0, 0))],
        out_shape=[jax.ShapeDtypeStruct((rows, chunk, width), jnp.float32),
                   jax.ShapeDtypeStruct((rows // span, 2 * n_heads, 4 * chunk), jnp.float32)],
        compiler_params=params(),
        cost_estimate=cost(rows * 0.3, rows * chunk * width * 12),
        name="merge",
    )(keep, got, stat, gstat)


def finish_body(n_heads, chunk, span, keep, got, far, stat, gstat, fstat, out):
    sets = [pack_rows([stat[i] for i in range(span)], span, chunk, 0),
            pack_rows([gstat[i] for i in range(span)], span, chunk, 2), fstat[0]]
    pairs = [(x[:n_heads], x[n_heads:]) for x in sets]
    top = jnp.maximum(jnp.maximum(pairs[0][0], pairs[1][0]), pairs[2][0])
    ws = [jnp.exp2(t - top) for t, _ in pairs]
    den = ws[0] * pairs[0][1] + ws[1] * pairs[1][1] + ws[2] * pairs[2][1]
    inv = 1.0 / den
    w = jnp.concatenate([x * inv for x in ws], axis=0).T
    tokens = span * chunk
    for h in range(n_heads):
        cols = slice(h * HD, (h + 1) * HD)
        val = keep[:, :, cols].reshape(tokens, HD) * w[:, h:h + 1]
        val = val + got[:, :, cols].reshape(tokens, HD) * w[:, n_heads + h:n_heads + h + 1]
        val = val + far[:, :, cols].reshape(tokens, HD) * w[:, 2 * n_heads + h:2 * n_heads + h + 1]
        out[:, :, cols] = val.astype(jnp.bfloat16).reshape(span, chunk, HD)


def finish(keep, got, far, stat, gstat, fstat, n_heads):
    rows, chunk2, width = keep.shape
    chunk = chunk2 // 2
    span = 4
    half = pl.BlockSpec((span, chunk, width), lambda i: (i, 0, 0))
    stats = pl.BlockSpec((span, 2 * n_heads, 4 * chunk), lambda i: (i, 0, 0))
    return pl.pallas_call(
        functools.partial(finish_body, n_heads, chunk, span),
        grid=(rows // span,),
        in_specs=[half, half, half, stats, stats, pl.BlockSpec((1, 2 * n_heads, 4 * chunk), lambda i: (i, 0, 0))],
        out_specs=half,
        out_shape=jax.ShapeDtypeStruct((rows, chunk, width), jnp.bfloat16),
        compiler_params=params(),
        cost_estimate=cost(rows * 0.4, rows * chunk * width * 14),
        name="finish",
    )(keep, got, far, stat, gstat, fstat)


def chain(o, steps):
    total = None
    for at, part in steps:
        term = jnp.dot(o[:, pl.ds(at, part.shape[0])], part[...], preferred_element_type=jnp.float32)
        total = term if total is None else total + term
    return total


def own_steps(w_own, core, half):
    steps = []
    for side in (core, 1 - core):
        at = 0
        for size in PIECES:
            lo = pl.multiple_of(side * half + at, HD)
            steps.append((lo, w_own.at[pl.ds(lo, size)]))
            at += size
    return steps


def peer_steps(near, far, core, half):
    steps = []
    for side, parts in ((core, near), (1 - core, far)):
        at = 0
        for size, part in zip(PIECES, parts):
            steps.append((pl.multiple_of(side * half + at, HD), part))
            at += size
    return steps


def gather_rows(dst, pieces):
    at = 0
    for piece in pieces:
        size = piece.shape[0]
        dst[at:at + size, :] = piece[...]
        at += size


def own_body(n, half, sc_ref, *refs):
    o_in = refs[:n]
    w_own, out, o = refs[n:]
    core = sc_ref[0] % 2

    @pl.when(pl.program_id(0) == 0)
    def _():
        gather_rows(o, o_in)

    out[...] = chain(o, own_steps(w_own, core, half))


def project_body(n, half, steps, block, row_starts, sc_ref, *refs):
    p = len(PIECES)
    j = pl.program_id(0)
    core = sc_ref[0] % 2
    ro_in, refs = refs[:n], refs[n:]
    near, far, refs = refs[:p], refs[p:2 * p], refs[2 * p:]
    x_hbm, gain, ready = refs[:3]
    out_hbm, ro, x, acc, ssq, sem, out_sem = refs[-7:]
    sizes = [r.shape[0] for r in ro_in]
    spots = [sum(sizes[:k]) for k in range(n)]

    def copies(out):
        made = []
        for k in range(n):
            there = pl.ds(row_starts[k], sizes[k])
            here = x.at[pl.ds(spots[k], sizes[k])]
            if out:
                made.append(pltpu.make_async_copy(here, out_hbm.at[there], out_sem.at[k]))
            else:
                made.append(pltpu.make_async_copy(x_hbm.at[there], here, sem.at[k]))
        return made

    @pl.when(j == 0)
    def _():
        for c in copies(False):
            c.start()
        gather_rows(ro, ro_in)

    a = ready[...] + chain(ro, peer_steps(near, far, core, half))
    acc[j] = a
    sq = jnp.sum(a * a, axis=-1, keepdims=True)
    ssq[...] = jnp.where(j == 0, sq, ssq[...] + sq)

    @pl.when(j == steps - 1)
    def _():
        for c in copies(False):
            c.wait()
        inv = lax.rsqrt(ssq[...] / (steps * block) + NORM_EPS)
        for k in range(steps):
            cols = slice(k * block, (k + 1) * block)
            y = x[:, cols].astype(jnp.float32) + acc[k] * inv * gain[:, cols].astype(jnp.float32)
            x[:, cols] = y.astype(jnp.bfloat16)
        for c in copies(True):
            c.start()
        for c in copies(True):
            c.wait()


def rows_spec(pieces):
    return [pl.BlockSpec(o.shape, lambda j, s: (0, 0), pipeline_mode=pl.Buffered(1)) for o in pieces]


def project_own(scalars, o_list, w_own):
    tokens, width = sum(o.shape[0] for o in o_list), o_list[0].shape[1]
    model = w_own.shape[1]
    block = P_BLOCK
    return pl.pallas_call(
        functools.partial(own_body, len(o_list), width // 2),
        grid_spec=pltpu.PrefetchScalarGridSpec(
            num_scalar_prefetch=1, grid=(model // block,),
            in_specs=rows_spec(o_list) + [pl.BlockSpec((width, block), lambda j, s: (0, j))],
            out_specs=pl.BlockSpec((tokens, block), lambda j, s: (0, j)),
            scratch_shapes=[pltpu.VMEM((tokens, width), jnp.bfloat16)]),
        out_shape=jax.ShapeDtypeStruct((tokens, model), jnp.float32),
        compiler_params=params(),
        cost_estimate=cost(6 + tokens * 0.02, 2 * width * model),
        name="project_own",
    )(scalars, *o_list, w_own)


def project(scalars, ready, ro_list, near, far, x, gain, row_starts, so_far):
    n = len(ro_list)
    tokens, width = sum(o.shape[0] for o in ro_list), ro_list[0].shape[1]
    model = x.shape[1]
    block = P_BLOCK
    steps = model // block
    anywhere = pl.BlockSpec(memory_space=pl.ANY)
    w_specs = [pl.BlockSpec((p.shape[0], block), lambda j, s: (0, j)) for p in list(near) + list(far)]
    specs = rows_spec(ro_list) + w_specs + [anywhere, pl.BlockSpec((1, model), lambda j, s: (0, 0)),
                                            pl.BlockSpec((tokens, block), lambda j, s: (0, j))]
    args = [*ro_list, *near, *far, x, gain, ready]
    alias = {}
    if so_far is not None:
        alias = {1 + len(args): 0}
        specs.append(anywhere)
        args.append(so_far)
    return pl.pallas_call(
        functools.partial(project_body, n, width // 2, steps, block, row_starts),
        grid_spec=pltpu.PrefetchScalarGridSpec(
            num_scalar_prefetch=1, grid=(steps,), in_specs=specs, out_specs=anywhere,
            scratch_shapes=[pltpu.VMEM((tokens, width), jnp.bfloat16), pltpu.VMEM((tokens, model), jnp.bfloat16),
                            pltpu.VMEM((steps, tokens, block), jnp.float32), pltpu.VMEM((tokens, 1), jnp.float32),
                            pltpu.SemaphoreType.DMA((n,)), pltpu.SemaphoreType.DMA((n,))]),
        out_shape=jax.ShapeDtypeStruct(x.shape, jnp.bfloat16),
        input_output_aliases=alias,
        compiler_params=params(),
        cost_estimate=cost(10 + tokens * 0.02, 2 * width * model),
        name="project",
    )(scalars, *args)


def solution(mesh):
    tp_size = mesh.shape['tp']
    OTHER_CHIP = [(0, 2), (2, 0), (1, 3), (3, 1)]
    OTHER_CORE = [(0, 1), (1, 0), (2, 3), (3, 2)]
    OTHER_HALF = [(0, 1), (1, 0)]

    def local_step(x_chunk, w_query, w_key, w_value, w_out, q_gain, k_gain, post_gain, cache_k, cache_v, prefix_len):
        rows, chunk, model = x_chunk.shape
        n_heads = cache_k.shape[2]
        width = n_heads * HD
        total_width = width * tp_size
        cp = lax.axis_index('cp')
        tp = lax.axis_index('tp')
        core = cp % 2
        tokens = x_chunk.reshape(rows * chunk, model)
        scalars = jnp.concatenate([cp[None], prefix_len]).astype(jnp.int32)
        places = jnp.stack([cp, tp]).astype(jnp.int32)
        positions = prefix_len[:, None] + cp * chunk + jnp.arange(chunk, dtype=jnp.int32)[None, :]
        inv_freq = ROPE_BASE ** (-(jnp.arange(HD // 2, dtype=jnp.float32) * 2.0 / HD))
        angles = positions.astype(jnp.float32).reshape(-1, 1) * inv_freq[None, :]
        cos_h, sin_h = jnp.cos(angles), jnp.sin(angles)
        cos = jnp.concatenate([cos_h, cos_h], axis=-1)
        sin = jnp.concatenate([-sin_h, sin_h], axis=-1)
        qg = q_gain.astype(jnp.float32)[None]
        kg = k_gain.astype(jnp.float32)[None]
        pg = post_gain[None]

        def after(value, done):
            return lax.optimization_barrier((value, done))[0]

        def swap(own):
            return own, lax.ppermute(own, 'tp', OTHER_HALF)

        def w_slice(n, done):
            lo = core * (width // 2) + sum(PIECES[:n])
            return lax.dynamic_slice_in_dim(after(w_out, done), lo, PIECES[n], axis=0)

        def rotated(raw, sums, gain, row0, count, raw_row0, done):
            return rope(raw, *sums, after(gain, done), cos, sin, row0 * chunk, total_width, count * chunk, raw_row0 * chunk)

        def spread(q):
            q = q.reshape(-1, chunk, width)
            q_chip = lax.ppermute(q, 'cp', OTHER_CHIP)
            q_core = lax.ppermute(q, 'cp', OTHER_CORE)
            return q, q_chip, q_core, lax.ppermute(q_chip, 'cp', OTHER_CORE)

        f32 = jnp.float32
        split, first_rows = GROUPS[0]
        raw0, own0 = dense(tokens, w_query, split * chunk, first_rows * chunk)
        sums0 = swap(own0)
        ws0 = w_slice(0, own0)
        q0 = rotated(raw0, sums0, qg, split, first_rows, split, ws0)
        q_sets = [spread(q0)]
        raw1, own1 = dense(after(tokens, q0), w_query, 0, split * chunk)
        sums1 = swap(own1)
        ws1 = w_slice(1, own1)
        last = ws1
        for g in range(1, len(GROUPS)):
            last = rotated(raw1, sums1, qg, *GROUPS[g], 0, last)
            q_sets.append(spread(last))
        wn0 = lax.ppermute(after(ws0, own1), 'tp', OTHER_HALF)
        k_raw = jnp.dot(after(tokens, last), w_key, preferred_element_type=f32)
        k_sums = swap(jnp.sum(k_raw * k_raw, axis=-1)[None])
        v_flat = jnp.dot(after(tokens, k_sums[0]), w_value, preferred_element_type=f32).astype(jnp.bfloat16)
        k_first = rotated(k_raw, k_sums, kg, split, first_rows, 0, v_flat)
        wn1 = lax.ppermute(after(ws1, k_sums[0]), 'tp', OTHER_HALF)
        near = (wn0, wn1)
        far_w = tuple(lax.ppermute(w, 'cp', OTHER_CORE) for w in near)
        v_new = v_flat.reshape(rows, chunk, width)
        k_new = [(k_first.reshape(-1, chunk, width), 0)]

        parts, merged, o_mine, o_peer = {}, {}, {}, {}

        def attend(g, done):
            row0 = GROUPS[g][0]
            ks, _ = k_new[min(g, 1)]
            keep, give, stat = attention(after(scalars, done), q_sets[g], cache_k, cache_v,
                                      ks, row0 if g else 0, v_new, row0, row0)
            parts[g] = (keep, give, stat, lax.ppermute(give, 'cp', OTHER_CORE), lax.ppermute(stat, 'cp', OTHER_CORE))
            return stat

        def combine(g, done):
            keep, _, stat, got, gstat = parts[g]
            send, sstat = merge(keep, got, after(stat, done), gstat, n_heads)
            merged[g] = (lax.ppermute(send, 'cp', OTHER_CHIP), lax.ppermute(sstat, 'cp', OTHER_CHIP))
            return sstat

        def close(g, done):
            keep, _, stat, got, gstat = parts[g]
            o = finish(keep, got, merged[g][0], after(stat, done), gstat, merged[g][1], n_heads)
            o_mine[g] = o.reshape(-1, width)
            o_peer[g] = lax.ppermute(o_mine[g], 'tp', OTHER_HALF)
            return o

        def mix(n, ready, so_far=None):
            groups = P_GROUPS[n]
            return project(places, ready, [o_peer[g] for g in groups],
                          near, far_w, tokens, pg, tuple(GROUPS[g][0] * chunk for g in groups), so_far)

        def own_part(n, done):
            return project_own(after(places, done), [o_mine[g] for g in P_GROUPS[n]], w_out)

        shape = (rows, chunk, n_heads, HD)
        last = attend(0, k_first)
        k_rest = rotated(k_raw, k_sums, kg, 0, split, 0, last)
        k_new.append((k_rest.reshape(-1, chunk, width), 0))
        last = combine(0, k_rest)
        last = attend(1, last)
        last = attend(2, last)
        last = combine(1, last)
        last = close(0, last)
        last = attend(3, last)
        last = combine(2, last)
        last = attend(4, last)
        last = combine(3, last)
        last = combine(4, last)
        last = close(1, last)
        block_out = mix(0, own_part(0, last))
        last = close(2, block_out)
        last = close(3, last)
        chunk_k = jnp.concatenate([after(k_rest, last), k_first], axis=0).reshape(shape)
        chunk_v = after(v_flat, last).reshape(shape)
        last = close(4, (chunk_k, chunk_v))
        block_out = mix(1, own_part(1, last), block_out)
        return block_out.reshape(rows, chunk, model), chunk_k, chunk_v

    x_spec = P('dp', 'cp', None)
    head_spec = P('dp', 'cp', 'tp', None)
    in_specs = (x_spec, P(None, 'tp'), P(None, 'tp'), P(None, 'tp'), P('tp', None), P('tp'), P('tp'), P(None), head_spec, head_spec, P('dp'))
    out_specs = (x_spec, head_spec, head_spec)

    return jax.shard_map(local_step, mesh=mesh, in_specs=in_specs, out_specs=out_specs, check_vma=False)
```

time: 731 us -> 584 us (0.80)
  waiting for transfers between devices: 319 us -> 203 us
  matrix products: 81.5 us -> 48.2 us
  local copies, waits for them, and re-layouts: 46.2 us -> 23.6 us
  Pallas kernels: 240 us -> 261 us
    ppermute x32, waiting for transfers between devices: 316 us -> 104 us  [the longest x5 36.3 us: close(): o_peer[g] = lax.ppermute(o_mine[g], 'tp', OTHER_HALF)]
    ppermute x5, waiting for transfers between devices: 2.51 us -> 98.7 us  [spread(): q_chip = lax.ppermute(q, 'cp', OTHER_CHIP)]
    pallas_call x3 -> x6, Pallas kernels: 72.4 us -> 106 us  [the longest x2 43.3 us: project(): pl.pallas_call(functools.partial(project_body, n, width // 2, steps, bloc...]
    dot_general x2 -> x0, matrix products: 33.5 us -> none  [the longest x1 24.4 us: local_step(): raw1 = jnp.dot(after(tokens, q0), w_query, preferred_element_type=f32)]
    unnamed x110 -> x96, local copies, waits for them, and re-layouts: 28.7 us -> 13.5 us
    pallas_call x5, Pallas kernels: 30.8 us -> 23.2 us  [finish(): pl.pallas_call(functools.partial(finish_body, n_heads, chunk, span), grid...]
    pallas_call x6 -> x7, Pallas kernels: 23.4 us -> 25.4 us  [rope(): pl.pallas_call(functools.partial(rope_body, total_width, width // HD), gr...]
  transfers between devices with their start and end apart: 47 -> 47, of which waited for: 13 -> 15; matrix products, arithmetic and copies ran while one was open for 14% -> 13% of each run, Pallas kernels for 29% -> 35%
where the time goes in v2:
time: 584 us; the launch traced here: 575 us
  Pallas kernels  261 us (45%)
  waiting for transfers between devices  203 us (35%)
  matrix products  48.2 us (8%)
  starting transfers between devices  29.8 us (5%)
  local copies, waits for them, and re-layouts  23.6 us (4%)
  other arithmetic  7.39 us (1%)
    ppermute x5, waiting for transfers between devices, spread(): q_chip = lax.ppermute(q, 'cp', OTHER_CHIP)  98.7 us
    pallas_call x5, Pallas kernels, attention(): pl.pallas_call(functools.partial(attn_body, n_heads, row0, chunk, slots,...  86.5 us
    pallas_call x2, Pallas kernels, project(): pl.pallas_call(functools.partial(project_body, n, width // 2, steps, bloc...  43.3 us
    ppermute x5, waiting for transfers between devices, close(): o_peer[g] = lax.ppermute(o_mine[g], 'tp', OTHER_HALF)  36.3 us
    pallas_call x2, Pallas kernels, project_own(): pl.pallas_call(functools.partial(own_body, len(o_list), width // 2), grid...  33.5 us
    ppermute x1, waiting for transfers between devices, local_step(): wn0 = lax.ppermute(after(ws0, own1), 'tp', OTHER_HALF)  30.1 us
    pallas_call x2, Pallas kernels, dense(): pl.pallas_call(functools.partial(dense_body, steps), grid=(steps,), in_sp...  29.5 us
    pallas_call x7, Pallas kernels, rope(): pl.pallas_call(functools.partial(rope_body, total_width, width // HD), gr...  25.4 us
  transfers between devices with their start and end apart: 47, of which 15 were waited for; matrix products, arithmetic and copies ran while one was open for 13% of the time, Pallas kernels for 35%

profile of v2, /device:TPU:0, one launch (start us, length us, event | category | flops | bytes accessed | tf_op | source)
XLA Modules:
  0.0 574.6 jit_solution(5191485624371773582)
XLA Ops:
  0.6 10.4 %dense.2 = (f32[256,2048]{1,0:T(8,128)}, f32[1,256]{1,0:T(1,128)}) custom-call(bf16[1024,4096]{1,0:T(8,128)(2,1)} %bitcast.76, bf16[4096,2048]{1,0:T(8,128)(2,1)} %w.3), custom_call_target="tpu_custom_call" | custom-call | flops 10656000000 | bytes 16777216 | tf_op jit(solution)/shard_map/dense/pallas_call | solution.py:54
  28.1 19.1 %dense.3 = (f32[768,2048]{1,0:T(8,128)}, f32[1,768]{1,0:T(1,128)}) custom-call(bf16[1024,4096]{1,0:T(8,128)(2,1)} %bitcast.77, bf16[4096,2048]{1,0:T(8,128)(2,1)} %w.3), custom_call_target="tpu_custom_call" | custom-call | flops 17568000000 | bytes 16777216 | tf_op jit(solution)/shard_map/dense/pallas_call | solution.py:54
  47.7 6.2 %constant_dynamic-slice_fusion = bf16[768,4096]{1,0:T(8,128)(2,1)} fusion(bf16[2048,4096]{1,0:T(8,128)(2,1)} %refs_3_.1, s32[]{:T(128)S(6)} %select_n.15), kind=kLoop, calls=%fused_computation.12 | loop fusion | bytes 12582916 | tf_op jit(solution)/shard_map/dynamic_slice | solution.py:448
  66.3 24.2 %multiply_reduce_fusion = (f32[1024]{0:T(1024)S(1)}, f32[1024,2048]{1,0:T(8,128)}) fusion(bf16[1024,4096]{1,0:T(8,128)(2,1)} %bitcast.78, bf16[4096,2048]{1,0:T(8,128)(2,1)} %param.13), kind=kOutput, calls=%fused_computation | convolution fusion | flops 17184063488 | bytes 33558528 | tf_op jit(solution)/shard_map/dot_general | solution.py:474
  92.1 24.0 %convolution_convert_fusion = bf16[1024,2048]{1,0:T(8,128)(2,1)} fusion(bf16[1024,4096]{1,0:T(8,128)(2,1)} %bitcast.79, bf16[4096,2048]{1,0:T(8,128)(2,1)} %param.14), kind=kOutput, calls=%fused_computation.2 | convolution fusion | flops 17181966336 | bytes 29360128 | tf_op jit(solution)/shard_map/dot_general | solution.py:476
  121.3 20.9 %attention.5 = (f32[8,64,2048]{2,1,0:T(8,128)}, f32[8,64,2048]{2,1,0:T(8,128)}, f32[8,32,128]{2,1,0:T(8,128)}) custom-call(s32[33]{0:T(128)} %pad_add_fusion.1.sc_ref, bf16[8,32,2048]{2,1,0:T(8,128)(2,1)} %bitcast.84, bf16[8,32,2048]{2,1,0:T(8,128)(2,1)} %copy-done.34, bf16[8,32,2048]{2,1,0:T(8,128)(2,1)} %copy-done.33, bf16[8,32,2048]{2,1,0:T(8,128)(2,1)} %copy-done.37, ...), custom_call_target="tpu_custom_call" | custom-call | flops 28080001024 | bytes 25165824 | tf_op jit(solution)/shard_map/attention/pallas_call | solution.py:166
  144.5 24.1 %collective-permute-done.8.qb = bf16[8,32,2048]{2,1,0:T(8,128)(2,1)} collective-permute-done((bf16[8,32,2048]{2,1,0:T(8,128)(2,1)S(1)}, bf16[8,32,2048]{2,1,0:T(8,128)(2,1)}, u32[]{:S(2)}, u32[]{:S(2)}) %collective-permute-start.8) | collective-permute-done | bytes 1048608 | tf_op jit(solution)/shard_map/ppermute | solution.py:455
  169.1 6.9 %rope.13 = bf16[768,2048]{1,0:T(8,128)(2,1)} custom-call(f32[1024,2048]{1,0:T(8,128)} %get-tuple-element.131.raw, f32[1,1024]{1,0:T(1,128)} %bitcast.75, f32[1,1024]{1,0:T(1,128)} %copy-done.28, f32[1,2048]{1,0:T(1,128)} %bitcast.72, f32[1024,128]{1,0:T(8,128)} %get-tuple-element.132.cos, f32[1024,128]{1,0:T(8,128)} %get-tuple-element.133.sin), custom_call_target="tpu_custom_call" | custom-call | flops 3456000000 | bytes 9437184 | tf_op jit(solution)/shard_map/rope/pallas_call | solution.py:84
  176.1 14.2 %collective-permute-done.11.qb = bf16[8,32,2048]{2,1,0:T(8,128)(2,1)S(1)} collective-permute-done((bf16[8,32,2048]{2,1,0:T(8,128)(2,1)S(1)}, bf16[8,32,2048]{2,1,0:T(8,128)(2,1)S(1)}, u32[]{:S(2)}, u32[]{:S(2)}) %collective-permute-start.11) | collective-permute-done | bytes 1048608 | tf_op jit(solution)/shard_map/ppermute | solution.py:455
  191.0 4.3 merge.5
  195.4 20.6 %attention.6 = (f32[8,64,2048]{2,1,0:T(8,128)}, f32[8,64,2048]{2,1,0:T(8,128)}, f32[8,32,128]{2,1,0:T(8,128)}) custom-call(s32[33]{0:T(128)} %pad_add_fusion.1.sc_ref, bf16[8,32,2048]{2,1,0:T(8,128)(2,1)} %bitcast.55, bf16[8,32,2048]{2,1,0:T(8,128)(2,1)} %collective-permute-done.8.qb, bf16[8,32,2048]{2,1,0:T(8,128)(2,1)} %collective-permute-done.9.qc, ...), custom_call_target="tpu_custom_call" | custom-call | flops 28080001024 | bytes 25165824 | tf_op jit(solution)/shard_map/attention/pallas_call | solution.py:166
  216.4 20.7 %attention.7 = (f32[8,64,2048]{2,1,0:T(8,128)}, f32[8,64,2048]{2,1,0:T(8,128)}, f32[8,32,128]{2,1,0:T(8,128)}) custom-call(s32[33]{0:T(128)} %pad_add_fusion.1.sc_ref, bf16[8,32,2048]{2,1,0:T(8,128)(2,1)} %bitcast.52, bf16[8,32,2048]{2,1,0:T(8,128)(2,1)} %copy-done.31, bf16[8,32,2048]{2,1,0:T(8,128)(2,1)} %collective-permute-done.12.qc, ...), custom_call_target="tpu_custom_call" | custom-call | flops 28080001024 | bytes 25165824 | tf_op jit(solution)/shard_map/attention/pallas_call | solution.py:166
  239.5 57.2 %collective-permute-done.19.qb = bf16[4,32,2048]{2,1,0:T(8,128)(2,1)S(1)} collective-permute-done((bf16[4,32,2048]{2,1,0:T(8,128)(2,1)S(1)}, bf16[4,32,2048]{2,1,0:T(8,128)(2,1)S(1)}, u32[]{:S(2)}, u32[]{:S(2)}) %collective-permute-start.19) | collective-permute-done | bytes 524320 | tf_op jit(solution)/shard_map/ppermute | solution.py:455
  303.0 4.6 merge.6
  307.6 5.2 finish.5
  316.6 11.9 %collective-permute-done.36.refs_3_.refs_4_ = bf16[768,4096]{1,0:T(8,128)(2,1)} collective-permute-done((bf16[768,4096]{1,0:T(8,128)(2,1)}, bf16[768,4096]{1,0:T(8,128)(2,1)}, u32[]{:S(2)}, u32[]{:S(2)}) %collective-permute-start.36) | collective-permute-done | bytes 6291488 | tf_op jit(solution)/shard_map/ppermute | solution.py:478
  328.5 12.1 %attention.8 = (f32[4,64,2048]{2,1,0:T(8,128)}, f32[4,64,2048]{2,1,0:T(8,128)}, f32[4,32,128]{2,1,0:T(8,128)}) custom-call(s32[33]{0:T(128)} %pad_add_fusion.1.sc_ref, bf16[4,32,2048]{2,1,0:T(8,128)(2,1)} %bitcast.47, bf16[4,32,2048]{2,1,0:T(8,128)(2,1)} %copy-done.10, bf16[4,32,2048]{2,1,0:T(8,128)(2,1)} %collective-permute-done.20.qc, ...), custom_call_target="tpu_custom_call" | custom-call | flops 14040000512 | bytes 12582912 | tf_op jit(solution)/shard_map/attention/pallas_call | solution.py:166
  341.4 4.4 merge.7
  345.8 12.2 %attention.9 = (f32[4,64,2048]{2,1,0:T(8,128)}, f32[4,64,2048]{2,1,0:T(8,128)}, f32[4,32,128]{2,1,0:T(8,128)}) custom-call(s32[33]{0:T(128)} %pad_add_fusion.1.sc_ref, bf16[4,32,2048]{2,1,0:T(8,128)(2,1)} %bitcast.44, bf16[4,32,2048]{2,1,0:T(8,128)(2,1)} %collective-permute-done.26.qb, bf16[4,32,2048]{2,1,0:T(8,128)(2,1)} %collective-permute-done.27.qc, ...), custom_call_target="tpu_custom_call" | custom-call | flops 14040000512 | bytes 12582912 | tf_op jit(solution)/shard_map/attention/pallas_call | solution.py:166
  358.9 30.1 %collective-permute-done.35.refs_2_.refs_3_ = bf16[256,4096]{1,0:T(8,128)(2,1)} collective-permute-done((bf16[256,4096]{1,0:T(8,128)(2,1)}, bf16[256,4096]{1,0:T(8,128)(2,1)}, u32[]{:S(2)}, u32[]{:S(2)}) %collective-permute-start.35) | collective-permute-done | bytes 2097184 | tf_op jit(solution)/shard_map/ppermute | solution.py:473
  400.6 6.3 %collective-permute-done.33.fstat = f32[2,32,128]{2,1,0:T(8,128)S(1)} collective-permute-done((f32[2,32,128]{2,1,0:T(8,128)S(1)}, f32[2,32,128]{2,1,0:T(8,128)S(1)}, u32[]{:S(2)}, u32[]{:S(2)}) %collective-permute-start.33) | collective-permute-done | bytes 32800 | tf_op jit(solution)/shard_map/ppermute | solution.py:497
  407.6 5.1 finish.6
  414.2 16.7 %project_own.2.refs_8_ = f32[512,4096]{1,0:T(8,128)} custom-call(s32[2]{0:T(128)} %pad_add_fusion.sc_ref, bf16[256,2048]{1,0:T(8,128)(2,1)} %bitcast.50, bf16[256,2048]{1,0:T(8,128)(2,1)} %bitcast.61, bf16[2048,4096]{1,0:T(8,128)(2,1)} %refs_3_.1), custom_call_target="tpu_custom_call" | custom-call | flops 14616000512 | bytes 16777216 | tf_op jit(solution)/shard_map/project_own/pallas_call | solution.py:368
  434.4 10.1 %collective-permute-done.34.refs_1_ = bf16[256,2048]{1,0:T(8,128)(2,1)S(1)} collective-permute-done((bf16[256,2048]{1,0:T(8,128)(2,1)}, bf16[256,2048]{1,0:T(8,128)(2,1)S(1)}, u32[]{:S(2)}, u32[]{:S(2)}) %collective-permute-start.34) | collective-permute-done | bytes 1048608 | tf_op jit(solution)/shard_map/ppermute | solution.py:504
  446.0 21.6 %project.2.refs_10_ = bf16[1024,4096]{1,0:T(8,128)(2,1)} custom-call(s32[2]{0:T(128)} %pad_add_fusion.sc_ref, bf16[256,2048]{1,0:T(8,128)(2,1)} %copy-done.32, bf16[256,2048]{1,0:T(8,128)(2,1)} %copy-done.35, bf16[256,4096]{1,0:T(8,128)(2,1)} %collective-permute-done.35.refs_2_.refs_3_, bf16[768,4096]{1,0:T(8,128)(2,1)} %collective-permute-done.36.refs_3_.refs_4_, ...), custom_call_target="tpu_custom_call" | custom-call | flops 18215999488 | bytes 16777216 | tf_op jit(solution)/shard_map/project/pallas_call | solution.py:398
  468.7 5.1 finish.7
  473.8 5.5 collective-permute-done.41.far
  492.5 8.0 %collective-permute-done.45.fstat = f32[1,32,128]{2,1,0:T(8,128)S(1)} collective-permute-done((f32[1,32,128]{2,1,0:T(8,128)S(1)}, f32[1,32,128]{2,1,0:T(8,128)S(1)}, u32[]{:S(2)}, u32[]{:S(2)}) %collective-permute-start.45) | collective-permute-done | bytes 16416 | tf_op jit(solution)/shard_map/ppermute | solution.py:497
  508.5 16.7 %project_own.3.refs_9_ = f32[512,4096]{1,0:T(8,128)} custom-call(s32[2]{0:T(128)} %pad_add_fusion.sc_ref, bf16[256,2048]{1,0:T(8,128)(2,1)} %bitcast.58, bf16[128,2048]{1,0:T(8,128)(2,1)} %bitcast.62, bf16[128,2048]{1,0:T(8,128)(2,1)} %bitcast.65, bf16[2048,4096]{1,0:T(8,128)(2,1)} %refs_3_.1), custom_call_target="tpu_custom_call" | custom-call | flops 14616000512 | bytes 16777216 | tf_op jit(solution)/shard_map/project_own/pallas_call | solution.py:368
  525.2 6.0 %collective-permute-done.43.refs_1_ = bf16[128,2048]{1,0:T(8,128)(2,1)S(1)} collective-permute-done((bf16[128,2048]{1,0:T(8,128)(2,1)S(1)}, bf16[128,2048]{1,0:T(8,128)(2,1)S(1)}, u32[]{:S(2)}, u32[]{:S(2)}) %collective-permute-start.43) | collective-permute-done | bytes 524320 | tf_op jit(solution)/shard_map/ppermute | solution.py:504
  531.2 20.2 %collective-permute-done.40.refs_0_ = bf16[256,2048]{1,0:T(8,128)(2,1)S(1)} collective-permute-done((bf16[256,2048]{1,0:T(8,128)(2,1)S(1)}, bf16[256,2048]{1,0:T(8,128)(2,1)S(1)}, u32[]{:S(2)}, u32[]{:S(2)}) %collective-permute-start.40) | collective-permute-done | bytes 1048608 | tf_op jit(solution)/shard_map/ppermute | solution.py:504
  552.4 21.6 %project.3 = bf16[1024,4096]{1,0:T(8,128)(2,1)} custom-call(s32[2]{0:T(128)} %pad_add_fusion.sc_ref, bf16[256,2048]{1,0:T(8,128)(2,1)} %copy-done.36, bf16[128,2048]{1,0:T(8,128)(2,1)} %copy-done.39, bf16[128,2048]{1,0:T(8,128)(2,1)} %copy-done.38, bf16[256,4096]{1,0:T(8,128)(2,1)} %collective-permute-done.35.refs_2_.refs_3_, ...), custom_call_target="tpu_custom_call", output_to_operand_aliasing={{}: (11, {})} | custom-call | flops 18215999488 | bytes 16777216 | tf_op jit(solution)/shard_map/project/pallas_call | solution.py:398
  (202 shorter events, 96.9 us)
Async XLA Ops:
  26.6 93.3 %collective-permute-start.4 = (bf16[8,32,2048]{2,1,0:T(8,128)(2,1)}, bf16[8,32,2048]{2,1,0:T(8,128)(2,1)S(1)}, u32[]{:S(2)}, u32[]{:S(2)}) collective-permute-start(bf16[8,32,2048]{2,1,0:T(8,128)(2,1)} %bitcast.82), channel_id=1, source_target_pairs={{0,1},{1,0},{2,3},{3,2},{4,5},{5,4},{6,7},{7,6}} | collective-permute-start | bytes 3145736 | tf_op jit(solution)/shard_map/ppermute | solution.py:456
  26.6 65.4 %collective-permute-start.3 = (bf16[8,32,2048]{2,1,0:T(8,128)(2,1)}, bf16[8,32,2048]{2,1,0:T(8,128)(2,1)S(1)}, u32[]{:S(2)}, u32[]{:S(2)}) collective-permute-start(bf16[8,32,2048]{2,1,0:T(8,128)(2,1)} %bitcast.83), channel_id=1, source_target_pairs={{0,2},{2,0},{1,3},{3,1},{4,6},{6,4},{5,7},{7,5}} | collective-permute-start | bytes 3145736 | tf_op jit(solution)/shard_map/ppermute | solution.py:455
  92.1 27.9 %collective-permute-start.5 = (bf16[8,32,2048]{2,1,0:T(8,128)(2,1)S(1)}, bf16[8,32,2048]{2,1,0:T(8,128)(2,1)S(1)}, u32[]{:S(2)}, u32[]{:S(2)}) collective-permute-start(bf16[8,32,2048]{2,1,0:T(8,128)(2,1)S(1)} %collective-permute-done.3.qb), channel_id=1, source_target_pairs={{0,1},{1,0},{2,3},{3,2},{4,5},{5,4},{6,7},{7,6}} | collective-permute-start | bytes 3145736 | tf_op jit(solution)/shard_map/ppermute | solution.py:457
  142.1 48.7 %collective-permute-start.6 = (f32[8,64,2048]{2,1,0:T(8,128)}, f32[8,64,2048]{2,1,0:T(8,128)}, u32[]{:S(2)}, u32[]{:S(2)}) collective-permute-start(f32[8,64,2048]{2,1,0:T(8,128)} %get-tuple-element.82), channel_id=1, source_target_pairs={{0,1},{1,0},{2,3},{3,2},{4,5},{5,4},{6,7},{7,6}} | collective-permute-start | bytes 12582920 | tf_op jit(solution)/shard_map/ppermute | solution.py:491
  142.5 26.1 %collective-permute-start.8 = (bf16[8,32,2048]{2,1,0:T(8,128)(2,1)S(1)}, bf16[8,32,2048]{2,1,0:T(8,128)(2,1)}, u32[]{:S(2)}, u32[]{:S(2)}) collective-permute-start(bf16[8,32,2048]{2,1,0:T(8,128)(2,1)S(1)} %bitcast.56), channel_id=1, source_target_pairs={{0,2},{2,0},{1,3},{3,1},{4,6},{6,4},{5,7},{7,5}} | collective-permute-start | bytes 3145736 | tf_op jit(solution)/shard_map/ppermute | solution.py:455
  143.0 47.2 %collective-permute-start.11 = (bf16[8,32,2048]{2,1,0:T(8,128)(2,1)S(1)}, bf16[8,32,2048]{2,1,0:T(8,128)(2,1)S(1)}, u32[]{:S(2)}, u32[]{:S(2)}) collective-permute-start(bf16[8,32,2048]{2,1,0:T(8,128)(2,1)S(1)} %bitcast.53), channel_id=1, source_target_pairs={{0,2},{2,0},{1,3},{3,1},{4,6},{6,4},{5,7},{7,5}} | collective-permute-start | bytes 3145736 | tf_op jit(solution)/shard_map/ppermute | solution.py:455
  144.5 50.9 %collective-permute-start.9 = (bf16[8,32,2048]{2,1,0:T(8,128)(2,1)S(1)}, bf16[8,32,2048]{2,1,0:T(8,128)(2,1)}, u32[]{:S(2)}, u32[]{:S(2)}) collective-permute-start(bf16[8,32,2048]{2,1,0:T(8,128)(2,1)S(1)} %bitcast.57), channel_id=1, source_target_pairs={{0,1},{1,0},{2,3},{3,2},{4,5},{5,4},{6,7},{7,6}} | collective-permute-start | bytes 3145736 | tf_op jit(solution)/shard_map/ppermute | solution.py:456
  168.6 26.8 %collective-permute-start.10 = (bf16[8,32,2048]{2,1,0:T(8,128)(2,1)}, bf16[8,32,2048]{2,1,0:T(8,128)(2,1)}, u32[]{:S(2)}, u32[]{:S(2)}) collective-permute-start(bf16[8,32,2048]{2,1,0:T(8,128)(2,1)} %collective-permute-done.8.qb), channel_id=1, source_target_pairs={{0,1},{1,0},{2,3},{3,2},{4,5},{5,4},{6,7},{7,6}} | collective-permute-start | bytes 3145736 | tf_op jit(solution)/shard_map/ppermute | solution.py:457
  190.2 26.2 %collective-permute-start.12 = (bf16[8,32,2048]{2,1,0:T(8,128)(2,1)S(1)}, bf16[8,32,2048]{2,1,0:T(8,128)(2,1)}, u32[]{:S(2)}, u32[]{:S(2)}) collective-permute-start(bf16[8,32,2048]{2,1,0:T(8,128)(2,1)S(1)} %bitcast.54), channel_id=1, source_target_pairs={{0,1},{1,0},{2,3},{3,2},{4,5},{5,4},{6,7},{7,6}} | collective-permute-start | bytes 3145736 | tf_op jit(solution)/shard_map/ppermute | solution.py:456
  190.2 138.2 %collective-permute-start.36 = (bf16[768,4096]{1,0:T(8,128)(2,1)}, bf16[768,4096]{1,0:T(8,128)(2,1)}, u32[]{:S(2)}, u32[]{:S(2)}) collective-permute-start(bf16[768,4096]{1,0:T(8,128)(2,1)} %constant_dynamic-slice_fusion), channel_id=1, source_target_pairs={{0,4},{4,0},{1,5},{5,1},{2,6},{6,2},{3,7},{7,3}} | collective-permute-start | bytes 18874376 | tf_op jit(solution)/shard_map/ppermute | solution.py:478
  190.8 25.6 %collective-permute-start.13 = (bf16[8,32,2048]{2,1,0:T(8,128)(2,1)S(1)}, bf16[8,32,2048]{2,1,0:T(8,128)(2,1)}, u32[]{:S(2)}, u32[]{:S(2)}) collective-permute-start(bf16[8,32,2048]{2,1,0:T(8,128)(2,1)S(1)} %collective-permute-done.11.qb), channel_id=1, source_target_pairs={{0,1},{1,0},{2,3},{3,2},{4,5},{5,4},{6,7},{7,6}} | collective-permute-start | bytes 3145736 | tf_op jit(solution)/shard_map/ppermute | solution.py:457
  216.1 86.4 %collective-permute-start.16 = (f32[8,64,2048]{2,1,0:T(8,128)}, f32[8,64,2048]{2,1,0:T(8,128)}, u32[]{:S(2)}, u32[]{:S(2)}) collective-permute-start(f32[8,64,2048]{2,1,0:T(8,128)} %get-tuple-element.95), channel_id=1, source_target_pairs={{0,1},{1,0},{2,3},{3,2},{4,5},{5,4},{6,7},{7,6}} | collective-permute-start | bytes 12582920 | tf_op jit(solution)/shard_map/ppermute | solution.py:491
  237.2 104.0 %collective-permute-start.14 = (f32[8,64,2048]{2,1,0:T(8,128)}, f32[8,64,2048]{2,1,0:T(8,128)}, u32[]{:S(2)}, u32[]{:S(2)}) collective-permute-start(f32[8,64,2048]{2,1,0:T(8,128)} %get-tuple-element.91), channel_id=1, source_target_pairs={{0,1},{1,0},{2,3},{3,2},{4,5},{5,4},{6,7},{7,6}} | collective-permute-start | bytes 12582920 | tf_op jit(solution)/shard_map/ppermute | solution.py:491
  237.5 65.0 %collective-permute-start.15 = (f32[8,32,2048]{2,1,0:T(8,128)}, f32[8,32,2048]{2,1,0:T(8,128)S(1)}, u32[]{:S(2)}, u32[]{:S(2)}) collective-permute-start(f32[8,32,2048]{2,1,0:T(8,128)} %get-tuple-element.93), channel_id=1, source_target_pairs={{0,2},{2,0},{1,3},{3,1},{4,6},{6,4},{5,7},{7,5}} | collective-permute-start | bytes 6291464 | tf_op jit(solution)/shard_map/ppermute | solution.py:497
  237.9 58.7 %collective-permute-start.19 = (bf16[4,32,2048]{2,1,0:T(8,128)(2,1)S(1)}, bf16[4,32,2048]{2,1,0:T(8,128)(2,1)S(1)}, u32[]{:S(2)}, u32[]{:S(2)}) collective-permute-start(bf16[4,32,2048]{2,1,0:T(8,128)(2,1)S(1)} %bitcast.48), channel_id=1, source_target_pairs={{0,2},{2,0},{1,3},{3,1},{4,6},{6,4},{5,7},{7,5}} | collective-permute-start | bytes 1572872 | tf_op jit(solution)/shard_map/ppermute | solution.py:455
  316.0 29.8 %collective-permute-start.27 = (bf16[4,32,2048]{2,1,0:T(8,128)(2,1)S(1)}, bf16[4,32,2048]{2,1,0:T(8,128)(2,1)}, u32[]{:S(2)}, u32[]{:S(2)}) collective-permute-start(bf16[4,32,2048]{2,1,0:T(8,128)(2,1)S(1)} %bitcast.46), channel_id=1, source_target_pairs={{0,1},{1,0},{2,3},{3,2},{4,5},{5,4},{6,7},{7,6}} | collective-permute-start | bytes 1572872 | tf_op jit(solution)/shard_map/ppermute | solution.py:456
  316.0 29.8 %collective-permute-start.28 = (bf16[4,32,2048]{2,1,0:T(8,128)(2,1)}, bf16[4,32,2048]{2,1,0:T(8,128)(2,1)}, u32[]{:S(2)}, u32[]{:S(2)}) collective-permute-start(bf16[4,32,2048]{2,1,0:T(8,128)(2,1)} %collective-permute-done.26.qb), channel_id=1, source_target_pairs={{0,1},{1,0},{2,3},{3,2},{4,5},{5,4},{6,7},{7,6}} | collective-permute-start | bytes 1572872 | tf_op jit(solution)/shard_map/ppermute | solution.py:457
  328.5 104.5 %collective-permute-start.38 = (bf16[768,4096]{1,0:T(8,128)(2,1)}, bf16[768,4096]{1,0:T(8,128)(2,1)}, u32[]{:S(2)}, u32[]{:S(2)}) collective-permute-start(bf16[768,4096]{1,0:T(8,128)(2,1)} %collective-permute-done.36.refs_3_.refs_4_), channel_id=1, source_target_pairs={{0,1},{1,0},{2,3},{3,2},{4,5},{5,4},{6,7},{7,6}} | collective-permute-start | bytes 18874376 | tf_op jit(solution)/shard_map/ppermute | solution.py:480
  340.6 48.4 %collective-permute-start.35 = (bf16[256,4096]{1,0:T(8,128)(2,1)}, bf16[256,4096]{1,0:T(8,128)(2,1)}, u32[]{:S(2)}, u32[]{:S(2)}) collective-permute-start(bf16[256,4096]{1,0:T(8,128)(2,1)} %constant_dynamic-slice_fusion.1), channel_id=1, source_target_pairs={{0,4},{4,0},{1,5},{5,1},{2,6},{6,2},{3,7},{7,3}} | collective-permute-start | bytes 6291464 | tf_op jit(solution)/shard_map/ppermute | solution.py:473
  341.2 50.4 %collective-permute-start.30 = (f32[4,64,2048]{2,1,0:T(8,128)}, f32[4,64,2048]{2,1,0:T(8,128)S(1)}, u32[]{:S(2)}, u32[]{:S(2)}) collective-permute-start(f32[4,64,2048]{2,1,0:T(8,128)} %get-tuple-element.110), channel_id=1, source_target_pairs={{0,1},{1,0},{2,3},{3,2},{4,5},{5,4},{6,7},{7,6}} | collective-permute-start | bytes 6291464 | tf_op jit(solution)/shard_map/ppermute | solution.py:491
  358.0 38.9 %collective-permute-start.29 = (f32[4,64,2048]{2,1,0:T(8,128)}, f32[4,64,2048]{2,1,0:T(8,128)}, u32[]{:S(2)}, u32[]{:S(2)}) collective-permute-start(f32[4,64,2048]{2,1,0:T(8,128)} %get-tuple-element.107), channel_id=1, source_target_pairs={{0,1},{1,0},{2,3},{3,2},{4,5},{5,4},{6,7},{7,6}} | collective-permute-start | bytes 6291464 | tf_op jit(solution)/shard_map/ppermute | solution.py:491
  358.3 49.0 %collective-permute-start.25 = (f32[8,32,2048]{2,1,0:T(8,128)}, f32[8,32,2048]{2,1,0:T(8,128)}, u32[]{:S(2)}, u32[]{:S(2)}) collective-permute-start(f32[8,32,2048]{2,1,0:T(8,128)} %get-tuple-element.103), channel_id=1, source_target_pairs={{0,2},{2,0},{1,3},{3,1},{4,6},{6,4},{5,7},{7,5}} | collective-permute-start | bytes 6291464 | tf_op jit(solution)/shard_map/ppermute | solution.py:497
  390.2 40.7 %collective-permute-start.37 = (bf16[256,4096]{1,0:T(8,128)(2,1)}, bf16[256,4096]{1,0:T(8,128)(2,1)}, u32[]{:S(2)}, u32[]{:S(2)}) collective-permute-start(bf16[256,4096]{1,0:T(8,128)(2,1)} %collective-permute-done.35.refs_2_.refs_3_), channel_id=1, source_target_pairs={{0,1},{1,0},{2,3},{3,2},{4,5},{5,4},{6,7},{7,6}} | collective-permute-start | bytes 6291464 | tf_op jit(solution)/shard_map/ppermute | solution.py:480
  396.9 35.4 %collective-permute-start.24 = (bf16[256,2048]{1,0:T(8,128)(2,1)S(1)}, bf16[256,2048]{1,0:T(8,128)(2,1)S(1)}, u32[]{:S(2)}, u32[]{:S(2)}) collective-permute-start(bf16[256,2048]{1,0:T(8,128)(2,1)S(1)} %bitcast.51), channel_id=1, source_target_pairs={{0,4},{4,0},{1,5},{5,1},{2,6},{6,2},{3,7},{7,3}} | collective-permute-start | bytes 3145736 | tf_op jit(solution)/shard_map/ppermute | solution.py:504
  407.0 61.7 %collective-permute-start.23 = (f32[8,32,2048]{2,1,0:T(8,128)}, f32[8,32,2048]{2,1,0:T(8,128)}, u32[]{:S(2)}, u32[]{:S(2)}) collective-permute-start(f32[8,32,2048]{2,1,0:T(8,128)} %get-tuple-element.102), channel_id=1, source_target_pairs={{0,2},{2,0},{1,3},{3,1},{4,6},{6,4},{5,7},{7,5}} | collective-permute-start | bytes 6291464 | tf_op jit(solution)/shard_map/ppermute | solution.py:497
  412.7 31.9 %collective-permute-start.34 = (bf16[256,2048]{1,0:T(8,128)(2,1)}, bf16[256,2048]{1,0:T(8,128)(2,1)S(1)}, u32[]{:S(2)}, u32[]{:S(2)}) collective-permute-start(bf16[256,2048]{1,0:T(8,128)(2,1)} %bitcast.60), channel_id=1, source_target_pairs={{0,4},{4,0},{1,5},{5,1},{2,6},{6,2},{3,7},{7,3}} | collective-permute-start | bytes 3145736 | tf_op jit(solution)/shard_map/ppermute | solution.py:504
  430.9 36.8 %collective-permute-start.39 = (f32[2,32,128]{2,1,0:T(8,128)S(1)}, f32[2,32,128]{2,1,0:T(8,128)S(1)}, u32[]{:S(2)}, u32[]{:S(2)}) collective-permute-start(f32[2,32,128]{2,1,0:T(8,128)S(1)} %copy-done.41), channel_id=1, source_target_pairs={{0,2},{2,0},{1,3},{3,1},{4,6},{6,4},{5,7},{7,5}} | collective-permute-start | bytes 98312 | tf_op jit(solution)/shard_map/ppermute | solution.py:497
  432.4 41.4 %collective-permute-start.42 = (f32[1,32,128]{2,1,0:T(8,128)S(1)}, f32[1,32,128]{2,1,0:T(8,128)S(1)}, u32[]{:S(2)}, u32[]{:S(2)}) collective-permute-start(f32[1,32,128]{2,1,0:T(8,128)S(1)} %copy-done.44), channel_id=1, source_target_pairs={{0,2},{2,0},{1,3},{3,1},{4,6},{6,4},{5,7},{7,5}} | collective-permute-start | bytes 49160 | tf_op jit(solution)/shard_map/ppermute | solution.py:497
  433.0 46.3 %collective-permute-start.41 = (f32[4,32,2048]{2,1,0:T(8,128)}, f32[4,32,2048]{2,1,0:T(8,128)}, u32[]{:S(2)}, u32[]{:S(2)}) collective-permute-start(f32[4,32,2048]{2,1,0:T(8,128)} %get-tuple-element.120), channel_id=1, source_target_pairs={{0,2},{2,0},{1,3},{3,1},{4,6},{6,4},{5,7},{7,5}} | collective-permute-start | bytes 3145736 | tf_op jit(solution)/shard_map/ppermute | solution.py:497
  444.5 56.0 %collective-permute-start.44 = (f32[4,32,2048]{2,1,0:T(8,128)}, f32[4,32,2048]{2,1,0:T(8,128)}, u32[]{:S(2)}, u32[]{:S(2)}) collective-permute-start(f32[4,32,2048]{2,1,0:T(8,128)} %get-tuple-element.122), channel_id=1, source_target_pairs={{0,2},{2,0},{1,3},{3,1},{4,6},{6,4},{5,7},{7,5}} | collective-permute-start | bytes 3145736 | tf_op jit(solution)/shard_map/ppermute | solution.py:497
  467.7 32.8 %collective-permute-start.45 = (f32[1,32,128]{2,1,0:T(8,128)S(1)}, f32[1,32,128]{2,1,0:T(8,128)S(1)}, u32[]{:S(2)}, u32[]{:S(2)}) collective-permute-start(f32[1,32,128]{2,1,0:T(8,128)S(1)} %copy-done.43), channel_id=1, source_target_pairs={{0,2},{2,0},{1,3},{3,1},{4,6},{6,4},{5,7},{7,5}} | collective-permute-start | bytes 49160 | tf_op jit(solution)/shard_map/ppermute | solution.py:497
  507.0 44.4 %collective-permute-start.40 = (bf16[256,2048]{1,0:T(8,128)(2,1)S(1)}, bf16[256,2048]{1,0:T(8,128)(2,1)S(1)}, u32[]{:S(2)}, u32[]{:S(2)}) collective-permute-start(bf16[256,2048]{1,0:T(8,128)(2,1)S(1)} %bitcast.59), channel_id=1, source_target_pairs={{0,4},{4,0},{1,5},{5,1},{2,6},{6,2},{3,7},{7,3}} | collective-permute-start | bytes 3145736 | tf_op jit(solution)/shard_map/ppermute | solution.py:504
  (62 other events, 1046.7 us)

commit v3 on v2

--- a/solution.py
+++ b/solution.py
@@ -13,11 +13,13 @@
 FLOOR = -5e29
 LOG2E = 1.4426950408889634
 HD = 128
-LAG = 1
+LAG = 2
 ROPE_BLOCK = 256
-P_BLOCK = 512
-GROUPS = ((24, 8), (0, 8), (8, 8), (16, 4), (20, 4))
-P_GROUPS = ((0, 1), (2, 3, 4))
+P_BLOCK = 1024
+GROUPS = ((24, 8), (0, 8), (8, 8), (16, 8))
+ATTEND = ((0, 0, 4), (0, 4, 4), (1, 0, 8), (2, 0, 8), (3, 0, 8))
+MERGE = ((0, 0, 4), (1, 0, 4), (2, 0, 8), (3, 0, 8), (4, 0, 4), (4, 4, 4))
+P_GROUPS = ((0, 1, 2), (3, 4, 5))
 PIECES = (256, 768)
 VMEM_LIMIT = 60 * 1024 * 1024
 
@@ -33,7 +35,7 @@
 def dense_body(steps, x, w, out, sums, acc):
     j = pl.program_id(0)
     r = jnp.dot(x[...], w[...], preferred_element_type=jnp.float32)
-    out[...] = r
+    out[...] = r.astype(out.dtype)
     sq = r * r
     part = sq[:, :HD]
     for c in range(HD, sq.shape[1], HD):
@@ -46,7 +48,7 @@
             sums[:, t:t + HD] = jnp.sum(acc[t:t + HD, :].T, axis=0, keepdims=True)
 
 
-def dense(x, w, row0, tokens):
+def dense(x, w, row0, tokens, dtype=jnp.float32):
     model, width = w.shape
     block = 512
     steps = width // block
@@ -57,7 +59,7 @@
         in_specs=[pl.BlockSpec((tokens, model), lambda j: (row_block, 0), pipeline_mode=pl.Buffered(1)),
                   pl.BlockSpec((model, block), lambda j: (0, j))],
         out_specs=[pl.BlockSpec((tokens, block), lambda j: (0, j)), pl.BlockSpec((1, tokens), lambda j: (0, 0))],
-        out_shape=[jax.ShapeDtypeStruct((tokens, width), jnp.float32), jax.ShapeDtypeStruct((1, tokens), jnp.float32)],
+        out_shape=[jax.ShapeDtypeStruct((tokens, width), dtype), jax.ShapeDtypeStruct((1, tokens), jnp.float32)],
         scratch_shapes=[pltpu.VMEM((tokens, HD), jnp.float32)],
         compiler_params=params(),
         cost_estimate=cost(8 + tokens * 0.015, model * width * 2),
@@ -152,11 +154,11 @@
             values(h, p_live.pop(h))
 
 
-def attention(scalars, q_parts, cache_k, cache_v, k_new, k_row, v_new, v_row, row0):
-    rows, chunk, width = q_parts[0].shape
+def attention(scalars, q_parts, q_row, rows, cache_k, cache_v, k_new, k_row, v_new, v_row, row0):
+    _, chunk, width = q_parts[0].shape
     _, slots, n_heads, _ = cache_k.shape
     pitch = n_heads + 8
-    q_spec = pl.BlockSpec((1, chunk, width), lambda b, s: (b, 0, 0))
+    q_spec = pl.BlockSpec((1, chunk, width), lambda b, s: (b + q_row, 0, 0))
     k_spec = pl.BlockSpec((1, chunk, width), lambda b, s: (b + k_row, 0, 0))
     v_spec = pl.BlockSpec((1, chunk, width), lambda b, s: (b + v_row, 0, 0))
     cache_spec = pl.BlockSpec((1, slots, n_heads, HD), lambda b, s: (b + row0, 0, 0, 0))
@@ -204,12 +206,13 @@
         out[:, :, cols] = val.reshape(span, chunk, HD)
 
 
-def merge(keep, got, stat, gstat, n_heads):
-    rows, chunk2, width = keep.shape
+def merge(keep, got, stat, gstat, n_heads, row, rows):
+    _, chunk2, width = keep.shape
     chunk = chunk2 // 2
     span = 4
-    half = pl.BlockSpec((span, chunk, width), lambda i: (i, 1, 0))
-    stats = pl.BlockSpec((span, 2 * n_heads, 4 * chunk), lambda i: (i, 0, 0))
+    lead = row // span
+    half = pl.BlockSpec((span, chunk, width), lambda i: (i + lead, 1, 0))
+    stats = pl.BlockSpec((span, 2 * n_heads, 4 * chunk), lambda i: (i + lead, 0, 0))
     return pl.pallas_call(
         functools.partial(merge_body, n_heads, chunk, span),
         grid=(rows // span,),
@@ -242,17 +245,19 @@
         out[:, :, cols] = val.astype(jnp.bfloat16).reshape(span, chunk, HD)
 
 
-def finish(keep, got, far, stat, gstat, fstat, n_heads):
-    rows, chunk2, width = keep.shape
+def finish(keep, got, far, stat, gstat, fstat, n_heads, row, rows):
+    _, chunk2, width = keep.shape
     chunk = chunk2 // 2
     span = 4
-    half = pl.BlockSpec((span, chunk, width), lambda i: (i, 0, 0))
-    stats = pl.BlockSpec((span, 2 * n_heads, 4 * chunk), lambda i: (i, 0, 0))
+    lead = row // span
+    half = pl.BlockSpec((span, chunk, width), lambda i: (i + lead, 0, 0))
+    plain = pl.BlockSpec((span, chunk, width), lambda i: (i, 0, 0))
+    stats = pl.BlockSpec((span, 2 * n_heads, 4 * chunk), lambda i: (i + lead, 0, 0))
     return pl.pallas_call(
         functools.partial(finish_body, n_heads, chunk, span),
         grid=(rows // span,),
-        in_specs=[half, half, half, stats, stats, pl.BlockSpec((1, 2 * n_heads, 4 * chunk), lambda i: (i, 0, 0))],
-        out_specs=half,
+        in_specs=[half, half, plain, stats, stats, pl.BlockSpec((1, 2 * n_heads, 4 * chunk), lambda i: (i, 0, 0))],
+        out_specs=plain,
         out_shape=jax.ShapeDtypeStruct((rows, chunk, width), jnp.bfloat16),
         compiler_params=params(),
         cost_estimate=cost(rows * 0.4, rows * chunk * width * 14),
@@ -473,66 +478,80 @@
         wn0 = lax.ppermute(after(ws0, own1), 'tp', OTHER_HALF)
         k_raw = jnp.dot(after(tokens, last), w_key, preferred_element_type=f32)
         k_sums = swap(jnp.sum(k_raw * k_raw, axis=-1)[None])
-        v_flat = jnp.dot(after(tokens, k_sums[0]), w_value, preferred_element_type=f32).astype(jnp.bfloat16)
-        k_first = rotated(k_raw, k_sums, kg, split, first_rows, 0, v_flat)
+        bf16 = jnp.bfloat16
+        v_first = dense(after(tokens, k_sums[0]), w_value, split * chunk, first_rows * chunk, bf16)[0]
+        k_first = rotated(k_raw, k_sums, kg, split, first_rows, 0, v_first)
         wn1 = lax.ppermute(after(ws1, k_sums[0]), 'tp', OTHER_HALF)
         near = (wn0, wn1)
         far_w = tuple(lax.ppermute(w, 'cp', OTHER_CORE) for w in near)
-        v_new = v_flat.reshape(rows, chunk, width)
-        k_new = [(k_first.reshape(-1, chunk, width), 0)]
+        v_new = [v_first.reshape(-1, chunk, width)]
+        k_new = [k_first.reshape(-1, chunk, width)]
 
         parts, merged, o_mine, o_peer = {}, {}, {}, {}
 
-        def attend(g, done):
-            row0 = GROUPS[g][0]
-            ks, _ = k_new[min(g, 1)]
-            keep, give, stat = attention(after(scalars, done), q_sets[g], cache_k, cache_v,
-                                      ks, row0 if g else 0, v_new, row0, row0)
-            parts[g] = (keep, give, stat, lax.ppermute(give, 'cp', OTHER_CORE), lax.ppermute(stat, 'cp', OTHER_CORE))
+        def attend(u, done):
+            g, off, count = ATTEND[u]
+            row0 = GROUPS[g][0] + off
+            side, kv_row = (1, row0) if g else (0, off)
+            keep, give, stat = attention(after(scalars, done), q_sets[g], off, count, cache_k, cache_v,
+                                      k_new[side], kv_row, v_new[side], kv_row, row0)
+            parts[u] = (keep, give, stat, lax.ppermute(give, 'cp', OTHER_CORE), lax.ppermute(stat, 'cp', OTHER_CORE))
             return stat
 
-        def combine(g, done):
-            keep, _, stat, got, gstat = parts[g]
-            send, sstat = merge(keep, got, after(stat, done), gstat, n_heads)
-            merged[g] = (lax.ppermute(send, 'cp', OTHER_CHIP), lax.ppermute(sstat, 'cp', OTHER_CHIP))
+        def combine(m, done):
+            u, off, count = MERGE[m]
+            keep, _, stat, got, gstat = parts[u]
+            send, sstat = merge(keep, got, after(stat, done), gstat, n_heads, off, count)
+            merged[m] = (lax.ppermute(send, 'cp', OTHER_CHIP), lax.ppermute(sstat, 'cp', OTHER_CHIP))
             return sstat
 
-        def close(g, done):
-            keep, _, stat, got, gstat = parts[g]
-            o = finish(keep, got, merged[g][0], after(stat, done), gstat, merged[g][1], n_heads)
-            o_mine[g] = o.reshape(-1, width)
-            o_peer[g] = lax.ppermute(o_mine[g], 'tp', OTHER_HALF)
+        def close(m, done):
+            u, off, count = MERGE[m]
+            keep, _, stat, got, gstat = parts[u]
+            o = finish(keep, got, merged[m][0], after(stat, done), gstat, merged[m][1], n_heads, off, count)
+            o_mine[m] = o.reshape(-1, width)
+            o_peer[m] = lax.ppermute(o_mine[m], 'tp', OTHER_HALF)
             return o
+
+        def row_of(m):
+            u, off, _ = MERGE[m]
+            g, a_off, _ = ATTEND[u]
+            return (GROUPS[g][0] + a_off + off) * chunk
 
         def mix(n, ready, so_far=None):
             groups = P_GROUPS[n]
             return project(places, ready, [o_peer[g] for g in groups],
-                          near, far_w, tokens, pg, tuple(GROUPS[g][0] * chunk for g in groups), so_far)
+                          near, far_w, tokens, pg, tuple(row_of(m) for m in groups), so_far)
 
         def own_part(n, done):
             return project_own(after(places, done), [o_mine[g] for g in P_GROUPS[n]], w_out)
 
         shape = (rows, chunk, n_heads, HD)
         last = attend(0, k_first)
+        last = attend(1, last)
+        last = combine(0, last)
+        v_rest = dense(after(tokens, last), w_value, 0, split * chunk, bf16)[0]
+        v_new.append(v_rest.reshape(-1, chunk, width))
+        last = combine(1, v_rest)
         k_rest = rotated(k_raw, k_sums, kg, 0, split, 0, last)
-        k_new.append((k_rest.reshape(-1, chunk, width), 0))
-        last = combine(0, k_rest)
-        last = attend(1, last)
-        last = attend(2, last)
-        last = combine(1, last)
+        k_new.append(k_rest.reshape(-1, chunk, width))
+        last = attend(2, k_rest)
+        chunk_k = jnp.concatenate([after(k_rest, last), k_first], axis=0).reshape(shape)
+        last = combine(2, chunk_k)
         last = close(0, last)
         last = attend(3, last)
-        last = combine(2, last)
+        chunk_v = jnp.concatenate([after(v_rest, last), v_first], axis=0).reshape(shape)
+        last = close(1, chunk_v)
+        last = combine(3, last)
         last = attend(4, last)
-        last = combine(3, last)
+        last = close(2, last)
         last = combine(4, last)
-        last = close(1, last)
-        block_out = mix(0, own_part(0, last))
-        last = close(2, block_out)
-        last = close(3, last)
-        chunk_k = jnp.concatenate([after(k_rest, last), k_first], axis=0).reshape(shape)
-        chunk_v = after(v_flat, last).reshape(shape)
-        last = close(4, (chunk_k, chunk_v))
+        last = combine(5, last)
+        ready = own_part(0, last)
+        last = close(3, ready)
+        block_out = mix(0, after(ready, last))
+        last = close(4, block_out)
+        last = close(5, last)
         block_out = mix(1, own_part(1, last), block_out)
         return block_out.reshape(rows, chunk, model), chunk_k, chunk_v
 

time: 584 us -> 637 us (1.091)
  waiting for transfers between devices: 203 us -> 248 us
  matrix products: 48.2 us -> 24.2 us
  Pallas kernels: 261 us -> 283 us
    ppermute x5 -> x6, waiting for transfers between devices: 17.7 us -> 76.8 us  [combine(): lax.ppermute(sstat, 'cp', OTHER_CHIP)]
    ppermute x5 -> x4, waiting for transfers between devices: 98.7 us -> 60.6 us  [spread(): q_chip = lax.ppermute(q, 'cp', OTHER_CHIP)]
    ppermute x1, waiting for transfers between devices: 11.9 us -> 42.8 us  [local_step(): wn1 = lax.ppermute(after(ws1, k_sums[0]), 'tp', OTHER_HALF)]
    pallas_call x2 -> x4, Pallas kernels: 29.5 us -> 58.8 us  [dense(): pl.pallas_call(functools.partial(dense_body, steps), grid=(steps,), in_sp...]
    dot_general x1 -> x0, matrix products: 24 us -> none  [local_step(): jnp.dot(after(tokens, k_sums[0]), w_value, preferred_element_type=f32)]
    ppermute x5 -> x6, waiting for transfers between devices: 36.3 us -> 13.1 us  [close(): o_peer[m] = lax.ppermute(o_mine[m], 'tp', OTHER_HALF)]
    ppermute x1, waiting for transfers between devices: 30.1 us -> 45.4 us  [local_step(): wn0 = lax.ppermute(after(ws0, own1), 'tp', OTHER_HALF)]
    pallas_call x5 -> x6, Pallas kernels: 23.2 us -> 26.2 us  [finish(): pl.pallas_call(functools.partial(finish_body, n_heads, chunk, span), grid...]
  transfers between devices with their start and end apart: 47 -> 47, of which waited for: 15 -> 11; matrix products, arithmetic and copies ran while one was open for 13% -> 8% of each run, Pallas kernels for 35% -> 32%
where the time goes in v3:
time: 637 us; the launch traced here: 627 us
  Pallas kernels  283 us (44%)
  waiting for transfers between devices  248 us (39%)
  starting transfers between devices  31.3 us (5%)
  local copies, waits for them, and re-layouts  28.1 us (4%)
  matrix products  24.2 us (4%)
  other arithmetic  10.5 us (2%)
    pallas_call x5, Pallas kernels, attention(): pl.pallas_call(functools.partial(attn_body, n_heads, row0, chunk, slots,...  81.4 us
    ppermute x6, waiting for transfers between devices, combine(): lax.ppermute(sstat, 'cp', OTHER_CHIP)  76.8 us
    ppermute x4, waiting for transfers between devices, spread(): q_chip = lax.ppermute(q, 'cp', OTHER_CHIP)  60.6 us
    pallas_call x4, Pallas kernels, dense(): pl.pallas_call(functools.partial(dense_body, steps), grid=(steps,), in_sp...  58.8 us
    ppermute x1, waiting for transfers between devices, local_step(): wn0 = lax.ppermute(after(ws0, own1), 'tp', OTHER_HALF)  45.4 us
    ppermute x1, waiting for transfers between devices, local_step(): wn1 = lax.ppermute(after(ws1, k_sums[0]), 'tp', OTHER_HALF)  42.8 us
    pallas_call x2, Pallas kernels, project(): pl.pallas_call(functools.partial(project_body, n, width // 2, steps, bloc...  40.7 us
    pallas_call x2, Pallas kernels, project_own(): pl.pallas_call(functools.partial(own_body, len(o_list), width // 2), grid...  30.4 us
  transfers between devices with their start and end apart: 47, of which 11 were waited for; matrix products, arithmetic and copies ran while one was open for 8% of the time, Pallas kernels for 32%

profile of v3, /device:TPU:0, one launch (start us, length us, event | category | flops | bytes accessed | tf_op | source)
XLA Modules:
  0.0 626.9 jit_solution(8851612378709326662)
XLA Ops:
  0.6 10.4 %dense.4 = (f32[256,2048]{1,0:T(8,128)}, f32[1,256]{1,0:T(1,128)}) custom-call(bf16[1024,4096]{1,0:T(8,128)(2,1)} %bitcast.77, bf16[4096,2048]{1,0:T(8,128)(2,1)} %w.5), custom_call_target="tpu_custom_call" | custom-call | flops 10656000000 | bytes 16777216 | tf_op jit(solution)/shard_map/dense/pallas_call | solution.py:56
  26.8 19.2 %dense.5 = (f32[768,2048]{1,0:T(8,128)}, f32[1,768]{1,0:T(1,128)}) custom-call(bf16[1024,4096]{1,0:T(8,128)(2,1)} %bitcast.78, bf16[4096,2048]{1,0:T(8,128)(2,1)} %w.5), custom_call_target="tpu_custom_call" | custom-call | flops 17568000000 | bytes 16777216 | tf_op jit(solution)/shard_map/dense/pallas_call | solution.py:56
  48.0 6.2 constant_dynamic-slice_fusion
  64.7 24.2 %multiply_reduce_fusion = (f32[1024]{0:T(1024)S(1)}, f32[1024,2048]{1,0:T(8,128)}) fusion(bf16[1024,4096]{1,0:T(8,128)(2,1)} %bitcast.79, bf16[4096,2048]{1,0:T(8,128)(2,1)} %param.13), kind=kOutput, calls=%fused_computation | convolution fusion | flops 17184063488 | bytes 33558528 | tf_op jit(solution)/shard_map/dot_general | solution.py:479
  90.7 10.3 %dense.6 = (bf16[256,2048]{1,0:T(8,128)(2,1)}, f32[1,256]{1,0:T(1,128)}) custom-call(bf16[1024,4096]{1,0:T(8,128)(2,1)} %bitcast.80, bf16[4096,2048]{1,0:T(8,128)(2,1)} %w.7), custom_call_target="tpu_custom_call" | custom-call | flops 10656000000 | bytes 16777216 | tf_op jit(solution)/shard_map/dense/pallas_call | solution.py:56
  105.9 11.4 %attention.5 = (f32[4,64,2048]{2,1,0:T(8,128)}, f32[4,64,2048]{2,1,0:T(8,128)}, f32[4,32,128]{2,1,0:T(8,128)}) custom-call(s32[33]{0:T(128)} %pad_add_fusion.1.sc_ref, bf16[8,32,2048]{2,1,0:T(8,128)(2,1)} %bitcast.35, bf16[8,32,2048]{2,1,0:T(8,128)(2,1)} %copy-done.4, bf16[8,32,2048]{2,1,0:T(8,128)(2,1)} %copy-done.5, ...), custom_call_target="tpu_custom_call" | custom-call | flops 14040000512 | bytes 12582912 | tf_op jit(solution)/shard_map/attention/pallas_call | solution.py:168
  118.1 11.4 %attention.6 = (f32[4,64,2048]{2,1,0:T(8,128)}, f32[4,64,2048]{2,1,0:T(8,128)}, f32[4,32,128]{2,1,0:T(8,128)}) custom-call(s32[33]{0:T(128)} %pad_add_fusion.1.sc_ref, bf16[8,32,2048]{2,1,0:T(8,128)(2,1)} %bitcast.36, bf16[8,32,2048]{2,1,0:T(8,128)(2,1)} %copy-done.4, bf16[8,32,2048]{2,1,0:T(8,128)(2,1)} %copy-done.5, ...), custom_call_target="tpu_custom_call" | custom-call | flops 14040000512 | bytes 12582912 | tf_op jit(solution)/shard_map/attention/pallas_call | solution.py:168
  130.1 12.9 %collective-permute-done.11.qb = bf16[8,32,2048]{2,1,0:T(8,128)(2,1)} collective-permute-done((bf16[8,32,2048]{2,1,0:T(8,128)(2,1)S(1)}, bf16[8,32,2048]{2,1,0:T(8,128)(2,1)}, u32[]{:S(2)}, u32[]{:S(2)}) %collective-permute-start.11) | collective-permute-done | bytes 1048608 | tf_op jit(solution)/shard_map/ppermute | solution.py:460
  147.0 18.9 %dense.7 = (bf16[768,2048]{1,0:T(8,128)(2,1)}, f32[1,768]{1,0:T(1,128)}) custom-call(bf16[1024,4096]{1,0:T(8,128)(2,1)} %bitcast.81, bf16[4096,2048]{1,0:T(8,128)(2,1)} %w.7), custom_call_target="tpu_custom_call" | custom-call | flops 17568000000 | bytes 16777216 | tf_op jit(solution)/shard_map/dense/pallas_call | solution.py:56
  170.7 6.9 %rope.11 = bf16[768,2048]{1,0:T(8,128)(2,1)} custom-call(f32[1024,2048]{1,0:T(8,128)} %get-tuple-element.145.raw, f32[1,1024]{1,0:T(1,128)} %bitcast.76, f32[1,1024]{1,0:T(1,128)} %copy-done.33, f32[1,2048]{1,0:T(1,128)} %bitcast.73, f32[1024,128]{1,0:T(8,128)} %get-tuple-element.146.cos, f32[1024,128]{1,0:T(8,128)} %get-tuple-element.147.sin), custom_call_target="tpu_custom_call" | custom-call | flops 3456000000 | bytes 9437184 | tf_op jit(solution)/shard_map/rope/pallas_call | solution.py:86
  177.6 19.6 %attention.7 = (f32[8,64,2048]{2,1,0:T(8,128)}, f32[8,64,2048]{2,1,0:T(8,128)}, f32[8,32,128]{2,1,0:T(8,128)}) custom-call(s32[33]{0:T(128)} %pad_add_fusion.1.sc_ref, bf16[8,32,2048]{2,1,0:T(8,128)(2,1)} %bitcast.53, bf16[8,32,2048]{2,1,0:T(8,128)(2,1)} %collective-permute-done.11.qb, bf16[8,32,2048]{2,1,0:T(8,128)(2,1)} %collective-permute-done.12.qc, ...), custom_call_target="tpu_custom_call" | custom-call | flops 28080001024 | bytes 25165824 | tf_op jit(solution)/shard_map/attention/pallas_call | solution.py:168
  199.8 24.1 %collective-permute-done.17.qb = bf16[8,32,2048]{2,1,0:T(8,128)(2,1)} collective-permute-done((bf16[8,32,2048]{2,1,0:T(8,128)(2,1)S(1)}, bf16[8,32,2048]{2,1,0:T(8,128)(2,1)}, u32[]{:S(2)}, u32[]{:S(2)}) %collective-permute-start.17) | collective-permute-done | bytes 1048608 | tf_op jit(solution)/shard_map/ppermute | solution.py:460
  231.0 4.3 merge.8
  235.3 10.4 %collective-permute-done.16.fstat = f32[1,32,128]{2,1,0:T(8,128)S(1)} collective-permute-done((f32[1,32,128]{2,1,0:T(8,128)S(1)}, f32[1,32,128]{2,1,0:T(8,128)S(1)}, u32[]{:S(2)}, u32[]{:S(2)}) %collective-permute-start.16) | collective-permute-done | bytes 16416 | tf_op jit(solution)/shard_map/ppermute | solution.py:505
  251.2 19.5 %attention.8 = (f32[8,64,2048]{2,1,0:T(8,128)}, f32[8,64,2048]{2,1,0:T(8,128)}, f32[8,32,128]{2,1,0:T(8,128)}) custom-call(s32[33]{0:T(128)} %pad_add_fusion.1.sc_ref, bf16[8,32,2048]{2,1,0:T(8,128)(2,1)} %bitcast.50, bf16[8,32,2048]{2,1,0:T(8,128)(2,1)} %collective-permute-done.17.qb, bf16[8,32,2048]{2,1,0:T(8,128)(2,1)} %collective-permute-done.18.qc, ...), custom_call_target="tpu_custom_call" | custom-call | flops 28080001024 | bytes 25165824 | tf_op jit(solution)/shard_map/attention/pallas_call | solution.py:168
  273.4 23.6 %collective-permute-done.25.qb = bf16[8,32,2048]{2,1,0:T(8,128)(2,1)} collective-permute-done((bf16[8,32,2048]{2,1,0:T(8,128)(2,1)S(1)}, bf16[8,32,2048]{2,1,0:T(8,128)(2,1)}, u32[]{:S(2)}, u32[]{:S(2)}) %collective-permute-start.25) | collective-permute-done | bytes 1048608 | tf_op jit(solution)/shard_map/ppermute | solution.py:460
  296.9 22.2 %collective-permute-done.22.fstat = f32[1,32,128]{2,1,0:T(8,128)S(1)} collective-permute-done((f32[1,32,128]{2,1,0:T(8,128)S(1)}, f32[1,32,128]{2,1,0:T(8,128)S(1)}, u32[]{:S(2)}, u32[]{:S(2)}) %collective-permute-start.22) | collective-permute-done | bytes 16416 | tf_op jit(solution)/shard_map/ppermute | solution.py:505
  325.1 42.8 %collective-permute-done.39.refs_4_ = bf16[768,4096]{1,0:T(8,128)(2,1)} collective-permute-done((bf16[768,4096]{1,0:T(8,128)(2,1)}, bf16[768,4096]{1,0:T(8,128)(2,1)}, u32[]{:S(2)}, u32[]{:S(2)}) %collective-permute-start.39) | collective-permute-done | bytes 6291488 | tf_op jit(solution)/shard_map/ppermute | solution.py:484
  368.8 3.9 finish.7
  372.7 5.7 collective-permute-done.23.gstat
  379.0 4.3 merge.9
  383.4 19.5 %attention.9 = (f32[8,64,2048]{2,1,0:T(8,128)}, f32[8,64,2048]{2,1,0:T(8,128)}, f32[8,32,128]{2,1,0:T(8,128)}) custom-call(s32[33]{0:T(128)} %pad_add_fusion.1.sc_ref, bf16[8,32,2048]{2,1,0:T(8,128)(2,1)} %bitcast.47, bf16[8,32,2048]{2,1,0:T(8,128)(2,1)} %collective-permute-done.25.qb, bf16[8,32,2048]{2,1,0:T(8,128)(2,1)} %collective-permute-done.26.qc, ...), custom_call_target="tpu_custom_call" | custom-call | flops 28080001024 | bytes 25165824 | tf_op jit(solution)/shard_map/attention/pallas_call | solution.py:168
  405.7 45.4 %collective-permute-done.38.refs_3_ = bf16[256,4096]{1,0:T(8,128)(2,1)} collective-permute-done((bf16[256,4096]{1,0:T(8,128)(2,1)S(1)}, bf16[256,4096]{1,0:T(8,128)(2,1)}, u32[]{:S(2)}, u32[]{:S(2)}) %collective-permute-start.38) | collective-permute-done | bytes 2097184 | tf_op jit(solution)/shard_map/ppermute | solution.py:478
  452.9 44.2 %collective-permute-done.30.fstat = f32[2,32,128]{2,1,0:T(8,128)S(1)} collective-permute-done((f32[2,32,128]{2,1,0:T(8,128)S(1)}, f32[2,32,128]{2,1,0:T(8,128)S(1)}, u32[]{:S(2)}, u32[]{:S(2)}) %collective-permute-start.30) | collective-permute-done | bytes 32800 | tf_op jit(solution)/shard_map/ppermute | solution.py:505
  497.7 5.5 finish.8
  514.3 15.1 %project_own.2.refs_9_ = f32[512,4096]{1,0:T(8,128)} custom-call(s32[2]{0:T(128)} %pad_add_fusion.sc_ref, bf16[128,2048]{1,0:T(8,128)(2,1)} %bitcast.60, bf16[128,2048]{1,0:T(8,128)(2,1)} %bitcast.62, bf16[256,2048]{1,0:T(8,128)(2,1)} %bitcast.58, bf16[2048,4096]{1,0:T(8,128)(2,1)} %refs_3_.3), custom_call_target="tpu_custom_call" | custom-call | flops 14616000512 | bytes 16777216 | tf_op jit(solution)/shard_map/project_own/pallas_call | solution.py:373
  529.5 5.2 finish.9
  538.8 13.1 %collective-permute-done.37.refs_2_ = bf16[256,2048]{1,0:T(8,128)(2,1)} collective-permute-done((bf16[256,2048]{1,0:T(8,128)(2,1)S(1)}, bf16[256,2048]{1,0:T(8,128)(2,1)}, u32[]{:S(2)}, u32[]{:S(2)}) %collective-permute-start.37) | collective-permute-done | bytes 1048608 | tf_op jit(solution)/shard_map/ppermute | solution.py:513
  552.2 20.4 %project.2.refs_10_ = bf16[1024,4096]{1,0:T(8,128)(2,1)} custom-call(s32[2]{0:T(128)} %pad_add_fusion.sc_ref, bf16[128,2048]{1,0:T(8,128)(2,1)} %collective-permute-done.35.refs_0_, bf16[128,2048]{1,0:T(8,128)(2,1)} %collective-permute-done.36.refs_1_, bf16[256,2048]{1,0:T(8,128)(2,1)} %collective-permute-done.37.refs_2_, ...), custom_call_target="tpu_custom_call" | custom-call | flops 18215999488 | bytes 16777216 | tf_op jit(solution)/shard_map/project/pallas_call | solution.py:403
  584.4 3.9 finish.11
  589.6 15.3 %project_own.3.refs_9_ = f32[512,4096]{1,0:T(8,128)} custom-call(s32[2]{0:T(128)} %pad_add_fusion.sc_ref, bf16[256,2048]{1,0:T(8,128)(2,1)} %bitcast.57, bf16[128,2048]{1,0:T(8,128)(2,1)} %bitcast.65, bf16[128,2048]{1,0:T(8,128)(2,1)} %bitcast.67, bf16[2048,4096]{1,0:T(8,128)(2,1)} %refs_3_.3), custom_call_target="tpu_custom_call" | custom-call | flops 14616000512 | bytes 16777216 | tf_op jit(solution)/shard_map/project_own/pallas_call | solution.py:373
  606.4 20.3 %project.3 = bf16[1024,4096]{1,0:T(8,128)(2,1)} custom-call(s32[2]{0:T(128)} %pad_add_fusion.sc_ref, bf16[256,2048]{1,0:T(8,128)(2,1)} %collective-permute-done.33.refs_0_, bf16[128,2048]{1,0:T(8,128)(2,1)} %copy-done.37, bf16[128,2048]{1,0:T(8,128)(2,1)} %copy-done.38, ...), custom_call_target="tpu_custom_call", output_to_operand_aliasing={{}: (11, {})} | custom-call | flops 18215999488 | bytes 16777216 | tf_op jit(solution)/shard_map/project/pallas_call | solution.py:403
  (205 shorter events, 105.7 us)
Async XLA Ops:
  46.0 44.4 %collective-permute-start.3 = (bf16[8,32,2048]{2,1,0:T(8,128)(2,1)S(1)}, bf16[8,32,2048]{2,1,0:T(8,128)(2,1)S(1)}, u32[]{:S(2)}, u32[]{:S(2)}) collective-permute-start(bf16[8,32,2048]{2,1,0:T(8,128)(2,1)S(1)} %bitcast.37), channel_id=1, source_target_pairs={{0,2},{2,0},{1,3},{3,1},{4,6},{6,4},{5,7},{7,5}} | collective-permute-start | bytes 3145736 | tf_op jit(solution)/shard_map/ppermute | solution.py:460
  48.0 56.9 %collective-permute-start.4 = (bf16[8,32,2048]{2,1,0:T(8,128)(2,1)S(1)}, bf16[8,32,2048]{2,1,0:T(8,128)(2,1)S(1)}, u32[]{:S(2)}, u32[]{:S(2)}) collective-permute-start(bf16[8,32,2048]{2,1,0:T(8,128)(2,1)S(1)} %bitcast.38), channel_id=1, source_target_pairs={{0,1},{1,0},{2,3},{3,2},{4,5},{5,4},{6,7},{7,6}} | collective-permute-start | bytes 3145736 | tf_op jit(solution)/shard_map/ppermute | solution.py:461
  117.3 26.2 %collective-permute-start.6 = (f32[4,64,2048]{2,1,0:T(8,128)}, f32[4,64,2048]{2,1,0:T(8,128)}, u32[]{:S(2)}, u32[]{:S(2)}) collective-permute-start(f32[4,64,2048]{2,1,0:T(8,128)} %get-tuple-element.89), channel_id=1, source_target_pairs={{0,1},{1,0},{2,3},{3,2},{4,5},{5,4},{6,7},{7,6}} | collective-permute-start | bytes 6291464 | tf_op jit(solution)/shard_map/ppermute | solution.py:498
  129.5 36.4 %collective-permute-start.9 = (f32[4,64,2048]{2,1,0:T(8,128)}, f32[4,64,2048]{2,1,0:T(8,128)S(1)}, u32[]{:S(2)}, u32[]{:S(2)}) collective-permute-start(f32[4,64,2048]{2,1,0:T(8,128)} %get-tuple-element.96), channel_id=1, source_target_pairs={{0,1},{1,0},{2,3},{3,2},{4,5},{5,4},{6,7},{7,6}} | collective-permute-start | bytes 6291464 | tf_op jit(solution)/shard_map/ppermute | solution.py:498
  130.0 47.6 %collective-permute-start.12 = (bf16[8,32,2048]{2,1,0:T(8,128)(2,1)S(1)}, bf16[8,32,2048]{2,1,0:T(8,128)(2,1)}, u32[]{:S(2)}, u32[]{:S(2)}) collective-permute-start(bf16[8,32,2048]{2,1,0:T(8,128)(2,1)S(1)} %bitcast.55), channel_id=1, source_target_pairs={{0,1},{1,0},{2,3},{3,2},{4,5},{5,4},{6,7},{7,6}} | collective-permute-start | bytes 3145736 | tf_op jit(solution)/shard_map/ppermute | solution.py:461
  143.0 34.7 %collective-permute-start.13 = (bf16[8,32,2048]{2,1,0:T(8,128)(2,1)}, bf16[8,32,2048]{2,1,0:T(8,128)(2,1)}, u32[]{:S(2)}, u32[]{:S(2)}) collective-permute-start(bf16[8,32,2048]{2,1,0:T(8,128)(2,1)} %collective-permute-done.11.qb), channel_id=1, source_target_pairs={{0,1},{1,0},{2,3},{3,2},{4,5},{5,4},{6,7},{7,6}} | collective-permute-start | bytes 3145736 | tf_op jit(solution)/shard_map/ppermute | solution.py:462
  197.3 33.4 %collective-permute-start.14 = (f32[8,64,2048]{2,1,0:T(8,128)}, f32[8,64,2048]{2,1,0:T(8,128)}, u32[]{:S(2)}, u32[]{:S(2)}) collective-permute-start(f32[8,64,2048]{2,1,0:T(8,128)} %get-tuple-element.105), channel_id=1, source_target_pairs={{0,1},{1,0},{2,3},{3,2},{4,5},{5,4},{6,7},{7,6}} | collective-permute-start | bytes 12582920 | tf_op jit(solution)/shard_map/ppermute | solution.py:498
  198.4 47.4 %collective-permute-start.8 = (f32[4,32,2048]{2,1,0:T(8,128)}, f32[4,32,2048]{2,1,0:T(8,128)S(1)}, u32[]{:S(2)}, u32[]{:S(2)}) collective-permute-start(f32[4,32,2048]{2,1,0:T(8,128)} %get-tuple-element.94), channel_id=1, source_target_pairs={{0,2},{2,0},{1,3},{3,1},{4,6},{6,4},{5,7},{7,5}} | collective-permute-start | bytes 3145736 | tf_op jit(solution)/shard_map/ppermute | solution.py:505
  199.8 51.4 %collective-permute-start.18 = (bf16[8,32,2048]{2,1,0:T(8,128)(2,1)S(1)}, bf16[8,32,2048]{2,1,0:T(8,128)(2,1)}, u32[]{:S(2)}, u32[]{:S(2)}) collective-permute-start(bf16[8,32,2048]{2,1,0:T(8,128)(2,1)S(1)} %bitcast.52), channel_id=1, source_target_pairs={{0,1},{1,0},{2,3},{3,2},{4,5},{5,4},{6,7},{7,6}} | collective-permute-start | bytes 3145736 | tf_op jit(solution)/shard_map/ppermute | solution.py:461
  223.9 27.3 %collective-permute-start.19 = (bf16[8,32,2048]{2,1,0:T(8,128)(2,1)}, bf16[8,32,2048]{2,1,0:T(8,128)(2,1)}, u32[]{:S(2)}, u32[]{:S(2)}) collective-permute-start(bf16[8,32,2048]{2,1,0:T(8,128)(2,1)} %collective-permute-done.17.qb), channel_id=1, source_target_pairs={{0,1},{1,0},{2,3},{3,2},{4,5},{5,4},{6,7},{7,6}} | collective-permute-start | bytes 3145736 | tf_op jit(solution)/shard_map/ppermute | solution.py:462
  230.1 137.7 %collective-permute-start.39 = (bf16[768,4096]{1,0:T(8,128)(2,1)}, bf16[768,4096]{1,0:T(8,128)(2,1)}, u32[]{:S(2)}, u32[]{:S(2)}) collective-permute-start(bf16[768,4096]{1,0:T(8,128)(2,1)} %constant_dynamic-slice_fusion), channel_id=1, source_target_pairs={{0,4},{4,0},{1,5},{5,1},{2,6},{6,2},{3,7},{7,3}} | collective-permute-start | bytes 18874376 | tf_op jit(solution)/shard_map/ppermute | solution.py:484
  270.7 107.7 %collective-permute-start.20 = (f32[8,64,2048]{2,1,0:T(8,128)}, f32[8,64,2048]{2,1,0:T(8,128)}, u32[]{:S(2)}, u32[]{:S(2)}) collective-permute-start(f32[8,64,2048]{2,1,0:T(8,128)} %get-tuple-element.113), channel_id=1, source_target_pairs={{0,1},{1,0},{2,3},{3,2},{4,5},{5,4},{6,7},{7,6}} | collective-permute-start | bytes 12582920 | tf_op jit(solution)/shard_map/ppermute | solution.py:498
  270.8 26.2 %collective-permute-start.25 = (bf16[8,32,2048]{2,1,0:T(8,128)(2,1)S(1)}, bf16[8,32,2048]{2,1,0:T(8,128)(2,1)}, u32[]{:S(2)}, u32[]{:S(2)}) collective-permute-start(bf16[8,32,2048]{2,1,0:T(8,128)(2,1)S(1)} %bitcast.48), channel_id=1, source_target_pairs={{0,2},{2,0},{1,3},{3,1},{4,6},{6,4},{5,7},{7,5}} | collective-permute-start | bytes 3145736 | tf_op jit(solution)/shard_map/ppermute | solution.py:460
  271.3 96.5 %collective-permute-start.21 = (f32[4,32,2048]{2,1,0:T(8,128)}, f32[4,32,2048]{2,1,0:T(8,128)S(1)}, u32[]{:S(2)}, u32[]{:S(2)}) collective-permute-start(f32[4,32,2048]{2,1,0:T(8,128)} %get-tuple-element.115), channel_id=1, source_target_pairs={{0,2},{2,0},{1,3},{3,1},{4,6},{6,4},{5,7},{7,5}} | collective-permute-start | bytes 3145736 | tf_op jit(solution)/shard_map/ppermute | solution.py:505
  272.8 46.3 %collective-permute-start.22 = (f32[1,32,128]{2,1,0:T(8,128)S(1)}, f32[1,32,128]{2,1,0:T(8,128)S(1)}, u32[]{:S(2)}, u32[]{:S(2)}) collective-permute-start(f32[1,32,128]{2,1,0:T(8,128)S(1)} %copy-done.41), channel_id=1, source_target_pairs={{0,2},{2,0},{1,3},{3,1},{4,6},{6,4},{5,7},{7,5}} | collective-permute-start | bytes 49160 | tf_op jit(solution)/shard_map/ppermute | solution.py:505
  296.9 86.5 %collective-permute-start.26 = (bf16[8,32,2048]{2,1,0:T(8,128)(2,1)S(1)}, bf16[8,32,2048]{2,1,0:T(8,128)(2,1)}, u32[]{:S(2)}, u32[]{:S(2)}) collective-permute-start(bf16[8,32,2048]{2,1,0:T(8,128)(2,1)S(1)} %bitcast.49), channel_id=1, source_target_pairs={{0,1},{1,0},{2,3},{3,2},{4,5},{5,4},{6,7},{7,6}} | collective-permute-start | bytes 3145736 | tf_op jit(solution)/shard_map/ppermute | solution.py:461
  319.1 64.3 %collective-permute-start.27 = (bf16[8,32,2048]{2,1,0:T(8,128)(2,1)}, bf16[8,32,2048]{2,1,0:T(8,128)(2,1)}, u32[]{:S(2)}, u32[]{:S(2)}) collective-permute-start(bf16[8,32,2048]{2,1,0:T(8,128)(2,1)} %collective-permute-done.25.qb), channel_id=1, source_target_pairs={{0,1},{1,0},{2,3},{3,2},{4,5},{5,4},{6,7},{7,6}} | collective-permute-start | bytes 3145736 | tf_op jit(solution)/shard_map/ppermute | solution.py:462
  367.8 169.3 %collective-permute-start.41 = (bf16[768,4096]{1,0:T(8,128)(2,1)}, bf16[768,4096]{1,0:T(8,128)(2,1)}, u32[]{:S(2)}, u32[]{:S(2)}) collective-permute-start(bf16[768,4096]{1,0:T(8,128)(2,1)} %collective-permute-done.39.refs_4_), channel_id=1, source_target_pairs={{0,1},{1,0},{2,3},{3,2},{4,5},{5,4},{6,7},{7,6}} | collective-permute-start | bytes 18874376 | tf_op jit(solution)/shard_map/ppermute | solution.py:486
  402.9 101.8 %collective-permute-start.28 = (f32[8,64,2048]{2,1,0:T(8,128)}, f32[8,64,2048]{2,1,0:T(8,128)}, u32[]{:S(2)}, u32[]{:S(2)}) collective-permute-start(f32[8,64,2048]{2,1,0:T(8,128)} %get-tuple-element.123), channel_id=1, source_target_pairs={{0,1},{1,0},{2,3},{3,2},{4,5},{5,4},{6,7},{7,6}} | collective-permute-start | bytes 12582920 | tf_op jit(solution)/shard_map/ppermute | solution.py:498
  403.1 48.0 %collective-permute-start.38 = (bf16[256,4096]{1,0:T(8,128)(2,1)S(1)}, bf16[256,4096]{1,0:T(8,128)(2,1)}, u32[]{:S(2)}, u32[]{:S(2)}) collective-permute-start(bf16[256,4096]{1,0:T(8,128)(2,1)S(1)} %copy-done.7), channel_id=1, source_target_pairs={{0,4},{4,0},{1,5},{5,1},{2,6},{6,2},{3,7},{7,3}} | collective-permute-start | bytes 6291464 | tf_op jit(solution)/shard_map/ppermute | solution.py:478
  403.7 93.5 %collective-permute-start.29 = (f32[8,32,2048]{2,1,0:T(8,128)}, f32[8,32,2048]{2,1,0:T(8,128)}, u32[]{:S(2)}, u32[]{:S(2)}) collective-permute-start(f32[8,32,2048]{2,1,0:T(8,128)} %get-tuple-element.125), channel_id=1, source_target_pairs={{0,2},{2,0},{1,3},{3,1},{4,6},{6,4},{5,7},{7,5}} | collective-permute-start | bytes 6291464 | tf_op jit(solution)/shard_map/ppermute | solution.py:505
  404.0 108.7 %collective-permute-start.24 = (f32[8,32,2048]{2,1,0:T(8,128)}, f32[8,32,2048]{2,1,0:T(8,128)}, u32[]{:S(2)}, u32[]{:S(2)}) collective-permute-start(f32[8,32,2048]{2,1,0:T(8,128)} %get-tuple-element.119), channel_id=1, source_target_pairs={{0,2},{2,0},{1,3},{3,1},{4,6},{6,4},{5,7},{7,5}} | collective-permute-start | bytes 6291464 | tf_op jit(solution)/shard_map/ppermute | solution.py:505
  451.1 46.0 %collective-permute-start.30 = (f32[2,32,128]{2,1,0:T(8,128)S(1)}, f32[2,32,128]{2,1,0:T(8,128)S(1)}, u32[]{:S(2)}, u32[]{:S(2)}) collective-permute-start(f32[2,32,128]{2,1,0:T(8,128)S(1)} %copy-done.39), channel_id=1, source_target_pairs={{0,2},{2,0},{1,3},{3,1},{4,6},{6,4},{5,7},{7,5}} | collective-permute-start | bytes 98312 | tf_op jit(solution)/shard_map/ppermute | solution.py:505
  497.1 37.5 %collective-permute-start.40 = (bf16[256,4096]{1,0:T(8,128)(2,1)}, bf16[256,4096]{1,0:T(8,128)(2,1)}, u32[]{:S(2)}, u32[]{:S(2)}) collective-permute-start(bf16[256,4096]{1,0:T(8,128)(2,1)} %collective-permute-done.38.refs_3_), channel_id=1, source_target_pairs={{0,1},{1,0},{2,3},{3,2},{4,5},{5,4},{6,7},{7,6}} | collective-permute-start | bytes 6291464 | tf_op jit(solution)/shard_map/ppermute | solution.py:486
  503.3 32.9 %collective-permute-start.35 = (bf16[128,2048]{1,0:T(8,128)(2,1)S(1)}, bf16[128,2048]{1,0:T(8,128)(2,1)}, u32[]{:S(2)}, u32[]{:S(2)}) collective-permute-start(bf16[128,2048]{1,0:T(8,128)(2,1)S(1)} %bitcast.61), channel_id=1, source_target_pairs={{0,4},{4,0},{1,5},{5,1},{2,6},{6,2},{3,7},{7,3}} | collective-permute-start | bytes 1572872 | tf_op jit(solution)/shard_map/ppermute | solution.py:513
  512.6 39.2 %collective-permute-start.37 = (bf16[256,2048]{1,0:T(8,128)(2,1)S(1)}, bf16[256,2048]{1,0:T(8,128)(2,1)}, u32[]{:S(2)}, u32[]{:S(2)}) collective-permute-start(bf16[256,2048]{1,0:T(8,128)(2,1)S(1)} %bitcast.59), channel_id=1, source_target_pairs={{0,4},{4,0},{1,5},{5,1},{2,6},{6,2},{3,7},{7,3}} | collective-permute-start | bytes 3145736 | tf_op jit(solution)/shard_map/ppermute | solution.py:513
  534.7 37.9 %collective-permute-start.42 = (f32[1,32,128]{2,1,0:T(8,128)S(1)}, f32[1,32,128]{2,1,0:T(8,128)S(1)}, u32[]{:S(2)}, u32[]{:S(2)}) collective-permute-start(f32[1,32,128]{2,1,0:T(8,128)S(1)} %copy-done.44), channel_id=1, source_target_pairs={{0,2},{2,0},{1,3},{3,1},{4,6},{6,4},{5,7},{7,5}} | collective-permute-start | bytes 49160 | tf_op jit(solution)/shard_map/ppermute | solution.py:505
  536.2 43.6 %collective-permute-start.45 = (f32[1,32,128]{2,1,0:T(8,128)S(1)}, f32[1,32,128]{2,1,0:T(8,128)S(1)}, u32[]{:S(2)}, u32[]{:S(2)}) collective-permute-start(f32[1,32,128]{2,1,0:T(8,128)S(1)} %copy-done.43), channel_id=1, source_target_pairs={{0,2},{2,0},{1,3},{3,1},{4,6},{6,4},{5,7},{7,5}} | collective-permute-start | bytes 49160 | tf_op jit(solution)/shard_map/ppermute | solution.py:505
  536.7 68.1 %collective-permute-start.33 = (bf16[256,2048]{1,0:T(8,128)(2,1)}, bf16[256,2048]{1,0:T(8,128)(2,1)}, u32[]{:S(2)}, u32[]{:S(2)}) collective-permute-start(bf16[256,2048]{1,0:T(8,128)(2,1)} %bitcast.56), channel_id=1, source_target_pairs={{0,4},{4,0},{1,5},{5,1},{2,6},{6,2},{3,7},{7,3}} | collective-permute-start | bytes 3145736 | tf_op jit(solution)/shard_map/ppermute | solution.py:513
  537.1 35.5 %collective-permute-start.34 = (f32[4,32,2048]{2,1,0:T(8,128)}, f32[4,32,2048]{2,1,0:T(8,128)S(1)}, u32[]{:S(2)}, u32[]{:S(2)}) collective-permute-start(f32[4,32,2048]{2,1,0:T(8,128)} %get-tuple-element.133), channel_id=1, source_target_pairs={{0,2},{2,0},{1,3},{3,1},{4,6},{6,4},{5,7},{7,5}} | collective-permute-start | bytes 3145736 | tf_op jit(solution)/shard_map/ppermute | solution.py:505
  551.9 31.6 %collective-permute-start.44 = (f32[4,32,2048]{2,1,0:T(8,128)S(1)}, f32[4,32,2048]{2,1,0:T(8,128)S(1)}, u32[]{:S(2)}, u32[]{:S(2)}) collective-permute-start(f32[4,32,2048]{2,1,0:T(8,128)S(1)} %copy-done.36), channel_id=1, source_target_pairs={{0,2},{2,0},{1,3},{3,1},{4,6},{6,4},{5,7},{7,5}} | collective-permute-start | bytes 3145736 | tf_op jit(solution)/shard_map/ppermute | solution.py:505
  578.1 26.8 %collective-permute-start.43 = (bf16[128,2048]{1,0:T(8,128)(2,1)}, bf16[128,2048]{1,0:T(8,128)(2,1)S(1)}, u32[]{:S(2)}, u32[]{:S(2)}) collective-permute-start(bf16[128,2048]{1,0:T(8,128)(2,1)} %bitcast.64), channel_id=1, source_target_pairs={{0,4},{4,0},{1,5},{5,1},{2,6},{6,2},{3,7},{7,3}} | collective-permute-start | bytes 1572872 | tf_op jit(solution)/shard_map/ppermute | solution.py:513
  (62 other events, 880.7 us)

commit v4 on v3

--- a/solution.py
+++ b/solution.py
@@ -14,7 +14,7 @@
 LOG2E = 1.4426950408889634
 HD = 128
 LAG = 2
-ROPE_BLOCK = 256
+ROPE_BLOCK = 384
 P_BLOCK = 1024
 GROUPS = ((24, 8), (0, 8), (8, 8), (16, 8))
 ATTEND = ((0, 0, 4), (0, 4, 4), (1, 0, 8), (2, 0, 8), (3, 0, 8))
@@ -132,8 +132,10 @@
         s = jnp.where(ok, s * scale, NEG)
         top = jnp.maximum(jnp.max(s, axis=0, keepdims=True), FLOOR)
         p = jnp.exp2(s - top)
-        stat[0, h:h + 1, :] = top
-        stat[0, n_heads + h:n_heads + h + 1, :] = jnp.sum(p, axis=0, keepdims=True)
+        den = jnp.sum(p, axis=0, keepdims=True)
+        for at, val in ((h, top), (n_heads + h, den)):
+            stat[0, at:at + 1, :] = val
+            give[0, at:at + 1, n_heads * HD:] = val
         return p.astype(jnp.bfloat16)
 
     def values(h, p):
@@ -164,15 +166,17 @@
     cache_spec = pl.BlockSpec((1, slots, n_heads, HD), lambda b, s: (b + row0, 0, 0, 0))
     out_spec = pl.BlockSpec((1, 2 * chunk, width), lambda b, s: (b, 0, 0))
     stat_spec = pl.BlockSpec((1, 2 * n_heads, 4 * chunk), lambda b, s: (b, 0, 0))
+    give_spec = pl.BlockSpec((1, 2 * chunk, width + 4 * chunk), lambda b, s: (b, 0, 0))
     out = jax.ShapeDtypeStruct((rows, 2 * chunk, width), jnp.float32)
+    give = jax.ShapeDtypeStruct((rows, 2 * chunk, width + 4 * chunk), jnp.float32)
     return pl.pallas_call(
         functools.partial(attn_body, n_heads, row0, chunk, slots, pitch),
         grid_spec=pltpu.PrefetchScalarGridSpec(
             num_scalar_prefetch=1, grid=(rows,),
             in_specs=[q_spec] * 4 + [cache_spec] * 2 + [k_spec, v_spec],
-            out_specs=[out_spec] * 2 + [stat_spec],
+            out_specs=[out_spec, give_spec, stat_spec],
             scratch_shapes=[pltpu.VMEM((slots * pitch, HD), jnp.float32)] * 2),
-        out_shape=[out, out, jax.ShapeDtypeStruct((rows, 2 * n_heads, 4 * chunk), jnp.float32)],
+        out_shape=[out, give, jax.ShapeDtypeStruct((rows, 2 * n_heads, 4 * chunk), jnp.float32)],
         compiler_params=params(),
         cost_estimate=cost(rows * 3.9, rows * slots * width * 6),
         name="attention",
@@ -213,10 +217,11 @@
     lead = row // span
     half = pl.BlockSpec((span, chunk, width), lambda i: (i + lead, 1, 0))
     stats = pl.BlockSpec((span, 2 * n_heads, 4 * chunk), lambda i: (i + lead, 0, 0))
+    given = pl.BlockSpec((span, 2 * n_heads, 4 * chunk), lambda i: (i + lead, 0, width // (4 * chunk)))
     return pl.pallas_call(
         functools.partial(merge_body, n_heads, chunk, span),
         grid=(rows // span,),
-        in_specs=[half, half, stats, stats],
+        in_specs=[half, half, stats, given],
         out_specs=[pl.BlockSpec((span, chunk, width), lambda i: (i, 0, 0)),
                    pl.BlockSpec((1, 2 * n_heads, 4 * chunk), lambda i: (i, 0, 0))],
         out_shape=[jax.ShapeDtypeStruct((rows, chunk, width), jnp.float32),
@@ -253,10 +258,11 @@
     half = pl.BlockSpec((span, chunk, width), lambda i: (i + lead, 0, 0))
     plain = pl.BlockSpec((span, chunk, width), lambda i: (i, 0, 0))
     stats = pl.BlockSpec((span, 2 * n_heads, 4 * chunk), lambda i: (i + lead, 0, 0))
+    given = pl.BlockSpec((span, 2 * n_heads, 4 * chunk), lambda i: (i + lead, 0, width // (4 * chunk)))
     return pl.pallas_call(
         functools.partial(finish_body, n_heads, chunk, span),
         grid=(rows // span,),
-        in_specs=[half, half, plain, stats, stats, pl.BlockSpec((1, 2 * n_heads, 4 * chunk), lambda i: (i, 0, 0))],
+        in_specs=[half, half, plain, stats, given, pl.BlockSpec((1, 2 * n_heads, 4 * chunk), lambda i: (i, 0, 0))],
         out_specs=plain,
         out_shape=jax.ShapeDtypeStruct((rows, chunk, width), jnp.bfloat16),
         compiler_params=params(),
@@ -495,7 +501,8 @@
             side, kv_row = (1, row0) if g else (0, off)
             keep, give, stat = attention(after(scalars, done), q_sets[g], off, count, cache_k, cache_v,
                                       k_new[side], kv_row, v_new[side], kv_row, row0)
-            parts[u] = (keep, give, stat, lax.ppermute(give, 'cp', OTHER_CORE), lax.ppermute(stat, 'cp', OTHER_CORE))
+            got = lax.ppermute(give, 'cp', OTHER_CORE)
+            parts[u] = (keep, give, stat, got, got)
             return stat
 
         def combine(m, done):

time: 637 us -> 641 us (level)
  waiting for transfers between devices: 248 us -> 256 us
    ppermute x1, waiting for transfers between devices: 42.8 us -> 54.7 us  [local_step(): wn1 = lax.ppermute(after(ws1, k_sums[0]), 'tp', OTHER_HALF)]
    unnamed x96 -> x86, local copies, waits for them, and re-layouts: 18 us -> 19 us
  transfers between devices with their start and end apart: 47 -> 42, of which waited for: 11 -> 10; matrix products, arithmetic and copies ran while one was open for 8% -> 8% of each run, Pallas kernels for 32% -> 28%
where the time goes in v4:
time: 641 us; the launch traced here: 630 us
  Pallas kernels  281 us (44%)
  waiting for transfers between devices  256 us (40%)
  starting transfers between devices  29.6 us (5%)
  local copies, waits for them, and re-layouts  29.1 us (5%)
  matrix products  24.2 us (4%)
  other arithmetic  10.1 us (2%)
    pallas_call x5, Pallas kernels, attention(): pl.pallas_call(functools.partial(attn_body, n_heads, row0, chunk, slots,...  81.6 us
    ppermute x6, waiting for transfers between devices, combine(): lax.ppermute(sstat, 'cp', OTHER_CHIP)  77.3 us
    ppermute x4, waiting for transfers between devices, spread(): q_chip = lax.ppermute(q, 'cp', OTHER_CHIP)  61 us
    pallas_call x4, Pallas kernels, dense(): pl.pallas_call(functools.partial(dense_body, steps), grid=(steps,), in_sp...  58.8 us
    ppermute x1, waiting for transfers between devices, local_step(): wn1 = lax.ppermute(after(ws1, k_sums[0]), 'tp', OTHER_HALF)  54.7 us
    ppermute x1, waiting for transfers between devices, local_step(): wn0 = lax.ppermute(after(ws0, own1), 'tp', OTHER_HALF)  45.6 us
    pallas_call x2, Pallas kernels, project(): pl.pallas_call(functools.partial(project_body, n, width // 2, steps, bloc...  40.8 us
    pallas_call x2, Pallas kernels, project_own(): pl.pallas_call(functools.partial(own_body, len(o_list), width // 2), grid...  30.6 us
  transfers between devices with their start and end apart: 42, of which 10 were waited for; matrix products, arithmetic and copies ran while one was open for 8% of the time, Pallas kernels for 28%

profile of v4, /device:TPU:0, one launch (start us, length us, event | category | flops | bytes accessed | tf_op | source)
XLA Modules:
  0.0 630.5 jit_solution(10988355843847139074)
XLA Ops:
  0.6 10.4 %dense.4 = (f32[256,2048]{1,0:T(8,128)}, f32[1,256]{1,0:T(1,128)}) custom-call(bf16[1024,4096]{1,0:T(8,128)(2,1)} %bitcast.77, bf16[4096,2048]{1,0:T(8,128)(2,1)} %w.5), custom_call_target="tpu_custom_call" | custom-call | flops 10656000000 | bytes 16777216 | tf_op jit(solution)/shard_map/dense/pallas_call | solution.py:56
  26.5 19.2 %dense.5 = (f32[768,2048]{1,0:T(8,128)}, f32[1,768]{1,0:T(1,128)}) custom-call(bf16[1024,4096]{1,0:T(8,128)(2,1)} %bitcast.78, bf16[4096,2048]{1,0:T(8,128)(2,1)} %w.5), custom_call_target="tpu_custom_call" | custom-call | flops 17568000000 | bytes 16777216 | tf_op jit(solution)/shard_map/dense/pallas_call | solution.py:56
  47.7 6.2 constant_dynamic-slice_fusion
  63.7 24.2 %multiply_reduce_fusion = (f32[1024]{0:T(1024)S(1)}, f32[1024,2048]{1,0:T(8,128)}) fusion(bf16[1024,4096]{1,0:T(8,128)(2,1)} %bitcast.79, bf16[4096,2048]{1,0:T(8,128)(2,1)} %param.13), kind=kOutput, calls=%fused_computation | convolution fusion | flops 17184063488 | bytes 33558528 | tf_op jit(solution)/shard_map/dot_general | solution.py:485
  89.7 10.3 %dense.6 = (bf16[256,2048]{1,0:T(8,128)(2,1)}, f32[1,256]{1,0:T(1,128)}) custom-call(bf16[1024,4096]{1,0:T(8,128)(2,1)} %bitcast.80, bf16[4096,2048]{1,0:T(8,128)(2,1)} %w.7), custom_call_target="tpu_custom_call" | custom-call | flops 10656000000 | bytes 16777216 | tf_op jit(solution)/shard_map/dense/pallas_call | solution.py:56
  104.5 11.6 %attention.5 = (f32[4,64,2048]{2,1,0:T(8,128)}, f32[4,64,2176]{2,1,0:T(8,128)}, f32[4,32,128]{2,1,0:T(8,128)}) custom-call(s32[33]{0:T(128)} %pad_add_fusion.1.sc_ref, bf16[8,32,2048]{2,1,0:T(8,128)(2,1)} %bitcast.35, bf16[8,32,2048]{2,1,0:T(8,128)(2,1)} %copy-done.4, bf16[8,32,2048]{2,1,0:T(8,128)(2,1)} %copy-done.5, ...), custom_call_target="tpu_custom_call" | custom-call | flops 14040000512 | bytes 12582912 | tf_op jit(solution)/shard_map/attention/pallas_call | solution.py:172
  116.9 11.3 %attention.6 = (f32[4,64,2048]{2,1,0:T(8,128)}, f32[4,64,2176]{2,1,0:T(8,128)}, f32[4,32,128]{2,1,0:T(8,128)}) custom-call(s32[33]{0:T(128)} %pad_add_fusion.1.sc_ref, bf16[8,32,2048]{2,1,0:T(8,128)(2,1)} %bitcast.36, bf16[8,32,2048]{2,1,0:T(8,128)(2,1)} %copy-done.4, bf16[8,32,2048]{2,1,0:T(8,128)(2,1)} %copy-done.5, ...), custom_call_target="tpu_custom_call" | custom-call | flops 14040000512 | bytes 12582912 | tf_op jit(solution)/shard_map/attention/pallas_call | solution.py:172
  128.7 13.1 %collective-permute-done.9.qb = bf16[8,32,2048]{2,1,0:T(8,128)(2,1)} collective-permute-done((bf16[8,32,2048]{2,1,0:T(8,128)(2,1)S(1)}, bf16[8,32,2048]{2,1,0:T(8,128)(2,1)}, u32[]{:S(2)}, u32[]{:S(2)}) %collective-permute-start.9) | collective-permute-done | bytes 1048608 | tf_op jit(solution)/shard_map/ppermute | solution.py:466
  145.2 18.9 %dense.7 = (bf16[768,2048]{1,0:T(8,128)(2,1)}, f32[1,768]{1,0:T(1,128)}) custom-call(bf16[1024,4096]{1,0:T(8,128)(2,1)} %bitcast.81, bf16[4096,2048]{1,0:T(8,128)(2,1)} %w.7), custom_call_target="tpu_custom_call" | custom-call | flops 17568000000 | bytes 16777216 | tf_op jit(solution)/shard_map/dense/pallas_call | solution.py:56
  168.9 5.3 rope.11
  174.2 19.6 %attention.7 = (f32[8,64,2048]{2,1,0:T(8,128)}, f32[8,64,2176]{2,1,0:T(8,128)}, f32[8,32,128]{2,1,0:T(8,128)}) custom-call(s32[33]{0:T(128)} %pad_add_fusion.1.sc_ref, bf16[8,32,2048]{2,1,0:T(8,128)(2,1)} %bitcast.53, bf16[8,32,2048]{2,1,0:T(8,128)(2,1)} %collective-permute-done.9.qb, bf16[8,32,2048]{2,1,0:T(8,128)(2,1)} %collective-permute-done.10.qc, ...), custom_call_target="tpu_custom_call" | custom-call | flops 28080001024 | bytes 25165824 | tf_op jit(solution)/shard_map/attention/pallas_call | solution.py:172
  196.4 24.1 %collective-permute-done.14.qb = bf16[8,32,2048]{2,1,0:T(8,128)(2,1)} collective-permute-done((bf16[8,32,2048]{2,1,0:T(8,128)(2,1)S(1)}, bf16[8,32,2048]{2,1,0:T(8,128)(2,1)}, u32[]{:S(2)}, u32[]{:S(2)}) %collective-permute-start.14) | collective-permute-done | bytes 1048608 | tf_op jit(solution)/shard_map/ppermute | solution.py:466
  226.6 4.6 merge.8
  231.2 11.1 %collective-permute-done.13.fstat = f32[1,32,128]{2,1,0:T(8,128)S(1)} collective-permute-done((f32[1,32,128]{2,1,0:T(8,128)S(1)}, f32[1,32,128]{2,1,0:T(8,128)S(1)}, u32[]{:S(2)}, u32[]{:S(2)}) %collective-permute-start.13) | collective-permute-done | bytes 16416 | tf_op jit(solution)/shard_map/ppermute | solution.py:512
  247.7 19.6 %attention.8 = (f32[8,64,2048]{2,1,0:T(8,128)}, f32[8,64,2176]{2,1,0:T(8,128)}, f32[8,32,128]{2,1,0:T(8,128)}) custom-call(s32[33]{0:T(128)} %pad_add_fusion.1.sc_ref, bf16[8,32,2048]{2,1,0:T(8,128)(2,1)} %bitcast.50, bf16[8,32,2048]{2,1,0:T(8,128)(2,1)} %collective-permute-done.14.qb, bf16[8,32,2048]{2,1,0:T(8,128)(2,1)} %collective-permute-done.15.qc, ...), custom_call_target="tpu_custom_call" | custom-call | flops 28080001024 | bytes 25165824 | tf_op jit(solution)/shard_map/attention/pallas_call | solution.py:172
  270.2 23.8 %collective-permute-done.21.qb = bf16[8,32,2048]{2,1,0:T(8,128)(2,1)} collective-permute-done((bf16[8,32,2048]{2,1,0:T(8,128)(2,1)S(1)}, bf16[8,32,2048]{2,1,0:T(8,128)(2,1)}, u32[]{:S(2)}, u32[]{:S(2)}) %collective-permute-start.21) | collective-permute-done | bytes 1048608 | tf_op jit(solution)/shard_map/ppermute | solution.py:466
  294.0 21.9 %collective-permute-done.19.fstat = f32[1,32,128]{2,1,0:T(8,128)S(1)} collective-permute-done((f32[1,32,128]{2,1,0:T(8,128)S(1)}, f32[1,32,128]{2,1,0:T(8,128)S(1)}, u32[]{:S(2)}, u32[]{:S(2)}) %collective-permute-start.19) | collective-permute-done | bytes 16416 | tf_op jit(solution)/shard_map/ppermute | solution.py:512
  322.6 3.9 finish.7
  326.5 4.3 merge.9
  330.8 19.6 %attention.9 = (f32[8,64,2048]{2,1,0:T(8,128)}, f32[8,64,2176]{2,1,0:T(8,128)}, f32[8,32,128]{2,1,0:T(8,128)}) custom-call(s32[33]{0:T(128)} %pad_add_fusion.1.sc_ref, bf16[8,32,2048]{2,1,0:T(8,128)(2,1)} %bitcast.47, bf16[8,32,2048]{2,1,0:T(8,128)(2,1)} %collective-permute-done.21.qb, bf16[8,32,2048]{2,1,0:T(8,128)(2,1)} %collective-permute-done.22.qc, ...), custom_call_target="tpu_custom_call" | custom-call | flops 28080001024 | bytes 25165824 | tf_op jit(solution)/shard_map/attention/pallas_call | solution.py:172
  350.9 54.7 %collective-permute-done.34.refs_4_ = bf16[768,4096]{1,0:T(8,128)(2,1)} collective-permute-done((bf16[768,4096]{1,0:T(8,128)(2,1)}, bf16[768,4096]{1,0:T(8,128)(2,1)}, u32[]{:S(2)}, u32[]{:S(2)}) %collective-permute-start.34) | collective-permute-done | bytes 6291488 | tf_op jit(solution)/shard_map/ppermute | solution.py:490
  408.1 45.6 %collective-permute-done.33.refs_3_ = bf16[256,4096]{1,0:T(8,128)(2,1)} collective-permute-done((bf16[256,4096]{1,0:T(8,128)(2,1)S(1)}, bf16[256,4096]{1,0:T(8,128)(2,1)}, u32[]{:S(2)}, u32[]{:S(2)}) %collective-permute-start.33) | collective-permute-done | bytes 2097184 | tf_op jit(solution)/shard_map/ppermute | solution.py:484
  455.4 44.3 %collective-permute-done.26.fstat = f32[2,32,128]{2,1,0:T(8,128)S(1)} collective-permute-done((f32[2,32,128]{2,1,0:T(8,128)S(1)}, f32[2,32,128]{2,1,0:T(8,128)S(1)}, u32[]{:S(2)}, u32[]{:S(2)}) %collective-permute-start.26) | collective-permute-done | bytes 32800 | tf_op jit(solution)/shard_map/ppermute | solution.py:512
  501.3 5.1 finish.8
  516.0 15.5 %project_own.2.refs_9_ = f32[512,4096]{1,0:T(8,128)} custom-call(s32[2]{0:T(128)} %pad_add_fusion.sc_ref, bf16[128,2048]{1,0:T(8,128)(2,1)} %bitcast.60, bf16[128,2048]{1,0:T(8,128)(2,1)} %bitcast.62, bf16[256,2048]{1,0:T(8,128)(2,1)} %bitcast.58, bf16[2048,4096]{1,0:T(8,128)(2,1)} %refs_3_.3), custom_call_target="tpu_custom_call" | custom-call | flops 14616000512 | bytes 16777216 | tf_op jit(solution)/shard_map/project_own/pallas_call | solution.py:379
  531.6 5.1 finish.9
  541.6 9.7 %collective-permute-done.32.refs_2_ = bf16[256,2048]{1,0:T(8,128)(2,1)} collective-permute-done((bf16[256,2048]{1,0:T(8,128)(2,1)S(1)}, bf16[256,2048]{1,0:T(8,128)(2,1)}, u32[]{:S(2)}, u32[]{:S(2)}) %collective-permute-start.32) | collective-permute-done | bytes 1048608 | tf_op jit(solution)/shard_map/ppermute | solution.py:520
  552.8 20.3 %project.2.refs_10_ = bf16[1024,4096]{1,0:T(8,128)(2,1)} custom-call(s32[2]{0:T(128)} %pad_add_fusion.sc_ref, bf16[128,2048]{1,0:T(8,128)(2,1)} %copy-done.30, bf16[128,2048]{1,0:T(8,128)(2,1)} %copy-done.31, bf16[256,2048]{1,0:T(8,128)(2,1)} %collective-permute-done.32.refs_2_, bf16[256,4096]{1,0:T(8,128)(2,1)} %collective-permute-done.33.refs_3_, ...), custom_call_target="tpu_custom_call" | custom-call | flops 18215999488 | bytes 16777216 | tf_op jit(solution)/shard_map/project/pallas_call | solution.py:409
  579.2 7.2 %collective-permute-done.39.far = f32[4,32,2048]{2,1,0:T(8,128)S(1)} collective-permute-done((f32[4,32,2048]{2,1,0:T(8,128)}, f32[4,32,2048]{2,1,0:T(8,128)S(1)}, u32[]{:S(2)}, u32[]{:S(2)}) %collective-permute-start.39) | collective-permute-done | bytes 1048608 | tf_op jit(solution)/shard_map/ppermute | solution.py:512
  587.5 3.9 finish.11
  592.8 15.1 %project_own.3.refs_9_ = f32[512,4096]{1,0:T(8,128)} custom-call(s32[2]{0:T(128)} %pad_add_fusion.sc_ref, bf16[256,2048]{1,0:T(8,128)(2,1)} %bitcast.57, bf16[128,2048]{1,0:T(8,128)(2,1)} %bitcast.65, bf16[128,2048]{1,0:T(8,128)(2,1)} %bitcast.67, bf16[2048,4096]{1,0:T(8,128)(2,1)} %refs_3_.3), custom_call_target="tpu_custom_call" | custom-call | flops 14616000512 | bytes 16777216 | tf_op jit(solution)/shard_map/project_own/pallas_call | solution.py:379
  609.8 20.5 %project.3 = bf16[1024,4096]{1,0:T(8,128)(2,1)} custom-call(s32[2]{0:T(128)} %pad_add_fusion.sc_ref, bf16[256,2048]{1,0:T(8,128)(2,1)} %copy-done.29, bf16[128,2048]{1,0:T(8,128)(2,1)} %copy-done.32, bf16[128,2048]{1,0:T(8,128)(2,1)} %copy-done.33, bf16[256,4096]{1,0:T(8,128)(2,1)} %collective-permute-done.33.refs_3_, ...), custom_call_target="tpu_custom_call", output_to_operand_aliasing={{}: (11, {})} | custom-call | flops 18215999488 | bytes 16777216 | tf_op jit(solution)/shard_map/project/pallas_call | solution.py:409
  (185 shorter events, 99.5 us)
Async XLA Ops:
  45.7 43.7 %collective-permute-start.3 = (bf16[8,32,2048]{2,1,0:T(8,128)(2,1)S(1)}, bf16[8,32,2048]{2,1,0:T(8,128)(2,1)S(1)}, u32[]{:S(2)}, u32[]{:S(2)}) collective-permute-start(bf16[8,32,2048]{2,1,0:T(8,128)(2,1)S(1)} %bitcast.37), channel_id=1, source_target_pairs={{0,2},{2,0},{1,3},{3,1},{4,6},{6,4},{5,7},{7,5}} | collective-permute-start | bytes 3145736 | tf_op jit(solution)/shard_map/ppermute | solution.py:466
  47.7 55.8 %collective-permute-start.4 = (bf16[8,32,2048]{2,1,0:T(8,128)(2,1)S(1)}, bf16[8,32,2048]{2,1,0:T(8,128)(2,1)S(1)}, u32[]{:S(2)}, u32[]{:S(2)}) collective-permute-start(bf16[8,32,2048]{2,1,0:T(8,128)(2,1)S(1)} %bitcast.38), channel_id=1, source_target_pairs={{0,1},{1,0},{2,3},{3,2},{4,5},{5,4},{6,7},{7,6}} | collective-permute-start | bytes 3145736 | tf_op jit(solution)/shard_map/ppermute | solution.py:467
  116.1 25.7 %collective-permute-start.6 = (f32[4,64,2176]{2,1,0:T(8,128)}, f32[4,64,2176]{2,1,0:T(8,128)}, u32[]{:S(2)}, u32[]{:S(2)}) collective-permute-start(f32[4,64,2176]{2,1,0:T(8,128)} %get-tuple-element.89), channel_id=1, source_target_pairs={{0,1},{1,0},{2,3},{3,2},{4,5},{5,4},{6,7},{7,6}} | collective-permute-start | bytes 6684680 | tf_op jit(solution)/shard_map/ppermute | solution.py:504
  128.2 36.0 %collective-permute-start.8 = (f32[4,64,2176]{2,1,0:T(8,128)}, f32[4,64,2176]{2,1,0:T(8,128)S(1)}, u32[]{:S(2)}, u32[]{:S(2)}) collective-permute-start(f32[4,64,2176]{2,1,0:T(8,128)} %get-tuple-element.96), channel_id=1, source_target_pairs={{0,1},{1,0},{2,3},{3,2},{4,5},{5,4},{6,7},{7,6}} | collective-permute-start | bytes 6684680 | tf_op jit(solution)/shard_map/ppermute | solution.py:504
  128.2 46.0 %collective-permute-start.10 = (bf16[8,32,2048]{2,1,0:T(8,128)(2,1)S(1)}, bf16[8,32,2048]{2,1,0:T(8,128)(2,1)}, u32[]{:S(2)}, u32[]{:S(2)}) collective-permute-start(bf16[8,32,2048]{2,1,0:T(8,128)(2,1)S(1)} %bitcast.55), channel_id=1, source_target_pairs={{0,1},{1,0},{2,3},{3,2},{4,5},{5,4},{6,7},{7,6}} | collective-permute-start | bytes 3145736 | tf_op jit(solution)/shard_map/ppermute | solution.py:467
  141.8 32.4 %collective-permute-start.11 = (bf16[8,32,2048]{2,1,0:T(8,128)(2,1)}, bf16[8,32,2048]{2,1,0:T(8,128)(2,1)}, u32[]{:S(2)}, u32[]{:S(2)}) collective-permute-start(bf16[8,32,2048]{2,1,0:T(8,128)(2,1)} %collective-permute-done.9.qb), channel_id=1, source_target_pairs={{0,1},{1,0},{2,3},{3,2},{4,5},{5,4},{6,7},{7,6}} | collective-permute-start | bytes 3145736 | tf_op jit(solution)/shard_map/ppermute | solution.py:468
  193.8 32.8 %collective-permute-start.12 = (f32[8,64,2176]{2,1,0:T(8,128)}, f32[8,64,2176]{2,1,0:T(8,128)}, u32[]{:S(2)}, u32[]{:S(2)}) collective-permute-start(f32[8,64,2176]{2,1,0:T(8,128)} %get-tuple-element.105), channel_id=1, source_target_pairs={{0,1},{1,0},{2,3},{3,2},{4,5},{5,4},{6,7},{7,6}} | collective-permute-start | bytes 13369352 | tf_op jit(solution)/shard_map/ppermute | solution.py:504
  194.3 26.1 %collective-permute-start.14 = (bf16[8,32,2048]{2,1,0:T(8,128)(2,1)S(1)}, bf16[8,32,2048]{2,1,0:T(8,128)(2,1)}, u32[]{:S(2)}, u32[]{:S(2)}) collective-permute-start(bf16[8,32,2048]{2,1,0:T(8,128)(2,1)S(1)} %bitcast.51), channel_id=1, source_target_pairs={{0,2},{2,0},{1,3},{3,1},{4,6},{6,4},{5,7},{7,5}} | collective-permute-start | bytes 3145736 | tf_op jit(solution)/shard_map/ppermute | solution.py:466
  194.8 47.4 %collective-permute-start.7 = (f32[4,32,2048]{2,1,0:T(8,128)}, f32[4,32,2048]{2,1,0:T(8,128)S(1)}, u32[]{:S(2)}, u32[]{:S(2)}) collective-permute-start(f32[4,32,2048]{2,1,0:T(8,128)} %get-tuple-element.94), channel_id=1, source_target_pairs={{0,2},{2,0},{1,3},{3,1},{4,6},{6,4},{5,7},{7,5}} | collective-permute-start | bytes 3145736 | tf_op jit(solution)/shard_map/ppermute | solution.py:512
  196.4 51.4 %collective-permute-start.15 = (bf16[8,32,2048]{2,1,0:T(8,128)(2,1)S(1)}, bf16[8,32,2048]{2,1,0:T(8,128)(2,1)}, u32[]{:S(2)}, u32[]{:S(2)}) collective-permute-start(bf16[8,32,2048]{2,1,0:T(8,128)(2,1)S(1)} %bitcast.52), channel_id=1, source_target_pairs={{0,1},{1,0},{2,3},{3,2},{4,5},{5,4},{6,7},{7,6}} | collective-permute-start | bytes 3145736 | tf_op jit(solution)/shard_map/ppermute | solution.py:467
  220.5 27.3 %collective-permute-start.16 = (bf16[8,32,2048]{2,1,0:T(8,128)(2,1)}, bf16[8,32,2048]{2,1,0:T(8,128)(2,1)}, u32[]{:S(2)}, u32[]{:S(2)}) collective-permute-start(bf16[8,32,2048]{2,1,0:T(8,128)(2,1)} %collective-permute-done.14.qb), channel_id=1, source_target_pairs={{0,1},{1,0},{2,3},{3,2},{4,5},{5,4},{6,7},{7,6}} | collective-permute-start | bytes 3145736 | tf_op jit(solution)/shard_map/ppermute | solution.py:468
  267.3 59.2 %collective-permute-start.17 = (f32[8,64,2176]{2,1,0:T(8,128)}, f32[8,64,2176]{2,1,0:T(8,128)}, u32[]{:S(2)}, u32[]{:S(2)}) collective-permute-start(f32[8,64,2176]{2,1,0:T(8,128)} %get-tuple-element.113), channel_id=1, source_target_pairs={{0,1},{1,0},{2,3},{3,2},{4,5},{5,4},{6,7},{7,6}} | collective-permute-start | bytes 13369352 | tf_op jit(solution)/shard_map/ppermute | solution.py:504
  267.3 138.2 %collective-permute-start.34 = (bf16[768,4096]{1,0:T(8,128)(2,1)}, bf16[768,4096]{1,0:T(8,128)(2,1)}, u32[]{:S(2)}, u32[]{:S(2)}) collective-permute-start(bf16[768,4096]{1,0:T(8,128)(2,1)} %constant_dynamic-slice_fusion), channel_id=1, source_target_pairs={{0,4},{4,0},{1,5},{5,1},{2,6},{6,2},{3,7},{7,3}} | collective-permute-start | bytes 18874376 | tf_op jit(solution)/shard_map/ppermute | solution.py:490
  267.9 26.1 %collective-permute-start.21 = (bf16[8,32,2048]{2,1,0:T(8,128)(2,1)S(1)}, bf16[8,32,2048]{2,1,0:T(8,128)(2,1)}, u32[]{:S(2)}, u32[]{:S(2)}) collective-permute-start(bf16[8,32,2048]{2,1,0:T(8,128)(2,1)S(1)} %bitcast.48), channel_id=1, source_target_pairs={{0,2},{2,0},{1,3},{3,1},{4,6},{6,4},{5,7},{7,5}} | collective-permute-start | bytes 3145736 | tf_op jit(solution)/shard_map/ppermute | solution.py:466
  268.2 53.4 %collective-permute-start.18 = (f32[4,32,2048]{2,1,0:T(8,128)}, f32[4,32,2048]{2,1,0:T(8,128)S(1)}, u32[]{:S(2)}, u32[]{:S(2)}) collective-permute-start(f32[4,32,2048]{2,1,0:T(8,128)} %get-tuple-element.115), channel_id=1, source_target_pairs={{0,2},{2,0},{1,3},{3,1},{4,6},{6,4},{5,7},{7,5}} | collective-permute-start | bytes 3145736 | tf_op jit(solution)/shard_map/ppermute | solution.py:512
  269.9 46.1 %collective-permute-start.19 = (f32[1,32,128]{2,1,0:T(8,128)S(1)}, f32[1,32,128]{2,1,0:T(8,128)S(1)}, u32[]{:S(2)}, u32[]{:S(2)}) collective-permute-start(f32[1,32,128]{2,1,0:T(8,128)S(1)} %copy-done.36), channel_id=1, source_target_pairs={{0,2},{2,0},{1,3},{3,1},{4,6},{6,4},{5,7},{7,5}} | collective-permute-start | bytes 49160 | tf_op jit(solution)/shard_map/ppermute | solution.py:512
  294.0 36.8 %collective-permute-start.22 = (bf16[8,32,2048]{2,1,0:T(8,128)(2,1)S(1)}, bf16[8,32,2048]{2,1,0:T(8,128)(2,1)}, u32[]{:S(2)}, u32[]{:S(2)}) collective-permute-start(bf16[8,32,2048]{2,1,0:T(8,128)(2,1)S(1)} %bitcast.49), channel_id=1, source_target_pairs={{0,1},{1,0},{2,3},{3,2},{4,5},{5,4},{6,7},{7,6}} | collective-permute-start | bytes 3145736 | tf_op jit(solution)/shard_map/ppermute | solution.py:467
  350.4 156.0 %collective-permute-start.24 = (f32[8,64,2176]{2,1,0:T(8,128)}, f32[8,64,2176]{2,1,0:T(8,128)}, u32[]{:S(2)}, u32[]{:S(2)}) collective-permute-start(f32[8,64,2176]{2,1,0:T(8,128)} %get-tuple-element.123), channel_id=1, source_target_pairs={{0,1},{1,0},{2,3},{3,2},{4,5},{5,4},{6,7},{7,6}} | collective-permute-start | bytes 13369352 | tf_op jit(solution)/shard_map/ppermute | solution.py:504
  405.6 134.5 %collective-permute-start.36 = (bf16[768,4096]{1,0:T(8,128)(2,1)}, bf16[768,4096]{1,0:T(8,128)(2,1)}, u32[]{:S(2)}, u32[]{:S(2)}) collective-permute-start(bf16[768,4096]{1,0:T(8,128)(2,1)} %collective-permute-done.34.refs_4_), channel_id=1, source_target_pairs={{0,1},{1,0},{2,3},{3,2},{4,5},{5,4},{6,7},{7,6}} | collective-permute-start | bytes 18874376 | tf_op jit(solution)/shard_map/ppermute | solution.py:492
  405.6 48.1 %collective-permute-start.33 = (bf16[256,4096]{1,0:T(8,128)(2,1)S(1)}, bf16[256,4096]{1,0:T(8,128)(2,1)}, u32[]{:S(2)}, u32[]{:S(2)}) collective-permute-start(bf16[256,4096]{1,0:T(8,128)(2,1)S(1)} %copy-done.6), channel_id=1, source_target_pairs={{0,4},{4,0},{1,5},{5,1},{2,6},{6,2},{3,7},{7,3}} | collective-permute-start | bytes 6291464 | tf_op jit(solution)/shard_map/ppermute | solution.py:484
  406.1 93.6 %collective-permute-start.25 = (f32[8,32,2048]{2,1,0:T(8,128)}, f32[8,32,2048]{2,1,0:T(8,128)}, u32[]{:S(2)}, u32[]{:S(2)}) collective-permute-start(f32[8,32,2048]{2,1,0:T(8,128)} %get-tuple-element.125), channel_id=1, source_target_pairs={{0,2},{2,0},{1,3},{3,1},{4,6},{6,4},{5,7},{7,5}} | collective-permute-start | bytes 6291464 | tf_op jit(solution)/shard_map/ppermute | solution.py:512
  406.4 108.1 %collective-permute-start.20 = (f32[8,32,2048]{2,1,0:T(8,128)}, f32[8,32,2048]{2,1,0:T(8,128)}, u32[]{:S(2)}, u32[]{:S(2)}) collective-permute-start(f32[8,32,2048]{2,1,0:T(8,128)} %get-tuple-element.119), channel_id=1, source_target_pairs={{0,2},{2,0},{1,3},{3,1},{4,6},{6,4},{5,7},{7,5}} | collective-permute-start | bytes 6291464 | tf_op jit(solution)/shard_map/ppermute | solution.py:512
  453.7 46.0 %collective-permute-start.26 = (f32[2,32,128]{2,1,0:T(8,128)S(1)}, f32[2,32,128]{2,1,0:T(8,128)S(1)}, u32[]{:S(2)}, u32[]{:S(2)}) collective-permute-start(f32[2,32,128]{2,1,0:T(8,128)S(1)} %copy-done.34), channel_id=1, source_target_pairs={{0,2},{2,0},{1,3},{3,1},{4,6},{6,4},{5,7},{7,5}} | collective-permute-start | bytes 98312 | tf_op jit(solution)/shard_map/ppermute | solution.py:512
  499.7 37.0 %collective-permute-start.35 = (bf16[256,4096]{1,0:T(8,128)(2,1)}, bf16[256,4096]{1,0:T(8,128)(2,1)}, u32[]{:S(2)}, u32[]{:S(2)}) collective-permute-start(bf16[256,4096]{1,0:T(8,128)(2,1)} %collective-permute-done.33.refs_3_), channel_id=1, source_target_pairs={{0,1},{1,0},{2,3},{3,2},{4,5},{5,4},{6,7},{7,6}} | collective-permute-start | bytes 6291464 | tf_op jit(solution)/shard_map/ppermute | solution.py:492
  499.7 38.5 %collective-permute-start.30 = (bf16[128,2048]{1,0:T(8,128)(2,1)S(1)}, bf16[128,2048]{1,0:T(8,128)(2,1)S(1)}, u32[]{:S(2)}, u32[]{:S(2)}) collective-permute-start(bf16[128,2048]{1,0:T(8,128)(2,1)S(1)} %bitcast.61), channel_id=1, source_target_pairs={{0,4},{4,0},{1,5},{5,1},{2,6},{6,2},{3,7},{7,3}} | collective-permute-start | bytes 1572872 | tf_op jit(solution)/shard_map/ppermute | solution.py:520
  514.5 36.8 %collective-permute-start.32 = (bf16[256,2048]{1,0:T(8,128)(2,1)S(1)}, bf16[256,2048]{1,0:T(8,128)(2,1)}, u32[]{:S(2)}, u32[]{:S(2)}) collective-permute-start(bf16[256,2048]{1,0:T(8,128)(2,1)S(1)} %bitcast.59), channel_id=1, source_target_pairs={{0,4},{4,0},{1,5},{5,1},{2,6},{6,2},{3,7},{7,3}} | collective-permute-start | bytes 3145736 | tf_op jit(solution)/shard_map/ppermute | solution.py:520
  536.7 36.5 %collective-permute-start.37 = (f32[1,32,128]{2,1,0:T(8,128)S(1)}, f32[1,32,128]{2,1,0:T(8,128)S(1)}, u32[]{:S(2)}, u32[]{:S(2)}) collective-permute-start(f32[1,32,128]{2,1,0:T(8,128)S(1)} %copy-done.39), channel_id=1, source_target_pairs={{0,2},{2,0},{1,3},{3,1},{4,6},{6,4},{5,7},{7,5}} | collective-permute-start | bytes 49160 | tf_op jit(solution)/shard_map/ppermute | solution.py:512
  538.2 41.0 %collective-permute-start.40 = (f32[1,32,128]{2,1,0:T(8,128)S(1)}, f32[1,32,128]{2,1,0:T(8,128)S(1)}, u32[]{:S(2)}, u32[]{:S(2)}) collective-permute-start(f32[1,32,128]{2,1,0:T(8,128)S(1)} %copy-done.37), channel_id=1, source_target_pairs={{0,2},{2,0},{1,3},{3,1},{4,6},{6,4},{5,7},{7,5}} | collective-permute-start | bytes 49160 | tf_op jit(solution)/shard_map/ppermute | solution.py:512
  539.6 68.3 %collective-permute-start.28 = (bf16[256,2048]{1,0:T(8,128)(2,1)}, bf16[256,2048]{1,0:T(8,128)(2,1)S(1)}, u32[]{:S(2)}, u32[]{:S(2)}) collective-permute-start(bf16[256,2048]{1,0:T(8,128)(2,1)} %bitcast.56), channel_id=1, source_target_pairs={{0,4},{4,0},{1,5},{5,1},{2,6},{6,2},{3,7},{7,3}} | collective-permute-start | bytes 3145736 | tf_op jit(solution)/shard_map/ppermute | solution.py:520
  540.1 33.1 %collective-permute-start.29 = (f32[4,32,2048]{2,1,0:T(8,128)}, f32[4,32,2048]{2,1,0:T(8,128)S(1)}, u32[]{:S(2)}, u32[]{:S(2)}) collective-permute-start(f32[4,32,2048]{2,1,0:T(8,128)} %get-tuple-element.133), channel_id=1, source_target_pairs={{0,2},{2,0},{1,3},{3,1},{4,6},{6,4},{5,7},{7,5}} | collective-permute-start | bytes 3145736 | tf_op jit(solution)/shard_map/ppermute | solution.py:512
  551.3 35.1 %collective-permute-start.39 = (f32[4,32,2048]{2,1,0:T(8,128)}, f32[4,32,2048]{2,1,0:T(8,128)S(1)}, u32[]{:S(2)}, u32[]{:S(2)}) collective-permute-start(f32[4,32,2048]{2,1,0:T(8,128)} %get-tuple-element.138), channel_id=1, source_target_pairs={{0,2},{2,0},{1,3},{3,1},{4,6},{6,4},{5,7},{7,5}} | collective-permute-start | bytes 3145736 | tf_op jit(solution)/shard_map/ppermute | solution.py:512
  578.7 29.2 %collective-permute-start.38 = (bf16[128,2048]{1,0:T(8,128)(2,1)}, bf16[128,2048]{1,0:T(8,128)(2,1)S(1)}, u32[]{:S(2)}, u32[]{:S(2)}) collective-permute-start(bf16[128,2048]{1,0:T(8,128)(2,1)} %bitcast.64), channel_id=1, source_target_pairs={{0,4},{4,0},{1,5},{5,1},{2,6},{6,2},{3,7},{7,3}} | collective-permute-start | bytes 1572872 | tf_op jit(solution)/shard_map/ppermute | solution.py:520
  (52 other events, 1046.7 us)
